TPU v7x, 32 devices: a whole 2x2x4 slice. The times are simulated.
32 devices in a mesh: fsdp: 16 (over z, x, core), dp: 2 (over y).
Axes of the slice: x: 2, y: 2, z: 4, core: 2. Of those that a mesh axis runs over, the one named last changes fastest.
Arguments:
- tokens: bfloat16 [64, 256, 1536], P(('fsdp', 'dp')), may hold values from -21 to 21
- segments: int32 [64, 256], P(('fsdp', 'dp')), may hold values from 0 to 2, never falling along the last dimension, each value on 1 to 192 neighbouring positions
- norm_gain: bfloat16 [1536], P('fsdp'), may hold values from 0.5 to 1.5
- w_in: bfloat16 [1536, 6448], P('fsdp'), may hold values from -1 to 1
- conv_weight: bfloat16 [4, 3328], P(None, 'fsdp'), may hold values from -3 to 3
- conv_bias: bfloat16 [3328], P('fsdp'), may hold values from -0.5 to 0.5
- dt_bias: float32 [48], replicated, may hold values from -1 to 2
- a_log: float32 [48], replicated, may hold values from 0 to 1.5
- d_skip: float32 [48], replicated, may hold values from 0.5 to 1.5
- gate_gain: bfloat16 [3072], P('fsdp'), may hold values from 0.5 to 1.5
- w_out: bfloat16 [3072, 1536], P('fsdp'), may hold values from -0.109375 to 0.109375
- cotangent: bfloat16 [64, 256, 1536], P(('fsdp', 'dp')), may hold values from -6 to 6
Outputs:
- block_out: bfloat16 [64, 256, 1536], P(('fsdp', 'dp'))
- grad_tokens: float32 [64, 256, 1536], P(('fsdp', 'dp'))
- grad_norm_gain: float32 [1536], P('fsdp')
- grad_w_in: float32 [1536, 6448], P('fsdp')
- grad_conv_weight: float32 [4, 3328], P(None, 'fsdp')
- grad_conv_bias: float32 [3328], P('fsdp')
- grad_dt_bias: float32 [48], replicated
- grad_a_log: float32 [48], replicated
- grad_d_skip: float32 [48], replicated
- grad_gate_gain: float32 [3072], P('fsdp')
- grad_w_out: float32 [3072, 1536], P('fsdp')
Inputs may be any that keep to these rules, and one draw needn't show every extreme that they name: `segments`: along each sequence the segment numbers never fall; every document runs 1 to 192 tokens and one runs exactly 192.
All inputs are finite; a program needn't handle non-finite values.
Results may differ from a plain program's by a relative error of at most 0.0064.
Values may be sent and summed in bfloat16 or wider, within the bound.
A program may use at most 320 MiB of HBM per device.

v0:
```python
import jax
import jax.numpy as jnp
from jax import lax
from jax.sharding import PartitionSpec as P

D = 1536
DI = 3072
H = 48
CONV = 4
BLOCK = 128
CONVDIM = 3328
PROJ = 6448


epsilon = 1e-05
highest = lax.Precision.HIGHEST


def mixer(projected, seg_row, conv_kernel, conv_shift, dt_offset, log_rate, skip_gain, out_gain):
    length = projected.shape[0]
    inner_width = out_gain.shape[0]
    head_count = dt_offset.shape[0]
    head_size = inner_width // head_count
    conv_width = conv_kernel.shape[1]
    state_size = (conv_width - inner_width) // 2
    kernel_taps = conv_kernel.shape[0]
    blocks = length // BLOCK
    gate_part = projected[:, :inner_width]
    conv_part = projected[:, inner_width : inner_width + conv_width]
    step_raw = projected[:, inner_width + conv_width :]
    padded = jnp.pad(conv_part, ((kernel_taps - 1, 0), (0, 0)))
    seg_padded = jnp.pad(seg_row, (kernel_taps - 1, 0), constant_values=-1)
    summed = jnp.zeros_like(conv_part) + conv_shift
    for offset in range(kernel_taps):
        window = padded[offset : offset + length]
        same_doc = (seg_padded[offset : offset + length] == seg_row).astype(jnp.float32)
        summed = summed + conv_kernel[offset] * window * same_doc[:, None]
    activated = jax.nn.silu(summed)
    head_inputs = activated[:, :inner_width].reshape(blocks, BLOCK, head_count, head_size)
    b_rows = activated[:, inner_width : inner_width + state_size].reshape(blocks, BLOCK, state_size)
    c_rows = activated[:, inner_width + state_size :].reshape(blocks, BLOCK, state_size)
    step_size = jax.nn.softplus(step_raw + dt_offset)
    log_decay = -step_size * jnp.exp(log_rate)
    cumulative = jnp.cumsum(log_decay.reshape(blocks, BLOCK, head_count), axis=1).transpose(0, 2, 1)
    step_heads = step_size.reshape(blocks, BLOCK, head_count).transpose(0, 2, 1)
    seg_blocks = seg_row.reshape(blocks, BLOCK)
    position = jnp.arange(BLOCK)
    causal = (position[:, None] >= position[None, :])[None] & (
        seg_blocks[:, :, None] == seg_blocks[:, None, :]
    )
    visible = causal[:, None]
    differences = cumulative[:, :, :, None] - cumulative[:, :, None, :]
    decay_mat = jnp.where(visible, jnp.exp(jnp.where(visible, differences, 0.0)), 0.0)
    scores = jnp.einsum("btn,bsn->bts", c_rows, b_rows, precision=highest)
    weights = decay_mat * scores[:, None] * step_heads[:, :, None, :]
    within = jnp.einsum("bhts,bshp->bthp", weights, head_inputs, precision=highest)
    last_seg = seg_blocks[:, -1]
    prev_seg = jnp.concatenate([jnp.full((1,), -1, seg_blocks.dtype), last_seg[:-1]])
    to_end = (seg_blocks == last_seg[:, None]).astype(jnp.float32)
    end_weight = jnp.exp(cumulative[:, :, -1:] - cumulative) * step_heads * to_end[:, None, :]
    local_state = jnp.einsum(
        "bhs,bshp,bsn->bhpn", end_weight, head_inputs, b_rows, precision=highest
    )
    carry_keep = jnp.exp(cumulative[:, :, -1]) * (last_seg == prev_seg).astype(jnp.float32)[:, None]

    def advance(state_now, inputs_now):
        keep_now, local_now = inputs_now
        return (keep_now[:, None, None] * state_now + local_now, state_now)

    final_state, entering = lax.scan(
        advance,
        jnp.zeros((head_count, head_size, state_size), jnp.float32),
        (carry_keep, local_state),
    )
    from_prev = (seg_blocks == prev_seg[:, None]).astype(jnp.float32)
    reach_in = jnp.exp(cumulative).transpose(0, 2, 1) * from_prev[:, :, None]
    across = jnp.einsum("btn,bhpn->bthp", c_rows, entering, precision=highest) * reach_in[..., None]
    ssm_out = (within + across + skip_gain[:, None] * head_inputs).reshape(length, inner_width)
    gated_out = ssm_out * jax.nn.silu(gate_part)
    norm_scale = lax.rsqrt(jnp.mean(gated_out * gated_out, axis=-1, keepdims=True) + epsilon)
    return gated_out * norm_scale * out_gain


def local(
    tokens,
    segments,
    norm_gain,
    w_in,
    conv_weight,
    conv_bias,
    dt_bias,
    a_log,
    d_skip,
    gate_gain,
    w_out,
    cotangent,
):
    micro_count = tokens.shape[0]
    total_norm = jnp.zeros((D,), jnp.float32)
    total_in = jnp.zeros((D, PROJ), jnp.float32)
    total_kernel = jnp.zeros((CONV, CONVDIM), jnp.float32)
    total_shift = jnp.zeros((CONVDIM,), jnp.float32)
    total_offset = jnp.zeros((H,), jnp.float32)
    total_rate = jnp.zeros((H,), jnp.float32)
    total_skip = jnp.zeros((H,), jnp.float32)
    total_gate = jnp.zeros((DI,), jnp.float32)
    total_out = jnp.zeros((DI, D), jnp.float32)
    block_list = []
    grad_list = []
    for number in range(micro_count):
        gain_full, w_in_full, kernel_full, shift_full, gate_full = (
            lax.all_gather(norm_gain, "fsdp", axis=0, tiled=True),
            lax.all_gather(w_in, "fsdp", axis=0, tiled=True),
            lax.all_gather(conv_weight, "fsdp", axis=1, tiled=True),
            lax.all_gather(conv_bias, "fsdp", axis=0, tiled=True),
            lax.all_gather(gate_gain, "fsdp", axis=0, tiled=True),
        )
        residual = tokens[number].astype(jnp.float32)
        rstd_rows = lax.rsqrt(jnp.mean(residual * residual, axis=-1, keepdims=True) + epsilon)
        unit_rows = residual * rstd_rows
        normed = (unit_rows * gain_full.astype(jnp.float32)).astype(jnp.bfloat16)
        projected = jnp.dot(normed, w_in_full, preferred_element_type=jnp.float32)
        seg_row = segments[number]

        def mixer_row(proj_in, kernel_arg, shift_arg, offset_arg, rate_arg, skip_arg, gain_arg):
            return mixer(
                proj_in, seg_row, kernel_arg, shift_arg, offset_arg, rate_arg, skip_arg, gain_arg
            )

        mixed_f, mixer_back = jax.vjp(
            mixer_row,
            projected,
            kernel_full.astype(jnp.float32),
            shift_full.astype(jnp.float32),
            dt_bias,
            a_log,
            d_skip,
            gate_full.astype(jnp.float32),
        )
        mixed = mixed_f.astype(jnp.bfloat16)
        w_out_full = lax.all_gather(w_out, "fsdp", axis=0, tiled=True)
        block_list.append(
            (residual + jnp.dot(mixed, w_out_full, preferred_element_type=jnp.float32)).astype(
                jnp.bfloat16
            )
        )
        grad_rows = cotangent[number]
        total_out = total_out + jnp.einsum(
            "ld,le->de", mixed, grad_rows, preferred_element_type=jnp.float32
        )
        w_out_back = lax.all_gather(w_out, "fsdp", axis=0, tiled=True)
        grad_mixed = jnp.einsum(
            "le,de->ld", grad_rows, w_out_back, preferred_element_type=jnp.float32
        )
        grad_proj, grad_kernel, grad_shift, grad_offset, grad_rate, grad_skip, grad_gate = (
            mixer_back(grad_mixed)
        )
        proj_back = grad_proj.astype(jnp.bfloat16)
        gain_back, w_in_back = (
            lax.all_gather(norm_gain, "fsdp", axis=0, tiled=True),
            lax.all_gather(w_in, "fsdp", axis=0, tiled=True),
        )
        total_in = total_in + jnp.einsum(
            "ld,lk->dk", normed, proj_back, preferred_element_type=jnp.float32
        )
        grad_normed = jnp.einsum(
            "lk,dk->ld", proj_back, w_in_back, preferred_element_type=jnp.float32
        )
        total_norm = total_norm + jnp.sum(grad_normed * unit_rows, axis=0)
        grad_unit = grad_normed * gain_back.astype(jnp.float32)
        grad_list.append(
            grad_rows.astype(jnp.float32)
            + rstd_rows
            * (grad_unit - unit_rows * jnp.mean(grad_unit * unit_rows, axis=-1, keepdims=True))
        )
        total_kernel = total_kernel + grad_kernel
        total_shift = total_shift + grad_shift
        total_offset = total_offset + grad_offset
        total_rate = total_rate + grad_rate
        total_skip = total_skip + grad_skip
        total_gate = total_gate + grad_gate
    shares = (
        lax.psum_scatter(total_norm, "fsdp", scatter_dimension=0, tiled=True),
        lax.psum_scatter(total_in, "fsdp", scatter_dimension=0, tiled=True),
        lax.psum_scatter(total_kernel, "fsdp", scatter_dimension=1, tiled=True),
        lax.psum_scatter(total_shift, "fsdp", scatter_dimension=0, tiled=True),
        lax.psum_scatter(total_gate, "fsdp", scatter_dimension=0, tiled=True),
        lax.psum_scatter(total_out, "fsdp", scatter_dimension=0, tiled=True),
    )
    owned = lax.psum((shares[0], shares[1], shares[2], shares[3], shares[4], shares[5]), "dp")
    head_grads = lax.psum((total_offset, total_rate, total_skip), ("fsdp", "dp"))
    return (
        jnp.stack(block_list),
        jnp.stack(grad_list),
        owned[0],
        owned[1],
        owned[2],
        owned[3],
        head_grads[0],
        head_grads[1],
        head_grads[2],
        owned[4],
        owned[5],
    )


def solution(mesh):
    placed = (
        P(("fsdp", "dp"), None, None),
        P(("fsdp", "dp"), None),
        P("fsdp"),
        P("fsdp", None),
        P(None, "fsdp"),
        P("fsdp"),
        P(),
        P(),
        P(),
        P("fsdp"),
        P("fsdp", None),
        P(("fsdp", "dp"), None, None),
    )
    return jax.shard_map(
        local,
        mesh=mesh,
        in_specs=placed,
        out_specs=(
            P(("fsdp", "dp"), None, None),
            P(("fsdp", "dp"), None, None),
            P("fsdp"),
            P("fsdp", None),
            P(None, "fsdp"),
            P("fsdp"),
            P(),
            P(),
            P(),
            P("fsdp"),
            P("fsdp", None),
        ),
        check_vma=False,
    )
```

profile of v0, /device:TPU:0, one launch (start us, length us, event | category | flops | bytes accessed | tf_op | source)
XLA Modules:
  0.0 1192.7 jit_solution(3348330027241150898)
XLA Ops:
  16.0 66.3 %all-reduce.46 = (bf16[1536]{0:T(1024)(128)(2,1)S(1)}, bf16[3328]{0:T(1024)(128)(2,1)S(1)}, bf16[3072]{0:T(1024)(128)(2,1)S(1)}) all-reduce(bf16[1536]{0:T(1024)(128)(2,1)S(1)} %dynamic-update-slice.1, bf16[3328]{0:T(1024)(128)(2,1)S(1)} %dynamic-update-slice, ...), channel_id=1, replica_groups=mesh['fsdp'=16,'dp'=2] {'fsdp'}, use_global_device_ids=true, to_apply=%add.37 | all-reduce | flops 7936 | bytes 31744
  82.3 17.9 %all-gather = bf16[16,208,4]{1,2,0:T(4,128)(2,1)S(1)} all-gather(bf16[1,208,4]{1,2,0:T(4,128)(2,1)S(1)} %bitcast.435), channel_id=1, replica_groups=mesh['fsdp'=16,'dp'=2] {'fsdp'}, dimensions={0}, use_global_device_ids=true | all-gather | bytes 28288 | tf_op jit(solution)/shard_map/all_gather | solution.py:114
  107.7 10.5 all-gather.4.cloned.1.call-done
  118.3 14.3 %fusion.194 = f32[256,6448]{0,1:T(8,128)} fusion(bf16[1536,6448]{1,0:T(8,128)(2,1)} %all-gather.4.cloned.1.call-done, f32[1536]{0:T(1024)S(1)} %convert_element_type.123, f32[256]{0:T(256)S(1)} %get-tuple-element.651, bf16[2,256,1536]{2,1,0:T(8,128)(2,1)} %param.21), kind=kOutput, calls=%fused_computation.289 | convolution fusion | flops 5072486400 | bytes 27450368 | tf_op jit(solution)/shard_map/dot_general | solution.py:122
  136.6 14.9 %fusion.190 = f32[256,6448]{0,1:T(8,128)} fusion(bf16[1536,6448]{1,0:T(8,128)(2,1)} %all-gather.4.cloned.1.call-done, f32[256]{0:T(256)S(1)} %get-tuple-element.650, f32[1536]{0:T(1024)S(1)} %convert_element_type.123, bf16[2,256,1536]{2,1,0:T(8,128)(2,1)S(1)} %copy-done.32), kind=kOutput, calls=%fused_computation.287 | convolution fusion | flops 5072486400 | bytes 27206656 | tf_op jit(solution)/shard_map/dot_general | solution.py:122
  160.4 19.0 %fusion.25 = (f32[256,3328]{0,1:T(8,128)}, f32[256,3328]{0,1:T(8,128)}, f32[256,3328]{0,1:T(8,128)S(1)}, f32[256,3328]{0,1:T(8,128)}) fusion(f32[256,3328]{0,1:T(8,128)} %slice.183, f32[3328]{0:T(1024)} %get-tuple-element.498, f32[256]{0:T(256)} %get-tuple-element.652, f32[3328]{0:T(1024)} %get-tuple-element.499, f32[256]{0:T(256)} %get-tuple-element.653, ...), kind=kLoop, calls=%fused_computation.78 | loop fusion | flops 25559040 | bytes 20519936 | tf_op jit(solution)/shard_map/jvp(jit(silu))/mul | solution.py:38
  224.7 13.0 %fusion.40 = f32[2,128,48,64]{1,3,2,0:T(8,128)S(1)} fusion(f32[2,128,48,64]{1,3,2,0:T(8,128)S(1)} %fusion.229, f32[2,128,48,64]{1,0,3,2:T(2,128)S(1)} %copy-done.14, f32[2,48,128]{2,1,0:T(8,128)S(1)} %copy-done.111, f32[2,128,128]{2,1,0:T(8,128)S(1)} %copy-done.88, f32[2,48,128]{2,1,0:T(8,128)S(1)} %copy-done.107, ...), kind=kOutput, calls=%fused_computation.110 | convolution fusion | flops 1218969600 | bytes 9748672 | tf_op jit(solution)/shard_map/jvp(bhts,bshp->bthp)/dot_general | solution.py:56
  274.4 13.0 %fusion.41 = f32[2,128,48,64]{1,3,2,0:T(8,128)S(1)} fusion(f32[2,128,48,64]{1,3,2,0:T(8,128)S(1)} %fusion.227, f32[2,128,48,64]{1,0,3,2:T(2,128)S(1)} %copy-done.12, f32[2,48,128]{2,1,0:T(8,128)S(1)} %copy-done.109, f32[2,128,128]{2,1,0:T(8,128)S(1)} %copy-done.86, f32[2,48,128]{2,1,0:T(8,128)S(1)} %copy-done.105, ...), kind=kOutput, calls=%fused_computation.112 | convolution fusion | flops 1218969600 | bytes 9748672 | tf_op jit(solution)/shard_map/jvp(bhts,bshp->bthp)/dot_general | solution.py:56
  307.0 11.8 convolution_add_fusion.1
  339.2 15.4 %multiply_reduce_fusion.17 = (f32[3072]{0:T(1024)}, f32[256,3072]{0,1:T(8,128)}, f32[256,3072]{0,1:T(8,128)}, f32[256,3072]{0,1:T(8,128)}, f32[3072]{0:T(1024)}, /*index=5*/f32[256,3072]{0,1:T(8,128)}) fusion(f32[256,3328]{0,1:T(8,128)S(1)} %copy-done.25, f32[256,6448]{0,1:T(8,128)} %fusion.194, f32[256,3072]{0,1:T(8,128)S(1)} %copy-done.10, ...), kind=kLoop, calls=%fused_computation.118 | loop fusion | flops 29878272 | bytes 44081152 | tf_op jit(solution)/shard_map/transpose(jvp())/reduce_sum | solution.py:78
  402.2 16.6 %fusion.29 = (f32[2,48,128]{2,1,0:T(8,128)}, f32[2,48,128]{2,1,0:T(8,128)}, f32[2,48,128]{2,1,0:T(8,128)}, f32[2,128,128]{2,1,0:T(8,128)S(1)}) fusion(f32[2,48,128]{2,1,0:T(8,128)S(1)} %copy-done.112, f32[2,128,128]{2,1,0:T(8,128)S(1)} %copy-done.89, f32[2,48,128]{2,1,0:T(8,128)S(1)} %copy-done.108, pred[2,128,128]{2,1,0:T(8,128)(4,1)S(1)} %copy-done.124, ...), kind=kOutput, calls=%fused_computation.83 | convolution fusion | flops 1231482880 | bytes 6832128 | tf_op jit(solution)/shard_map/transpose(jvp(bhts,bshp->bthp))/dot_general | solution.py:56
  439.9 9.0 while.70
  475.6 16.6 %fusion.27 = (f32[2,48,128]{2,1,0:T(8,128)}, f32[2,48,128]{2,1,0:T(8,128)}, f32[2,48,128]{2,1,0:T(8,128)}, f32[2,128,128]{2,1,0:T(8,128)S(1)}) fusion(f32[2,48,128]{2,1,0:T(8,128)S(1)} %copy-done.110, f32[2,128,128]{2,1,0:T(8,128)S(1)} %copy-done.87, f32[2,48,128]{2,1,0:T(8,128)S(1)} %copy-done.106, pred[2,128,128]{2,1,0:T(8,128)(4,1)S(1)} %copy-done.122, ...), kind=kOutput, calls=%fused_computation.81 | convolution fusion | flops 1231482880 | bytes 6832128 | tf_op jit(solution)/shard_map/transpose(jvp(bhts,bshp->bthp))/dot_general | solution.py:56
  539.3 12.3 %multiply_reduce_fusion.6 = (f32[3328]{0:T(1024)S(1)}, f32[3328]{0:T(1024)}, f32[3328]{0:T(1024)}, f32[3328]{0:T(1024)S(1)}, f32[3328]{0:T(1024)S(1)}, /*index=5*/f32[256,3328]{0,1:T(8,128)S(1)}) fusion(f32[256,3328]{0,1:T(8,128)} %slice.193, f32[256]{0:T(256)} %get-tuple-element.641, f32[256]{0:T(256)} %get-tuple-element.640, f32[256]{0:T(256)} %get-tuple-element.639, ...), kind=kLoop, calls=%fused_computation.68 | loop fusion | flops 19578624 | bytes 17108992 | tf_op jit(solution)/shard_map/transpose(jvp())/reduce_sum | solution.py:37
  551.7 10.2 multiply_reduce_fusion.10
  570.5 9.5 pad_add_fusion
  582.7 18.8 %fusion.192 = f32[1536,6448]{1,0:T(8,128)} fusion(f32[1536]{0:T(1024)S(1)} %copy-done.72, f32[256]{0:T(256)S(1)} %copy-done.97, bf16[2,256,1536]{2,1,0:T(8,128)(2,1)S(1)} %copy-done.33, f32[256,3072]{0,1:T(8,128)} %get-tuple-element.594, f32[256,3328]{0,1:T(8,128)S(1)} %pad_add_fusion.3, f32[256,48]{0,1:T(8,128)S(1)} %get-tuple-element.575), kind=kOutput, calls=%fused_computation.288 | convolution fusion | flops 5077438464 | bytes 47014912 | tf_op jit(solution)/shard_map/ld,lk->dk/dot_general | solution.py:163
  601.6 27.0 %convolution_add_fusion = f32[1536,6448]{1,0:T(8,128)} fusion(f32[1536,6448]{1,0:T(8,128)} %fusion.192, f32[256]{0:T(256)S(1)} %copy-done.119, f32[1536]{0:T(1024)S(1)} %copy-done.72, bf16[2,256,1536]{2,1,0:T(8,128)(2,1)S(1)} %copy-done.33, f32[256,3072]{0,1:T(8,128)} %get-tuple-element.620, f32[256,3328]{0,1:T(8,128)} %pad_add_fusion, ...), kind=kOutput, calls=%fused_computation.22 | convolution fusion | flops 5087342592 | bytes 86631424 | tf_op jit(solution)/shard_map/ld,lk->dk/dot_general | solution.py:163
  633.0 15.7 %fusion.213 = f32[256,1536]{1,0:T(8,128)} fusion(bf16[1536,6448]{1,0:T(8,128)(2,1)} %all-gather.4.cloned.1.call-done, f32[256,3072]{0,1:T(8,128)S(1)} %copy-done.41, f32[256,3328]{0,1:T(8,128)} %pad_add_fusion, f32[256,48]{0,1:T(8,128)S(1)} %get-tuple-element.629), kind=kOutput, calls=%fused_computation.355 | convolution fusion | flops 5075865600 | bytes 27983872 | tf_op jit(solution)/shard_map/lk,dk->ld/dot_general | solution.py:166
  648.8 368.4 %reduce-scatter.6.cloned.1.call-done = f32[96,6448]{1,0:T(8,128)} async-done(((f32[1536,6448]{1,0:T(8,128)}), f32[96,6448]{1,0:T(8,128)}) %reduce-scatter.6.cloned.1.call-update) | async-done | bytes 2476048 | tf_op jit(solution)/shard_map/reduce_scatter | solution.py:184
  1017.3 13.6 %fusion.134 = (f32[1536]{0:T(1024)S(1)}, f32[256]{0:T(256)S(1)}, f32[256]{0:T(256)S(1)}, f32[1536]{0:T(1024)S(1)}, f32[256,1536]{1,0:T(8,128)}) fusion(f32[256]{0:T(256)S(1)} %copy-done.98, bf16[2,256,1536]{2,1,0:T(8,128)(2,1)} %param.21, f32[1536]{0:T(1024)S(1)} %copy-done.72, f32[256]{0:T(256)S(1)} %copy-done.120, f32[256,1536]{1,0:T(8,128)} %fusion.213, ...), kind=kOutput, calls=%fused_computation.213 | convolution fusion | flops 5081367040 | bytes 31152128 | tf_op jit(solution)/shard_map/lk,dk->ld/dot_general | solution.py:166
  1031.1 59.7 %all-reduce.43 = (f32[1536]{0:T(1024)S(1)}, f32[3328]{0:T(1024)S(1)}, f32[3072]{0:T(1024)S(1)}) all-reduce(f32[1536]{0:T(1024)S(1)} %add.324, f32[3328]{0:T(1024)S(1)} %add.327, f32[3072]{0:T(1024)S(1)} %add.331), channel_id=2, replica_groups=mesh['fsdp'=16,'dp'=2] {'fsdp'}, use_global_device_ids=true, to_apply=%region_36.38.clone | all-reduce | flops 7936 | bytes 63488
  1091.3 38.2 %all-reduce.42 = (f32[48]{0:T(128)}, f32[48]{0:T(128)}, f32[48]{0:T(128)}) all-reduce(f32[48]{0:T(128)S(1)} %add.328, f32[48]{0:T(128)S(1)} %add_multiply_fusion, f32[48]{0:T(128)S(1)} %add.330), channel_id=1, replica_groups=mesh['fsdp'=16,'dp'=2] {'fsdp','dp'}, use_global_device_ids=true, to_apply=%region_56.58 | all-reduce | flops 144 | bytes 1152 | tf_op jit(solution)/shard_map/psum | solution.py:191
  1156.8 24.3 %all-reduce.49.cloned.1.call-done = (f32[96,6448]{1,0:T(8,128)}, f32[192,1536]{1,0:T(8,128)}) async-done(((f32[96,6448]{1,0:T(8,128)}, f32[192,1536]{1,0:T(8,128)}), (f32[96,6448]{1,0:T(8,128)}, f32[192,1536]{1,0:T(8,128)})) %all-reduce.49.cloned.1.call-update) | async-done | bytes 3655696 | tf_op jit(solution)/shard_map/psum | solution.py:190
  (579 shorter events, 364.9 us)
Async XLA Ops:
  7.2 75.1 %copy-start.144 = (bf16[4,208]{1,0:T(4,128)(2,1)S(1)}, bf16[4,208]{1,0:T(4,128)(2,1)}, u32[]{:S(2)}) copy-start(bf16[4,208]{1,0:T(4,128)(2,1)} %param.25) | copy-start | bytes 4996
  7.2 94.4 %copy-start.153 = (f32[48]{0:T(128)S(1)}, f32[48]{0:T(128)}, u32[]{:S(2)}) copy-start(f32[48]{0:T(128)} %param.28) | copy-start | bytes 580
  7.2 111.0 %all-gather.4.cloned.1.call-start = ((), (), s32[]{:S(2)}) async-start(), calls=%async_computation.3 | async-start | bytes 21307392 | tf_op jit(solution)/shard_map/all_gather | solution.py:113
  8.0 310.9 %all-gather.6.cloned.1.call-start = ((), (), s32[]{:S(2)}) async-start(), calls=%async_computation.4 | async-start | bytes 10027008 | tf_op jit(solution)/shard_map/all_gather | solution.py:141
  8.7 640.0 %reduce-scatter.8.cloned.1.call-start = ((), (), s32[]{:S(2)}) async-start(), calls=%async_computation.6 | async-start | bytes 20054016 | tf_op jit(solution)/shard_map/reduce_scatter | solution.py:188
  82.3 54.2 %copy-start.71 = (f32[1536]{0:T(1024)}, f32[1536]{0:T(1024)S(1)}, u32[]{:S(2)}) copy-start(f32[1536]{0:T(1024)S(1)} %convert_element_type.123) | copy-start | bytes 18436
  101.7 53.7 %copy-start.147 = (f32[48]{0:T(128)}, f32[48]{0:T(128)S(1)}, u32[]{:S(2)}) copy-start(f32[48]{0:T(128)S(1)} %exp.61) | copy-start | bytes 580
  102.6 236.6 %copy-start.53 = (f32[3072]{0:T(1024)}, f32[3072]{0:T(1024)S(1)}, u32[]{:S(2)}) copy-start(f32[3072]{0:T(1024)S(1)} %convert_element_type.130) | copy-start | bytes 36868
  159.1 92.7 %copy-start.44 = (f32[2,128,48]{2,1,0:T(8,128)}, f32[2,128,48]{2,1,0:T(8,128)S(1)}, u32[]{:S(2)}) copy-start(f32[2,128,48]{2,1,0:T(8,128)S(1)} %reduce_window_sum.34) | copy-start | bytes 147460
  294.8 44.4 %copy-start.3 = (f32[256,3072]{0,1:T(8,128)}, f32[256,3072]{0,1:T(8,128)S(1)}, u32[]{:S(2)}) copy-start(f32[256,3072]{0,1:T(8,128)S(1)} %get-tuple-element.585) | copy-start | bytes 9437188
  295.4 43.8 %copy-start.114 = (f32[256]{0:T(256)}, f32[256]{0:T(256)S(1)}, u32[]{:S(2)}) copy-start(f32[256]{0:T(256)S(1)} %fusion.205) | copy-start | bytes 3076
  318.8 698.3 %reduce-scatter.6.cloned.1.call-start = ((), (), s32[]{:S(2)}) async-start(), calls=%async_computation.5 | async-start | bytes 42614784 | tf_op jit(solution)/shard_map/reduce_scatter | solution.py:184
  628.6 521.1 %reduce-scatter.10.cloned.1.call-start = ((), (), s32[]{:S(2)}) async-start(), calls=%async_computation.7 | async-start | bytes 1810432
  633.0 548.1 %all-reduce.49.cloned.1.call-start = ((), (), s32[]{:S(2)}) async-start(), calls=%async_computation.8 | async-start | bytes 7372800 | tf_op jit(solution)/shard_map/psum | solution.py:190
  648.8 368.4 %copy-start.98 = (f32[256]{0:T(256)S(1)}, f32[256]{0:T(256)}, u32[]{:S(2)}) copy-start(f32[256]{0:T(256)} %copy-done.96) | copy-start | bytes 3076
  648.8 368.4 %copy-start.120 = (f32[256]{0:T(256)S(1)}, f32[256]{0:T(256)}, u32[]{:S(2)}) copy-start(f32[256]{0:T(256)} %copy-done.118) | copy-start | bytes 3076
  1017.2 73.8 %copy-start.155 = (f32[48]{0:T(128)S(1)}, f32[48]{0:T(128)}, u32[]{:S(2)}) copy-start(f32[48]{0:T(128)} %get-tuple-element.574) | copy-start | bytes 580
  1017.3 73.8 %copy-start.156 = (f32[48]{0:T(128)S(1)}, f32[48]{0:T(128)}, u32[]{:S(2)}) copy-start(f32[48]{0:T(128)} %get-tuple-element.628) | copy-start | bytes 580
  1017.3 74.0 %copy-start.148 = (f32[48]{0:T(128)S(1)}, f32[48]{0:T(128)}, u32[]{:S(2)}) copy-start(f32[48]{0:T(128)} %get-tuple-element.611) | copy-start | bytes 580
  1017.3 74.0 %copy-start.149 = (f32[48]{0:T(128)S(1)}, f32[48]{0:T(128)}, u32[]{:S(2)}) copy-start(f32[48]{0:T(128)} %get-tuple-element.627) | copy-start | bytes 580
  1017.3 74.0 %copy-start.154 = (f32[48]{0:T(128)S(1)}, f32[48]{0:T(128)}, u32[]{:S(2)}) copy-start(f32[48]{0:T(128)} %param.28) | copy-start | bytes 580
  1017.3 112.3 %copy-start.4 = (f32[256,3072]{0,1:T(8,128)S(1)}, f32[256,3072]{0,1:T(8,128)}, u32[]{:S(2)}) copy-start(f32[256,3072]{0,1:T(8,128)} %copy-done.3) | copy-start | bytes 9437188
  1017.3 112.3 %copy-start.54 = (f32[3072]{0:T(1024)S(1)}, f32[3072]{0:T(1024)}, u32[]{:S(2)}) copy-start(f32[3072]{0:T(1024)} %copy-done.53) | copy-start | bytes 36868
  1017.3 112.3 %copy-start.115 = (f32[256]{0:T(256)S(1)}, f32[256]{0:T(256)}, u32[]{:S(2)}) copy-start(f32[256]{0:T(256)} %copy-done.114) | copy-start | bytes 3076
  (152 other events, 1216.1 us)
Sparse Core Ops, SparseCore 0:
  9.6 108.5 all-gather.3
  120.5 81.1 all-gather.5
  318.9 194.3 reduce-scatter.7
  628.7 388.3 reduce-scatter.5
  1021.3 59.4 reduce-scatter.9
  1082.9 98.1 all-reduce.48
where the time goes:
time: 1200 us; the launch traced here: 1190 us
  waiting for transfers between devices  405 us (34%)
  matrix products  303 us (25%)
  blocking collectives  188 us (16%)
  other arithmetic  148 us (12%)
  local copies, waits for them, and re-layouts  128 us (11%)
  between operations  20.6 us (2%)
    reduce_scatter x1, waiting for transfers between devices, local(): lax.psum_scatter(total_in, 'fsdp', scatter_dimension=0, tiled=True)  368 us
    unnamed x2, blocking collectives  126 us
    dot_general x6, matrix products, mixer(): jnp.einsum('bhts,bshp->bthp', weights, head_inputs, precision=highest)  74.3 us
    dot_general x2, matrix products, local(): jnp.einsum('ld,lk->dk', normed, proj_back, preferred_element_type=jnp.flo...  45.8 us
    psum x1, blocking collectives, local(): lax.psum((total_offset, total_rate, total_skip), ('fsdp', 'dp'))  38.2 us
    dot_general x6, matrix products, mixer(): jnp.einsum('bhs,bshp,bsn->bhpn', end_weight, head_inputs, b_rows, precisi...  35.8 us
    dot_general x6, matrix products, mixer(): jnp.einsum('btn,bhpn->bthp', c_rows, entering, precision=highest)  33.3 us
    unnamed x342, local copies, waits for them, and re-layouts  29.9 us
  transfers between devices with their start and end apart: 6, of which 3 were waited for; matrix products, arithmetic and copies ran while one was open for 46% of the time, Pallas kernels for 0%

commit v1 on v0

v1 whole, which is shorter than its diff:
```python
import functools

import jax
import jax.numpy as jnp
from jax import lax
from jax.experimental import pallas as pl
from jax.experimental.pallas import tpu as pltpu
from jax.sharding import PartitionSpec as P

f32, bf16 = jnp.float32, jnp.bfloat16
highest = lax.Precision.HIGHEST
epsilon = 1e-05
LANES = 128
BLOCK = 128
GROUP = 512
PAIRS = GROUP // LANES
NT = (((1,), (1,)), ((), ()))
NN = (((1,), (0,)), ((), ()))


def dot(a, b, dims=NN, precision=None):
    return lax.dot_general(a, b, dims, precision=precision, preferred_element_type=f32)


def sigmoid(v):
    return 0.5 + 0.5 * jnp.tanh(0.5 * v)


def conv_taps(xin, masks):
    taps = []
    for shift in (3, 2, 1):
        taps.append(pltpu.roll(xin, shift, 0) * masks[3 - shift])
    taps.append(xin)
    return taps


def conv_sum(taps, cw):
    total = cw[4:5, :] + cw[3:4, :] * taps[3]
    for k in range(3):
        total = total + cw[k : k + 1, :] * taps[k]
    return total


def conv_back(gsum, xin, cw, masks, length):
    grads = []
    gx = cw[3:4, :] * gsum
    for shift in (3, 2, 1):
        masked = gsum * masks[3 - shift]
        grads.append(jnp.sum(masked * pltpu.roll(xin, shift, 0), axis=0, keepdims=True))
        gx = gx + cw[3 - shift : 4 - shift, :] * pltpu.roll(masked, length - shift, 0)
    grads.append(jnp.sum(gsum * xin, axis=0, keepdims=True))
    grads.append(jnp.sum(gsum, axis=0, keepdims=True))
    return gx, grads


def prologue(heads, bc_ref, dtr_ref, segc_ref, segr_ref, cwbc_ref, hp_ref, mask_s, b_s, c_s, dt_s, cum_s, cumt_s, ef_s, la_s, sp_s):
    length = bc_ref.shape[0]
    segc = segc_ref[0]
    for j in range(3):
        mask_s[2 - j] = jnp.broadcast_to(segc[:, j + 1 : j + 2], (length, LANES))
    masks = [mask_s[k] for k in range(3)]
    for half, ref in ((0, b_s), (1, c_s)):
        sl = slice(half * LANES, (half + 1) * LANES)
        taps = conv_taps(bc_ref[:, sl], masks)
        summed = conv_sum(taps, cwbc_ref[:, sl])
        ref[...] = summed * sigmoid(summed)
    lane = lax.broadcasted_iota(jnp.int32, (length, LANES), 1)
    raw = jnp.where(lane < heads, dtr_ref[...] + hp_ref[0:1, :], 0.0)
    soft = jnp.maximum(raw, 0.0) + jnp.log1p(jnp.exp(-jnp.abs(raw)))
    dt = jnp.where(lane < heads, soft, 0.0)
    la = -dt * jnp.exp(hp_ref[1:2, :])
    row = lax.broadcasted_iota(jnp.int32, (length, length), 0)
    col = lax.broadcasted_iota(jnp.int32, (length, length), 1)
    tri = jnp.where(row >= col, 1.0, 0.0).astype(f32)
    cum = dot(tri, la, precision=highest)
    dt_s[...] = dt
    la_s[...] = la
    cum_s[...] = cum
    cumt_s[...] = cum.T
    sp_s[...] = sigmoid(raw)
    mid = cum[BLOCK - 1 : BLOCK, :]
    ef_s[:BLOCK] = jnp.exp(jnp.minimum(mid - cum[:BLOCK], 0.0))
    ef_s[BLOCK:] = jnp.exp(jnp.minimum(cum[BLOCK:] - mid, 0.0))
    same = (segc[:, 0:1] == segr_ref[0, 0:1, :]).astype(f32)
    return row, col, same


def headpick(first, shape):
    source = lax.broadcasted_iota(jnp.int32, shape, 0) // 64
    target = lax.broadcasted_iota(jnp.int32, shape, 1)
    source = source - 2 * (source // 2)
    return jnp.where(target == source + first, 1.0, 0.0).astype(bf16)


def headsum(value, pick):
    hi = value.astype(bf16)
    lo = (value - hi.astype(f32)).astype(bf16)
    return dot(jnp.concatenate([hi, lo], axis=1), pick)


def fwd_kernel(heads, z_ref, x_ref, bc_ref, dtr_ref, gm_ref, segc_ref, segr_ref, cwx_ref, cwbc_ref, hp_ref, cp_ref,
               mixed_ref, gz_ref, gy_ref, rs_ref, gg_ref,
               mask_s, b_s, c_s, dt_s, cum_s, cumt_s, ef_s, la_s, sp_s, sm_s, ssm_s, yd_s, u_s, st_s, rs_s):
    phase, group = pl.program_id(1), pl.program_id(2)
    length = z_ref.shape[0]
    lane = lax.broadcasted_iota(jnp.int32, (length, LANES), 1)
    first = lane < 64
    half = lax.broadcasted_iota(jnp.int32, (BLOCK, LANES), 1) < 64

    @pl.when((phase == 0) & (group == 0))
    def _():
        row, col, same = prologue(heads, bc_ref, dtr_ref, segc_ref, segr_ref, cwbc_ref, hp_ref, mask_s, b_s, c_s, dt_s, cum_s, cumt_s, ef_s, la_s, sp_s)
        scores = dot(c_s[...], b_s[...], NT, precision=highest)
        sm_s[...] = jnp.where(row >= col, scores * same, 0.0)
        st_s[...] = jnp.zeros_like(st_s)

    width = jnp.int32(8)
    shift = lax.rem(jnp.int32(LANES) - width * group, jnp.int32(LANES))

    @pl.when(phase == 0)
    def _():
        masks = [mask_s[k] for k in range(3)]
        dtg = pltpu.roll(dt_s[...], shift, 1)
        cumg = pltpu.roll(cum_s[...], shift, 1)
        efg = pltpu.roll(ef_s[...], shift, 1)
        cumt = cumt_s[pl.ds(pl.multiple_of(group * 8, 8), 8), :]
        square, across = st_s[0], st_s[1]
        for j in range(PAIRS):
            sl = slice(j * LANES, (j + 1) * LANES)
            place = pl.ds(pl.multiple_of(group * GROUP + j * LANES, LANES), LANES)
            xin = x_ref[:, sl]
            summed = conv_sum(conv_taps(xin, masks), cwx_ref[:, sl])
            xs = summed * sigmoid(summed)
            dtb = jnp.where(first, dtg[:, 2 * j : 2 * j + 1], dtg[:, 2 * j + 1 : 2 * j + 2])
            efb = jnp.where(first, efg[:, 2 * j : 2 * j + 1], efg[:, 2 * j + 1 : 2 * j + 2])
            xd = xs * dtb
            for i in range(2):
                rows = slice(i * BLOCK, (i + 1) * BLOCK)
                part = xd[rows]
                stack = jnp.concatenate([jnp.where(half, part, 0.0), jnp.where(half, 0.0, part)], axis=0).astype(bf16)
                decays = []
                for h in range(2):
                    arg = cumg[rows, 2 * j + h : 2 * j + h + 1] - cumt[2 * j + h : 2 * j + h + 1, rows]
                    decays.append((jnp.exp(jnp.minimum(arg, 0.0)) * sm_s[rows, rows]).astype(bf16))
                yd_s[rows, place] = dot(jnp.concatenate(decays, axis=1), stack)
            far = (xd[:BLOCK] * efb[:BLOCK]).astype(bf16)
            u = dot(sm_s[BLOCK:, :BLOCK].astype(bf16), far)
            u_s[:, place] = u
            base = yd_s[:, place] + cp_ref[0:1, sl] * xs
            ssm = jnp.concatenate([base[:BLOCK], base[BLOCK:] + efb[BLOCK:] * u], axis=0)
            ssm_s[:, place] = ssm
            zin = z_ref[:, sl]
            gated = ssm * (zin * sigmoid(zin))
            square = square + gated * gated
            across = across + gm_ref[:, sl] * cp_ref[1:2, sl] * gated
        st_s[0] = square
        st_s[1] = across

    @pl.when((phase == 1) & (group == 0))
    def _():
        inner = heads * 64
        mean = jnp.sum(st_s[0], axis=1, keepdims=True) / inner
        scale = lax.rsqrt(mean + epsilon)
        inward = jnp.sum(st_s[1], axis=1, keepdims=True) / inner
        st_s[0] = jnp.broadcast_to(scale, (length, LANES))
        st_s[1] = jnp.broadcast_to(scale * scale * scale * inward, (length, LANES))
        rs_s[...] = jnp.zeros_like(rs_s)

    @pl.when(phase == 1)
    def _():
        scale, lean = st_s[0], st_s[1]
        efg = pltpu.roll(ef_s[...], shift, 1)
        total = rs_s[...]
        for j in range(PAIRS):
            sl = slice(j * LANES, (j + 1) * LANES)
            place = pl.ds(pl.multiple_of(group * GROUP + j * LANES, LANES), LANES)
            zin = z_ref[:, sl]
            sg = sigmoid(zin)
            silu = zin * sg
            dsilu = sg + silu * (1.0 - sg)
            ssm = ssm_s[:, place]
            gated = ssm * silu
            unit = gated * scale
            gain = cp_ref[1:2, sl]
            gm = gm_ref[:, sl]
            mixed_ref[:, sl] = (unit * gain).astype(bf16)
            gg_ref[0, :, sl] = jnp.broadcast_to(jnp.sum(gm * unit, axis=0, keepdims=True), (8, LANES))
            ggated = scale * (gm * gain) - gated * lean
            gz_ref[:, sl] = (ggated * ssm * dsilu).astype(bf16)
            gy = ggated * silu
            gy_ref[:, sl] = gy
            efb = jnp.where(first, efg[:, 2 * j : 2 * j + 1], efg[:, 2 * j + 1 : 2 * j + 2])
            near = gy.astype(bf16).astype(f32) * yd_s[:, place]
            fare = (gy[BLOCK:] * efb[BLOCK:]).astype(bf16).astype(f32) * u_s[:, place]
            value = jnp.concatenate([near[:BLOCK], near[BLOCK:] + fare], axis=0)
            total = total + headsum(value, headpick(8 * group + 2 * j, (2 * LANES, LANES)))
        rs_s[...] = total
        rs_ref[0] = total


def bwd_kernel(heads, x_ref, bc_ref, dtr_ref, gy_ref, rs_ref, segc_ref, segr_ref, cwx_ref, cwbc_ref, hp_ref, cp_ref,
               px_ref, pr_ref, gp_ref, gbc_ref, gh_ref,
               mask_s, b_s, c_s, dt_s, cum_s, cumt_s, ef_s, la_s, sp_s, smt_s, gst_s, gc_s, gd_s):
    group = pl.program_id(1)
    length = x_ref.shape[0]
    lane = lax.broadcasted_iota(jnp.int32, (length, LANES), 1)
    first = lane < 64
    half = lax.broadcasted_iota(jnp.int32, (BLOCK, LANES), 1) < 64

    @pl.when(group == 0)
    def _():
        row, col, same = prologue(heads, bc_ref, dtr_ref, segc_ref, segr_ref, cwbc_ref, hp_ref, mask_s, b_s, c_s, dt_s, cum_s, cumt_s, ef_s, la_s, sp_s)
        scores = dot(b_s[...], c_s[...], NT, precision=highest)
        smt_s[...] = jnp.where(row <= col, scores * same, 0.0)
        gst_s[...] = jnp.zeros_like(gst_s)
        gc_s[...] = jnp.zeros_like(gc_s)
        gd_s[...] = jnp.zeros_like(gd_s)

    shift = lax.rem(jnp.int32(LANES) - jnp.int32(8) * group, jnp.int32(LANES))
    masks = [mask_s[k] for k in range(3)]
    dtg = pltpu.roll(dt_s[...], shift, 1)
    cumg = pltpu.roll(cum_s[...], shift, 1)
    efg = pltpu.roll(ef_s[...], shift, 1)
    cumt = cumt_s[pl.ds(pl.multiple_of(group * 8, 8), 8), :]
    gcum, gdir = gc_s[...], gd_s[...]
    for j in range(PAIRS):
        sl = slice(j * LANES, (j + 1) * LANES)
        xin = x_ref[:, sl]
        cw = cwx_ref[:, sl]
        summed = conv_sum(conv_taps(xin, masks), cw)
        sg = sigmoid(summed)
        xs = summed * sg
        dtb = jnp.where(first, dtg[:, 2 * j : 2 * j + 1], dtg[:, 2 * j + 1 : 2 * j + 2])
        efb = jnp.where(first, efg[:, 2 * j : 2 * j + 1], efg[:, 2 * j + 1 : 2 * j + 2])
        xd = xs * dtb
        gy = gy_ref[:, sl]
        gyb = gy.astype(bf16)
        inner = []
        for i in range(2):
            rows = slice(i * BLOCK, (i + 1) * BLOCK)
            part, gpart = xd[rows], gy[rows]
            stack = jnp.concatenate([jnp.where(half, part, 0.0), jnp.where(half, 0.0, part)], axis=0).astype(bf16)
            gstack = jnp.concatenate([jnp.where(half, gpart, 0.0), jnp.where(half, 0.0, gpart)], axis=0).astype(bf16)
            gw = dot(stack, gyb[rows], NT)
            weights = []
            gscore = gst_s[rows, rows]
            for h in range(2):
                arg = cumt[2 * j + h : 2 * j + h + 1, rows] - cumg[rows, 2 * j + h : 2 * j + h + 1]
                decay = jnp.exp(jnp.minimum(arg, 0.0))
                weights.append((decay * smt_s[rows, rows]).astype(bf16))
                gscore = gscore + gw[h * BLOCK : (h + 1) * BLOCK] * decay
            gst_s[rows, rows] = gscore
            inner.append(dot(jnp.concatenate(weights, axis=1), gstack))
        far = (xd[:BLOCK] * efb[:BLOCK]).astype(bf16)
        ge = (gy[BLOCK:] * efb[BLOCK:]).astype(bf16)
        gst_s[:BLOCK, BLOCK:] += dot(far, ge, NT)
        gfar = dot(smt_s[:BLOCK, BLOCK:].astype(bf16), ge)
        xdb = xd.astype(bf16).astype(f32)
        fall0 = xdb[:BLOCK] * inner[0] + far.astype(f32) * gfar
        fall = jnp.concatenate([fall0, xdb[BLOCK:] * inner[1]], axis=0)
        gxd = jnp.concatenate([inner[0] + efb[:BLOCK] * gfar, inner[1]], axis=0)
        sums = headsum(jnp.concatenate([fall, xs * gxd], axis=0), headpick(8 * group + 2 * j, (2 * LANES, LANES)))
        gcum = gcum - sums[:length]
        gdir = gdir + sums[length:]
        gxs = cp_ref[0:1, sl] * gy + dtb * gxd
        gsum = gxs * (sg + xs * (1.0 - sg))
        gx, grads = conv_back(gsum, xin, cw, masks, length)
        px_ref[:, sl] = gx.astype(bf16)
        grads.append(jnp.sum(gy * xs, axis=0, keepdims=True))
        for k, value in enumerate(grads):
            gp_ref[0, k : k + 1, sl] = value
        gp_ref[0, 6:8, sl] = jnp.zeros((2, LANES), f32)
    gc_s[...] = gcum
    gd_s[...] = gdir

    @pl.when(group == pl.num_programs(1) - 1)
    def _():
        row = lax.broadcasted_iota(jnp.int32, (length, length), 0)
        col = lax.broadcasted_iota(jnp.int32, (length, length), 1)
        same = segc_ref[0][:, 0:1] == segr_ref[0, 0:1, :]
        gscore = jnp.where((row <= col) & same, gst_s[...], 0.0)
        backs = (dot(gscore, c_s[...], precision=highest), dot(gscore.T, b_s[...], precision=highest))
        for part in range(2):
            sl = slice(part * LANES, (part + 1) * LANES)
            xin = bc_ref[:, sl]
            cw = cwbc_ref[:, sl]
            summed = conv_sum(conv_taps(xin, masks), cw)
            sg = sigmoid(summed)
            gsum = backs[part] * (sg + summed * sg * (1.0 - sg))
            gx, grads = conv_back(gsum, xin, cw, masks, length)
            pr_ref[:, sl] = gx.astype(bf16)
            for k, value in enumerate(grads):
                gbc_ref[0, k : k + 1, sl] = value
            gbc_ref[0, 5:8, sl] = jnp.zeros((3, LANES), f32)
        upper = jnp.where(row <= col, 1.0, 0.0).astype(f32)
        gla = dot(upper, gc_s[...] + rs_ref[0], precision=highest)
        graw = (gd_s[...] - gla * jnp.exp(hp_ref[1:2, :])) * sp_s[...]
        graw = jnp.where(lane < heads, graw, 0.0)
        pr_ref[:, 2 * LANES :] = graw.astype(bf16)
        gh_ref[0, 0:1] = jnp.sum(graw, axis=0, keepdims=True)
        gh_ref[0, 1:2] = jnp.sum(jnp.where(lane < heads, gla * la_s[...], 0.0), axis=0, keepdims=True)
        gh_ref[0, 2:8] = jnp.zeros((6, LANES), f32)


def small_scratch(length):
    return [
        pltpu.VMEM((3, length, LANES), f32),
        pltpu.VMEM((length, LANES), f32),
        pltpu.VMEM((length, LANES), f32),
        pltpu.VMEM((length, LANES), f32),
        pltpu.VMEM((length, LANES), f32),
        pltpu.VMEM((LANES, length), f32),
        pltpu.VMEM((length, LANES), f32),
        pltpu.VMEM((length, LANES), f32),
        pltpu.VMEM((length, LANES), f32),
    ]


def mixer_forward(projected, gm, segc, segr, cw, hp, cp, heads, state):
    seqs, length = segc.shape[:2]
    inner = gm.shape[1]
    groups = inner // GROUP
    rows = seqs * length
    kernel = functools.partial(fwd_kernel, heads)
    out_row = lambda b, p, g: (b, g * p)
    return pl.pallas_call(
        kernel,
        grid=(seqs, 2, groups),
        in_specs=[
            pl.BlockSpec((length, GROUP), lambda b, p, g: (b, g)),
            pl.BlockSpec((length, GROUP), lambda b, p, g: (b, groups + g * (1 - p) + (groups - 1) * p)),
            pl.BlockSpec((length, 2 * state), lambda b, p, g: (b, 2 * inner // (2 * state))),
            pl.BlockSpec((length, LANES), lambda b, p, g: (b, (2 * inner + 2 * state) // LANES)),
            pl.BlockSpec((length, GROUP), lambda b, p, g: (b, g)),
            pl.BlockSpec((1, length, LANES), lambda b, p, g: (b, 0, 0)),
            pl.BlockSpec((1, 8, length), lambda b, p, g: (b, 0, 0)),
            pl.BlockSpec((8, GROUP), lambda b, p, g: (0, g)),
            pl.BlockSpec((8, 2 * state), lambda b, p, g: (0, inner // (2 * state))),
            pl.BlockSpec((8, LANES), lambda b, p, g: (0, 0)),
            pl.BlockSpec((8, GROUP), lambda b, p, g: (0, g)),
        ],
        out_specs=[
            pl.BlockSpec((length, GROUP), out_row),
            pl.BlockSpec((length, GROUP), out_row),
            pl.BlockSpec((length, GROUP), out_row),
            pl.BlockSpec((1, length, LANES), lambda b, p, g: (b, 0, 0)),
            pl.BlockSpec((1, 8, GROUP), lambda b, p, g: (b, 0, g * p)),
        ],
        out_shape=[
            jax.ShapeDtypeStruct((rows, inner), bf16),
            jax.ShapeDtypeStruct((rows, inner), bf16),
            jax.ShapeDtypeStruct((rows, inner), f32),
            jax.ShapeDtypeStruct((seqs, length, LANES), f32),
            jax.ShapeDtypeStruct((seqs, 8, inner), f32),
        ],
        scratch_shapes=small_scratch(length) + [
            pltpu.VMEM((length, length), f32),
            pltpu.VMEM((length, inner), f32),
            pltpu.VMEM((length, inner), f32),
            pltpu.VMEM((length - BLOCK, inner), f32),
            pltpu.VMEM((2, length, LANES), f32),
            pltpu.VMEM((length, LANES), f32),
        ],
        compiler_params=pltpu.CompilerParams(vmem_limit_bytes=48 << 20),
        cost_estimate=pl.CostEstimate(flops=10**10, bytes_accessed=45 * 10**6, transcendentals=10**7),
        name="mixer_forward",
    )(projected, projected, projected, projected, gm, segc, segr, cw, cw, hp, cp)


def mixer_backward(projected, gy, rs, segc, segr, cw, hp, cp, heads, state):
    seqs, length = segc.shape[:2]
    inner = gy.shape[1]
    groups = inner // GROUP
    rows = seqs * length
    kernel = functools.partial(bwd_kernel, heads)
    return pl.pallas_call(
        kernel,
        grid=(seqs, groups),
        in_specs=[
            pl.BlockSpec((length, GROUP), lambda b, g: (b, groups + g)),
            pl.BlockSpec((length, 2 * state), lambda b, g: (b, 2 * inner // (2 * state))),
            pl.BlockSpec((length, LANES), lambda b, g: (b, (2 * inner + 2 * state) // LANES)),
            pl.BlockSpec((length, GROUP), lambda b, g: (b, g)),
            pl.BlockSpec((1, length, LANES), lambda b, g: (b, 0, 0)),
            pl.BlockSpec((1, length, LANES), lambda b, g: (b, 0, 0)),
            pl.BlockSpec((1, 8, length), lambda b, g: (b, 0, 0)),
            pl.BlockSpec((8, GROUP), lambda b, g: (0, g)),
            pl.BlockSpec((8, 2 * state), lambda b, g: (0, inner // (2 * state))),
            pl.BlockSpec((8, LANES), lambda b, g: (0, 0)),
            pl.BlockSpec((8, GROUP), lambda b, g: (0, g)),
        ],
        out_specs=[
            pl.BlockSpec((length, GROUP), lambda b, g: (b, g)),
            pl.BlockSpec((length, 3 * LANES), lambda b, g: (b, 0)),
            pl.BlockSpec((1, 8, GROUP), lambda b, g: (b, 0, g)),
            pl.BlockSpec((1, 8, 2 * state), lambda b, g: (b, 0, 0)),
            pl.BlockSpec((1, 8, LANES), lambda b, g: (b, 0, 0)),
        ],
        out_shape=[
            jax.ShapeDtypeStruct((rows, inner), bf16),
            jax.ShapeDtypeStruct((rows, 3 * LANES), bf16),
            jax.ShapeDtypeStruct((seqs, 8, inner), f32),
            jax.ShapeDtypeStruct((seqs, 8, 2 * state), f32),
            jax.ShapeDtypeStruct((seqs, 8, LANES), f32),
        ],
        scratch_shapes=small_scratch(length) + [
            pltpu.VMEM((length, length), f32),
            pltpu.VMEM((length, length), f32),
            pltpu.VMEM((length, LANES), f32),
            pltpu.VMEM((length, LANES), f32),
        ],
        compiler_params=pltpu.CompilerParams(vmem_limit_bytes=48 << 20),
        cost_estimate=pl.CostEstimate(flops=10**10, bytes_accessed=30 * 10**6, transcendentals=10**7),
        name="mixer_backward",
    )(projected, projected, projected, gy, rs, segc, segr, cw, cw, hp, cp)


def pad_lanes(v, width=LANES):
    return jnp.pad(v, ((0, 0), (0, width - v.shape[1])))


def mixer_tables(segments, kernel_full, shift_full, dt_bias, a_log, d_skip, gate_full):
    taps = kernel_full.shape[0]
    seqs, length = segments.shape
    columns = [segments.astype(f32)]
    where = jnp.arange(length)[None, :]
    for j in range(1, taps):
        before = jnp.pad(segments, ((0, 0), (j, 0)))[:, :length]
        columns.append(((before == segments) & (where >= j)).astype(f32))
    segc = jnp.pad(jnp.stack(columns, axis=-1), ((0, 0), (0, 0), (0, LANES - taps)))
    segr = jnp.broadcast_to(segments.astype(f32)[:, None, :], (seqs, 8, length))
    cw = jnp.concatenate([kernel_full.astype(f32), jnp.broadcast_to(shift_full.astype(f32)[None], (8 - taps, shift_full.shape[0]))])
    hp = pad_lanes(jnp.concatenate([dt_bias[None], jnp.broadcast_to(a_log[None], (7, a_log.shape[0]))]))
    heads = dt_bias.shape[0]
    size = gate_full.shape[0] // heads
    cp = jnp.concatenate([jnp.repeat(d_skip, size)[None], jnp.broadcast_to(gate_full.astype(f32)[None], (7, gate_full.shape[0]))])
    return segc, segr, cw, hp, cp


MESH = pl.DeviceIdType.MESH
PIECES = 3


def ring_place(chip, chips):
    wide = chips // 4
    z, q = chip // wide, chip % wide
    up = 1 + 3 * q + jnp.where(q % 2 == 0, z - 1, 3 - z)
    back = jnp.where(q == 0, 0, 4 * wide - q)
    return jnp.where(z == 0, back, up)


def ring_chip(place, chips):
    wide = chips // 4
    place = place % chips
    q = (place - 1 + chips) % chips // 3
    r = (place - 1 + chips) % chips % 3
    z = jnp.where(q % 2 == 0, 1 + r, 3 - r)
    inner = z * wide + q
    outer = (4 * wide - place) % (4 * wide)
    return jnp.where((place == 0) | (place > 3 * wide), outer, inner)


def gather_kernel(chips, count, *refs):
    ins, outs = refs[:count], refs[count : 2 * count]
    ring_send, ring_recv, far_send, far_recv, pair_send, pair_recv, own_sem = refs[2 * count :]
    me = lax.axis_index("fsdp")
    plane = lax.axis_index("dp")
    chip, core = me // 2, me % 2
    place = ring_place(chip, chips)
    right = 2 * ring_chip(place + 1, chips) + core
    left = 2 * ring_chip(place + chips - 1, chips) + core
    pair = {"fsdp": me + 1 - 2 * core}
    peer = {"dp": 1 - plane}
    ways = ({"fsdp": right}, {"fsdp": left})

    barrier = pltpu.get_barrier_semaphore()
    for other in (ways[0], ways[1], pair, peer):
        pl.semaphore_signal(barrier, inc=1, device_id=other, device_id_type=MESH)
    pl.semaphore_wait(barrier, 4)

    half = chips // 2
    whole = [k == count - 1 for k in range(count)]

    def steps(way, slot):
        return half if way == slot else half - 1

    def owner(way, step):
        move = -step if way == 0 else step
        return 2 * ring_chip(place + move + chips, chips) + core

    def part(refs, k, index, slot):
        if whole[k]:
            return refs[k].at[index]
        piece = 0 if slot == 0 else 1 + plane
        return refs[k].at[index, piece]

    def mine(k, slot):
        if whole[k]:
            return ins[k]
        piece = 0 if slot == 0 else 1 + plane
        return ins[k].at[piece]

    def slots(k):
        return (0,) if whole[k] else (0, 1)

    pending = []

    def send(source, target, send_sem, recv_sem, device):
        copy = pltpu.make_async_remote_copy(
            src_ref=source, dst_ref=target, send_sem=send_sem, recv_sem=recv_sem, device_id=device, device_id_type=MESH)
        copy.start()
        pending.append(copy)

    def arrived(target, send_sem, recv_sem):
        pltpu.make_async_remote_copy(
            src_ref=target, dst_ref=target, send_sem=send_sem, recv_sem=recv_sem, device_id=pair, device_id_type=MESH).wait_recv()

    def ring_sem(sem, way, step, k, slot):
        return sem.at[(way * half + step - 1) * 2 * count + 2 * k + slot]

    def far_sem(sem, way, step, k):
        return sem.at[(way * half + step - 1) * count + k]

    def pair_sem(sem, turn, k, slot):
        return sem.at[(turn * count + k) * 3 + slot]

    def turn(way, step):
        return 1 + (step - 1) * 2 + way

    local = []
    for k in range(count):
        for slot in slots(k):
            for way in range(2):
                send(mine(k, slot), part(outs, k, me, slot), ring_sem(ring_send, way, 1, k, slot), ring_sem(ring_recv, way, 1, k, slot), ways[way])
        send(ins[k], outs[k].at[me], pair_sem(pair_send, 0, k, 0), pair_sem(pair_recv, 0, k, 0), pair)
        copy = pltpu.make_async_copy(ins[k], outs[k].at[me], own_sem.at[k])
        copy.start()
        local.append(copy)

    def from_peer(way, step):
        index = owner(way, step)
        for k in range(count):
            if whole[k] or step > steps(way, 1):
                continue
            target = outs[k].at[index, 2 - plane]
            arrived(target, far_sem(far_send, way, step, k), far_sem(far_recv, way, step, k))
            send(target, target, pair_sem(pair_send, turn(way, step), k, 2), pair_sem(pair_recv, turn(way, step), k, 2), pair)

    for step in range(1, half + 1):
        for way in range(2):
            index = owner(way, step)
            for k in range(count):
                for slot in slots(k):
                    if step > steps(way, slot):
                        continue
                    target = part(outs, k, index, slot)
                    arrived(target, ring_sem(ring_send, way, step, k, slot), ring_sem(ring_recv, way, step, k, slot))
                    if step + 1 <= steps(way, slot):
                        send(target, target, ring_sem(ring_send, way, step + 1, k, slot), ring_sem(ring_recv, way, step + 1, k, slot), ways[way])
                    if slot == 1:
                        send(target, target, far_sem(far_send, way, step, k), far_sem(far_recv, way, step, k), peer)
                    send(target, target, pair_sem(pair_send, turn(way, step), k, slot), pair_sem(pair_recv, turn(way, step), k, slot), pair)
        if step > 1:
            for way in range(2):
                from_peer(way, step - 1)
    for way in range(2):
        from_peer(way, half)
    for k in range(count):
        other = outs[k].at[me + 1 - 2 * core]
        arrived(other, pair_sem(pair_send, 0, k, 0), pair_sem(pair_recv, 0, k, 0))
    for step in range(1, half + 1):
        for way in range(2):
            index = owner(way, step) + 1 - 2 * core
            for k in range(count):
                for slot in slots(k) + (() if whole[k] else (2,)):
                    if step > steps(way, min(slot, 1)):
                        continue
                    if slot == 2:
                        target = outs[k].at[index, 2 - plane]
                    else:
                        target = part(outs, k, index, slot)
                    sems = turn(way, step), k, slot
                    arrived(target, pair_sem(pair_send, *sems), pair_sem(pair_recv, *sems))
    for copy in local:
        copy.wait()
    for copy in pending:
        copy.wait_send()


def gather(arrays, devices):
    count = len(arrays)
    chips = devices // 2
    half = chips // 2
    dma = pltpu.SemaphoreType.DMA
    return pl.pallas_call(
        functools.partial(gather_kernel, chips, count),
        in_specs=[pl.BlockSpec(memory_space=pl.ANY)] * count,
        out_specs=[pl.BlockSpec(memory_space=pl.ANY)] * count,
        out_shape=[jax.ShapeDtypeStruct((devices,) + a.shape, a.dtype) for a in arrays],
        scratch_shapes=[
            dma((4 * half * count,)), dma((4 * half * count,)),
            dma((2 * half * count,)), dma((2 * half * count,)),
            dma(((2 * half + 1) * count * 3,)), dma(((2 * half + 1) * count * 3,)),
            dma((count,)),
        ],
        compiler_params=pltpu.CompilerParams(collective_id=0, has_side_effects=True),
        name="gather_weights",
    )(*arrays)


def small_rows(size):
    return 16 * (-(-size // (16 * LANES)))


def flat_pack(parts, rows):
    flat = jnp.concatenate([p.reshape(-1) for p in parts])
    return jnp.pad(flat, (0, rows * LANES - flat.shape[0])).reshape(rows, LANES)


def local(devices, tokens, segments, norm_gain, w_in, conv_weight, conv_bias, dt_bias, a_log, d_skip, gate_gain, w_out, cotangent):
    seqs, length, width = tokens.shape
    rows = seqs * length
    proj_width = w_in.shape[1]
    inner = devices * w_out.shape[0]
    taps = conv_weight.shape[0]
    heads = dt_bias.shape[0]
    share_n, share_c, share_g = norm_gain.shape[0], conv_bias.shape[0], gate_gain.shape[0]
    conv_width = devices * share_c
    state = (conv_width - inner) // 2

    size = share_n + share_g + (taps + 1) * share_c
    pack = flat_pack([norm_gain, gate_gain, conv_weight, conv_bias], small_rows(size))
    win_all, wout_all, pack_all = gather(
        [w_in.reshape(PIECES, -1, proj_width), w_out.reshape(PIECES, -1, width), pack], devices)
    w_in_full = win_all.reshape(width, proj_width)
    w_out_full = wout_all.reshape(inner, width)
    pack_all = pack_all.reshape(devices, -1)
    cuts = [share_n, share_n + share_g, share_n + share_g + taps * share_c, size]
    gain_full = pack_all[:, : cuts[0]].reshape(width)
    gate_full = pack_all[:, cuts[0] : cuts[1]].reshape(inner)
    kernel_full = pack_all[:, cuts[1] : cuts[2]].reshape(devices, taps, share_c).transpose(1, 0, 2).reshape(taps, conv_width)
    shift_full = pack_all[:, cuts[2] : cuts[3]].reshape(conv_width)

    residual = tokens.reshape(rows, width).astype(f32)
    rstd = lax.rsqrt(jnp.mean(residual * residual, axis=-1, keepdims=True) + epsilon)
    unit = residual * rstd
    gain_f = gain_full.astype(f32)
    normed = (unit * gain_f).astype(bf16)
    grad_rows = cotangent.reshape(rows, width)
    projected = dot(normed, w_in_full)
    gm = dot(grad_rows, w_out_full, NT)
    tables = mixer_tables(segments, kernel_full, shift_full, dt_bias, a_log, d_skip, gate_full)
    mixed, gz, gy, rs, gg = mixer_forward(projected, gm, *tables, heads, state)
    block_out = (residual + dot(mixed, w_out_full)).astype(bf16)
    grad_w_out = lax.dot_general(mixed, grad_rows, (((0,), (0,)), ((), ())), preferred_element_type=f32).astype(bf16)
    px, pr, gp, gbc, gh = mixer_backward(projected, gy, rs, *tables, heads, state)
    proj_back = jnp.concatenate([gz, px, pr[:, : 2 * state + heads]], axis=1)
    grad_normed = dot(proj_back, w_in_full, NT)
    grad_w_in = lax.dot_general(normed, proj_back, (((0,), (0,)), ((), ())), preferred_element_type=f32).astype(bf16)
    grad_norm = jnp.sum(grad_normed * unit, axis=0)
    grad_unit = grad_normed * gain_f
    grad_tokens = grad_rows.astype(f32) + rstd * (grad_unit - unit * jnp.mean(grad_unit * unit, axis=-1, keepdims=True))

    gp, gbc, gh = gp.sum(0), gbc.sum(0), gh.sum(0)
    grad_kernel = jnp.concatenate([gp[:taps], gbc[:taps]], axis=1)
    grad_shift = jnp.concatenate([gp[taps], gbc[taps]])
    grad_gate = gg[:, 0].sum(0)
    grad_skip = gp[taps + 1].reshape(heads, inner // heads).sum(1)

    small = jnp.concatenate([
        grad_norm.reshape(devices, share_n), grad_gate.reshape(devices, share_g),
        grad_kernel.reshape(taps, devices, share_c).transpose(1, 0, 2).reshape(devices, taps * share_c),
        grad_shift.reshape(devices, share_c)], axis=1)
    small = lax.psum_scatter(small, "fsdp", scatter_dimension=0, tiled=True)
    small = lax.psum(small, "dp")[0]
    head_grads = lax.psum(jnp.stack([gh[0, :heads], gh[1, :heads], grad_skip]), ("fsdp", "dp"))

    def owned(full):
        mine = lax.psum_scatter(full, "fsdp", scatter_dimension=0, tiled=True)
        other = lax.ppermute(mine, "dp", [(0, 1), (1, 0)])
        return mine.astype(f32) + other.astype(f32)

    return (
        block_out.reshape(seqs, length, width),
        grad_tokens.reshape(seqs, length, width),
        small[: cuts[0]],
        owned(grad_w_in),
        small[cuts[1] : cuts[2]].reshape(taps, share_c),
        small[cuts[2] : cuts[3]],
        head_grads[0],
        head_grads[1],
        head_grads[2],
        small[cuts[0] : cuts[1]],
        owned(grad_w_out),
    )


def solution(mesh):
    rows3, rows2 = P(("fsdp", "dp"), None, None), P(("fsdp", "dp"), None)
    return jax.shard_map(
        functools.partial(local, mesh.shape["fsdp"]),
        mesh=mesh,
        in_specs=(rows3, rows2, P("fsdp"), P("fsdp", None), P(None, "fsdp"), P("fsdp"), P(), P(), P(), P("fsdp"), P("fsdp", None), rows3),
        out_specs=(rows3, rows3, P("fsdp"), P("fsdp", None), P(None, "fsdp"), P("fsdp"), P(), P(), P(), P("fsdp"), P("fsdp", None)),
        check_vma=False,
    )
```

time: 1200 us -> 641 us (0.53)
  matrix products: 303 us -> 78.6 us
  Pallas kernels: 0 us -> 193 us
  blocking collectives: 188 us -> 46.7 us
  other arithmetic: 148 us -> 9.97 us
  waiting for transfers between devices: 405 us -> 278 us
  local copies, waits for them, and re-layouts: 128 us -> 15.4 us
    dot_general x36 -> x6, matrix products: 303 us -> 78.6 us  [the longest x4 54.2 us: dot(): lax.dot_general(a, b, dims, precision=precision, preferred_element_type=f32)]
    pallas_call x0 -> x3, Pallas kernels: none -> 193 us  [the longest x1 121 us: gather(): pl.pallas_call(functools.partial(gather_kernel, chips, count), in_specs=[...]
    reduce_scatter x2, waiting for transfers between devices: 368 us -> 190 us  [owned(): mine = lax.psum_scatter(full, 'fsdp', scatter_dimension=0, tiled=True)]
    unnamed x2 -> x0, blocking collectives: 126 us -> none
    unnamed x7 -> x4, waiting for transfers between devices: 1.44 us -> 88 us
    reduce_sum x16 -> x5, other arithmetic: 63.2 us -> 0.17 us  [the longest x1 0.11 us: local(): grad_skip = gp[taps + 1].reshape(heads, inner // heads).sum(1)]
    mul x12 -> x0, other arithmetic: 36.8 us -> none  [the longest x1 19 us: mixer(): activated = jax.nn.silu(summed)]
    reshape x36 -> x8, local copies, waits for them, and re-layouts: 32 us -> 2.58 us  [the longest x1 0.87 us: flat_pack(): flat = jnp.concatenate([p.reshape(-1) for p in parts])]
  transfers between devices with their start and end apart: 6 -> 5, of which waited for: 3 -> 2; matrix products, arithmetic and copies ran while one was open for 46% -> 9% of each run, Pallas kernels for 0% -> 6%
where the time goes in v1:
time: 641 us; the launch traced here: 640 us
  waiting for transfers between devices  278 us (43%)
  Pallas kernels  193 us (30%)
  matrix products  78.6 us (12%)
  blocking collectives  46.7 us (7%)
  local copies, waits for them, and re-layouts  15.4 us (2%)
  between operations  14.2 us (2%)
  other arithmetic  9.97 us (2%)
    reduce_scatter x2, waiting for transfers between devices, owned(): mine = lax.psum_scatter(full, 'fsdp', scatter_dimension=0, tiled=True)  190 us
    pallas_call x1, Pallas kernels, gather(): pl.pallas_call(functools.partial(gather_kernel, chips, count), in_specs=[...  121 us
    unnamed x4, waiting for transfers between devices  88 us
    dot_general x4, matrix products, dot(): lax.dot_general(a, b, dims, precision=precision, preferred_element_type=f32)  54.2 us
    psum x1, blocking collectives, local(): lax.psum(jnp.stack([gh[0, :heads], gh[1, :heads], grad_skip]), ('fsdp', '...  41.8 us
    pallas_call x1, Pallas kernels, mixer_forward(): pl.pallas_call(kernel, grid=(seqs, 2, groups), in_specs=[pl.BlockSpec((le...  36.9 us
    pallas_call x1, Pallas kernels, mixer_backward(): pl.pallas_call(kernel, grid=(seqs, groups), in_specs=[pl.BlockSpec((lengt...  35.2 us
    dot_general x1, matrix products, local(): lax.dot_general(normed, proj_back, (((0,), (0,)), ((), ())), preferred_el...  17 us
  transfers between devices with their start and end apart: 5, of which 2 were waited for; matrix products, arithmetic and copies ran while one was open for 9% of the time, Pallas kernels for 6%

profile of v1, /device:TPU:0, one launch (start us, length us, event | category | flops | bytes accessed | tf_op | source)
XLA Modules:
  0.0 640.1 jit_solution(1891133241558745680)
XLA Ops:
  7.3 0.9 reshape.159
  8.1 2.1 concatenate.24
  10.8 121.3 %gather_weights.1 = (bf16[16,3,32,6448]{3,2,1,0:T(8,128)(2,1)}, bf16[16,3,64,1536]{3,2,1,0:T(8,128)(2,1)}, bf16[16,16,128]{2,1,0:T(8,128)(2,1)}) custom-call(bf16[3,32,6448]{2,1,0:T(8,128)(2,1)} %bitcast.74, bf16[3,64,1536]{2,1,0:T(8,128)(2,1)} %bitcast.75, bf16[16,128]{1,0:T(8,128)(2,1)} %pad_bitcast_fusion.refs_2_), custom_call_target="tpu_custom_call" | custom-call | tf_op jit(solution)/shard_map/gather_weights/pallas_call | solution.py:595
  134.0 0.9 fusion.2
  137.0 18.0 %fusion.9.z_ref.x_ref.bc_ref.dtr_ref = f32[512,6448]{1,0:T(8,128)} fusion(bf16[512,1536]{1,0:T(8,128)(2,1)S(1)} %bitcast.73, bf16[1536,6448]{1,0:T(8,128)(2,1)} %bitcast.91), kind=kOutput, calls=%fused_computation.60 | convolution fusion | flops 10141827072 | bytes 34586624 | tf_op jit(solution)/shard_map/dot_general | solution.py:22
  155.2 7.0 %convolution_bitcast_fusion.gm_ref = f32[512,3072]{1,0:T(8,128)} fusion(bf16[3072,1536]{1,0:T(8,128)(2,1)S(1)} %bitcast.96, bf16[512,1536]{1,0:T(8,128)(2,1)S(1)} %bitcast.71), kind=kOutput, calls=%fused_computation.3 | convolution fusion | flops 4831838208 | bytes 17301504 | tf_op jit(solution)/shard_map/dot_general | solution.py:22
  162.5 36.9 %mixer_forward.1 = (bf16[512,3072]{1,0:T(8,128)(2,1)S(1)}, bf16[512,3072]{1,0:T(8,128)(2,1)}, f32[512,3072]{1,0:T(8,128)}, f32[2,256,128]{2,1,0:T(8,128)S(1)}, f32[2,8,3072]{2,1,0:T(8,128)S(1)}) custom-call(f32[512,6448]{1,0:T(8,128)} %fusion.9.z_ref.x_ref.bc_ref.dtr_ref, f32[512,6448]{1,0:T(8,128)} %fusion.9.z_ref.x_ref.bc_ref.dtr_ref, ...), custom_call_target="tpu_custom_call" | custom-call | flops 10000000000 | bytes 45000000 | tf_op jit(solution)/shard_map/mixer_forward/pallas_call | solution.py:326
  199.4 1.7 copy-done
  201.1 7.4 %convolution_convert_fusion.1 = bf16[3072,1536]{1,0:T(8,128)(2,1)} fusion(bf16[512,3072]{1,0:T(8,128)(2,1)S(1)} %get-tuple-element.27, bf16[512,1536]{1,0:T(8,128)(2,1)S(1)} %bitcast.72), kind=kOutput, calls=%fused_computation.1 | convolution fusion | flops 4836556800 | bytes 14155776 | tf_op jit(solution)/shard_map/dot_general | solution.py:655
  208.6 35.2 %mixer_backward.1 = (bf16[512,3072]{1,0:T(8,128)(2,1)S(1)}, bf16[512,384]{1,0:T(8,128)(2,1)S(1)}, f32[2,8,3072]{2,1,0:T(8,128)S(1)}, f32[2,8,256]{2,1,0:T(8,128)S(1)}, f32[2,8,128]{2,1,0:T(8,128)S(1)}) custom-call(f32[512,6448]{1,0:T(8,128)} %fusion.9.z_ref.x_ref.bc_ref.dtr_ref, f32[512,6448]{1,0:T(8,128)} %fusion.9.z_ref.x_ref.bc_ref.dtr_ref, ...), custom_call_target="tpu_custom_call" | custom-call | flops 10000000000 | bytes 30000000 | tf_op jit(solution)/shard_map/mixer_backward/pallas_call | solution.py:376
  243.8 1.6 copy-done.1
  245.4 18.8 %multiply_reduce_fusion = (f32[1536]{0:T(1024)S(1)}, f32[512]{0:T(512)S(1)}, bf16[512,1536]{1,0:T(8,128)(2,1)}, f32[512,1536]{1,0:T(8,128)}) fusion(bf16[2,256,1536]{2,1,0:T(8,128)(2,1)S(1)} %copy-done.2, f32[512]{0:T(512)S(1)} %bitcast.84, f32[1536]{0:T(1024)S(1)} %reshape.174, bf16[1536,6448]{1,0:T(8,128)(2,1)} %bitcast.92, ...), kind=kOutput, calls=%fused_computation.7 | convolution fusion | flops 10168711168 | bytes 32718848 | tf_op jit(solution)/shard_map/dot_general | solution.py:22
  264.2 17.0 %convolution_convert_fusion = bf16[1536,6448]{1,0:T(8,128)(2,1)} fusion(bf16[512,1536]{1,0:T(8,128)(2,1)} %get-tuple-element.39, bf16[512,304]{1,0:T(8,128)(2,1)S(1)} %bitcast.68, bf16[512,3072]{1,0:T(8,128)(2,1)} %copy-done.1, bf16[512,3072]{1,0:T(8,128)(2,1)} %get-tuple-element.28), kind=kOutput, calls=%fused_computation | convolution fusion | flops 10171539456 | bytes 27983872 | tf_op jit(solution)/shard_map/dot_general | solution.py:659
  283.0 41.8 %psum.15 = f32[3,48]{1,0:T(4,128)S(1)} all-reduce(f32[3,48]{1,0:T(4,128)S(1)} %pad_maximum_fusion.7), channel_id=1, replica_groups=mesh['fsdp'=16,'dp'=2] {'fsdp','dp'}, use_global_device_ids=true, to_apply=%region_11.12 | all-reduce | flops 144 | bytes 1152 | tf_op jit(solution)/shard_map/psum | solution.py:676
  324.8 10.4 %fusion = bf16[512,1536]{1,0:T(8,128)(2,1)} fusion(bf16[512,3072]{1,0:T(8,128)(2,1)} %copy-done, bf16[3072,1536]{1,0:T(8,128)(2,1)} %bitcast.93, bf16[512,1536]{1,0:T(8,128)(2,1)S(1)} %bitcast.69), kind=kOutput, calls=%fused_computation.12 | convolution fusion | flops 4834197504 | bytes 15728640 | tf_op jit(solution)/shard_map/dot_general | solution.py:22
  335.2 2.8 multiply_add_fusion
  338.0 2.3 collective-permute-start.1
  340.3 189.8 %reduce-scatter.3.cloned.1.call-done = bf16[96,6448]{1,0:T(8,128)(2,1)} async-done(((bf16[1536,6448]{1,0:T(8,128)(2,1)}), bf16[96,6448]{1,0:T(8,128)(2,1)}) %reduce-scatter.3.cloned.1.call-update) | async-done | bytes 1238032 | tf_op jit(solution)/shard_map/reduce_scatter | solution.py:679
  530.1 1.5 collective-permute-start
  532.7 88.0 %all-reduce.9.cloned.1.call-done = f32[16,1328]{1,0:T(8,128)} async-done(((f32[16,1328]{1,0:T(8,128)}), f32[16,1328]{1,0:T(8,128)}) %all-reduce.9.cloned.1.call-update) | async-done | bytes 85008
  620.7 1.4 constant_dynamic-slice_fusion
  622.1 5.0 psum.14
  629.6 2.3 convert_add_fusion.1
  631.9 1.7 convert_add_fusion
  (98 shorter events, 10.2 us)
Async XLA Ops:
  7.2 128.4 %copy-start.2 = (bf16[2,256,1536]{2,1,0:T(8,128)(2,1)S(1)}, bf16[2,256,1536]{2,1,0:T(8,128)(2,1)}, u32[]{:S(2)}) copy-start(bf16[2,256,1536]{2,1,0:T(8,128)(2,1)} %param.12) | copy-start | bytes 4718596
  7.2 129.2 %copy-start.7 = (f32[48]{0:T(128)S(1)}, f32[48]{0:T(128)}, u32[]{:S(2)}) copy-start(f32[48]{0:T(128)} %param.20) | copy-start | bytes 580
  7.2 330.8 %reduce-scatter.5.cloned.1.call-start = ((), (), s32[]{:S(2)}) async-start(), calls=%async_computation.3 | async-start | bytes 10027008 | tf_op jit(solution)/shard_map/reduce_scatter | solution.py:679
  136.6 18.6 %slice-start = ((s8[9437184]{0:T(1024)(128)(4,1)}), s8[4194304]{0:T(1024)(128)(4,1)S(1)}, s32[]{:S(2)}) async-start(s8[9437184]{0:T(1024)(128)(4,1)} %bitcast.94), calls=%async_computation.5 | async-start | bytes 8388608
  137.0 18.1 %copy-start.4 = (bf16[2,256,1536]{2,1,0:T(8,128)(2,1)S(1)}, bf16[2,256,1536]{2,1,0:T(8,128)(2,1)}, u32[]{:S(2)}) copy-start(bf16[2,256,1536]{2,1,0:T(8,128)(2,1)} %param.23) | copy-start | bytes 4718596
  137.0 18.1 %slice-start.1 = ((s8[9437184]{0:T(1024)(128)(4,1)}), s8[4194304]{0:T(1024)(128)(4,1)S(1)}, s32[]{:S(2)}) async-start(s8[9437184]{0:T(1024)(128)(4,1)} %bitcast.94), calls=%async_computation.6 | async-start | bytes 8388608
  137.0 18.1 %slice-start.2 = ((s8[9437184]{0:T(1024)(128)(4,1)}), s8[1048576]{0:T(1024)(128)(4,1)S(1)}, s32[]{:S(2)}) async-start(s8[9437184]{0:T(1024)(128)(4,1)} %bitcast.94), calls=%async_computation.7 | async-start | bytes 2097152
  155.2 7.0 %copy-start.8 = (f32[48]{0:T(128)S(1)}, f32[48]{0:T(128)}, u32[]{:S(2)}) copy-start(f32[48]{0:T(128)} %param.19) | copy-start | bytes 580
  155.2 7.0 %copy-start.9 = (f32[48]{0:T(128)S(1)}, f32[48]{0:T(128)}, u32[]{:S(2)}) copy-start(f32[48]{0:T(128)} %param.18) | copy-start | bytes 580
  199.4 1.7 copy-start
  208.5 321.6 %reduce-scatter.3.cloned.1.call-start = ((), (), s32[]{:S(2)}) async-start(), calls=%async_computation.2 | async-start | bytes 21307392 | tf_op jit(solution)/shard_map/reduce_scatter | solution.py:679
  243.8 1.6 copy-start.1
  281.3 339.4 %all-reduce.9.cloned.1.call-start = ((), (), s32[]{:S(2)}) async-start(), calls=%async_computation.4 | async-start | bytes 180224
  324.8 10.4 %copy-start.3 = (f32[512,1536]{1,0:T(8,128)S(1)}, f32[512,1536]{1,0:T(8,128)}, u32[]{:S(2)}) copy-start(f32[512,1536]{1,0:T(8,128)} %get-tuple-element.52) | copy-start | bytes 9437188
  324.8 10.4 %copy-start.5 = (bf16[2,256,1536]{2,1,0:T(8,128)(2,1)S(1)}, bf16[2,256,1536]{2,1,0:T(8,128)(2,1)}, u32[]{:S(2)}) copy-start(bf16[2,256,1536]{2,1,0:T(8,128)(2,1)} %param.23) | copy-start | bytes 4718596
  335.2 197.0 %copy-start.10 = (u32[32]{0:T(128)S(1)}, u32[32]{0:T(128)}, u32[]{:S(2)}) copy-start(u32[32]{0:T(128)} %constant.36) | copy-start | bytes 388
  338.0 291.6 %collective-permute-start.1 = (bf16[192,1536]{1,0:T(8,128)(2,1)}, bf16[192,1536]{1,0:T(8,128)(2,1)S(1)}, u32[]{:S(2)}, u32[]{:S(2)}) collective-permute-start(bf16[192,1536]{1,0:T(8,128)(2,1)} %reduce-scatter.5.cloned.1.call-done), channel_id=1, source_target_pairs={{0,1},{1,0},{2,3},{3,2},{4,5},{5,4},{6,7},{7,6},{8,9},{9,8},{10,11... | collective-permute-start | bytes 1769480 | tf_op jit(solution)/shard_map/ppermute | solution.py:680
  530.1 101.8 %copy-start.6 = (bf16[96,6448]{1,0:T(8,128)(2,1)S(1)}, bf16[96,6448]{1,0:T(8,128)(2,1)}, u32[]{:S(2)}) copy-start(bf16[96,6448]{1,0:T(8,128)(2,1)} %reduce-scatter.3.cloned.1.call-done) | copy-start | bytes 3714052
  530.1 101.8 %collective-permute-start = (bf16[96,6448]{1,0:T(8,128)(2,1)}, bf16[96,6448]{1,0:T(8,128)(2,1)S(1)}, u32[]{:S(2)}, u32[]{:S(2)}) collective-permute-start(bf16[96,6448]{1,0:T(8,128)(2,1)} %reduce-scatter.3.cloned.1.call-done), channel_id=1, source_target_pairs={{0,1},{1,0},{2,3},{3,2},{4,5},{5,4},{6,7},{7,6},{8,9},{9,8},{10,11... | collective-permute-start | bytes 3714056 | tf_op jit(solution)/shard_map/ppermute | solution.py:680
Sparse Core Ops, SparseCore 0:
  208.7 111.9 reduce-scatter.4
  324.9 205.1 reduce-scatter.2
  534.2 86.4 all-reduce.8

commit v2 on v1

--- a/solution.py
+++ b/solution.py
@@ -608,6 +608,287 @@
     )(*arrays)
 
 
+QUARTERS = 4
+TILE = 512
+
+
+def reduce_kernel(chips, items, rounds, *refs):
+    count = len(items)
+    parts, small_in = refs[:count], refs[count]
+    outs, small_out = refs[count + 1 : 2 * count + 1], refs[2 * count + 1]
+    scratch = refs[2 * count + 2 :]
+    held, ring_in, ring_out, peer_in, last_out, last_in = (scratch[i * count : (i + 1) * count] for i in range(6))
+    (small_recv, small_sent, held_sem, ring_send, ring_recv, peer_send, peer_recv, last_send, last_recv, small_send, small_sem) = scratch[6 * count :]
+    me = lax.axis_index("fsdp")
+    plane = lax.axis_index("dp")
+    chip, core = me // 2, me % 2
+    place = ring_place(chip, chips)
+    ways = (
+        {"fsdp": 2 * ring_chip(place + 1, chips) + core},
+        {"fsdp": 2 * ring_chip(place + chips - 1, chips) + core},
+    )
+    peer = {"dp": 1 - plane}
+    turns = [{"fsdp": me + bit - 2 * bit * ((me // bit) % 2)} for bit in [1 << k for k in range(rounds - 1)]] + [peer]
+    half = chips // 2
+
+    barrier = pltpu.get_barrier_semaphore()
+    greet = list(ways) + turns
+    for other in greet:
+        pl.semaphore_signal(barrier, inc=1, device_id=other, device_id_type=MESH)
+    pl.semaphore_wait(barrier, len(greet))
+
+    pending = []
+
+    def send(source, target, send_sem, recv_sem, device):
+        copy = pltpu.make_async_remote_copy(
+            src_ref=source, dst_ref=target, send_sem=send_sem, recv_sem=recv_sem, device_id=device, device_id_type=MESH)
+        copy.start()
+        pending.append(copy)
+
+    def arrived(target, send_sem, recv_sem):
+        pltpu.make_async_remote_copy(
+            src_ref=target, dst_ref=target, send_sem=send_sem, recv_sem=recv_sem, device_id=peer, device_id_type=MESH).wait_recv()
+
+    def hops(k, way, slot):
+        return half - (slot + (k if slot == 2 else 0) + way) % 2
+
+    def target(k, way, slot, step):
+        ahead = hops(k, way, slot) - step + 1
+        return ring_chip(place + (ahead if way == 0 else chips - ahead), chips)
+
+    def quarter(slot):
+        return slot if slot < 2 else 2 + plane
+
+    def ring_at(way, step, slot):
+        return (way * half + step - 1) * 3 + slot
+
+    def sems(k, way, step, slot):
+        at = k * 6 * half + ring_at(way, step, slot)
+        return ring_send.at[at], ring_recv.at[at]
+
+    def add_up(k, sources, store, width):
+        tile = min(TILE, width)
+        def one(i, carry):
+            cols = pl.ds(pl.multiple_of(i * tile, LANES), tile)
+            total = sources[0][:, cols].astype(f32)
+            for source in sources[1:]:
+                total = total + source[:, cols].astype(f32)
+            store[:, cols] = total.astype(store.dtype)
+            return carry
+        lax.fori_loop(0, width // tile, one, 0)
+        rest = width % tile
+        if rest:
+            cols = slice(width - rest, width)
+            total = sources[0][:, cols].astype(f32)
+            for source in sources[1:]:
+                total = total + source[:, cols].astype(f32)
+            store[:, cols] = total.astype(store.dtype)
+
+    for slot in (0, 1):
+        for k in range(count):
+            for way in range(2):
+                send(parts[k].at[target(k, way, slot, 1), slot], ring_in[k].at[ring_at(way, 1, slot)], *sems(k, way, 1, slot), ways[way])
+    order = []
+    for ahead in range(half, -1, -1):
+        order.append((place + ahead) % chips)
+        if 0 < ahead < half:
+            order.append((place + chips - ahead) % chips)
+    for where in order:
+        chunk = ring_chip(where, chips)
+        for k in range(count):
+            send(parts[k].at[chunk, 3 - plane], peer_in[k].at[where], peer_send.at[k * chips + where], peer_recv.at[k * chips + where], peer)
+    loads = []
+    for k in range(count):
+        for slot in range(3):
+            copy = pltpu.make_async_copy(parts[k].at[:, quarter(slot)], held[k].at[slot], held_sem.at[k * 3 + slot])
+            copy.start()
+            loads.append(copy)
+
+    def small_round(turn):
+        value = small_in if turn == 0 else small_sent.at[turn - 1]
+        send(value, small_recv.at[turn], small_send.at[turn], small_sem.at[turn], turns[turn])
+
+    def small_finish(turn):
+        value = small_in if turn == 0 else small_sent.at[turn - 1]
+        arrived(small_recv.at[turn], small_send.at[turn], small_sem.at[turn])
+        store = small_out if turn == rounds - 1 else small_sent.at[turn]
+        store[...] = value[...] + small_recv[turn]
+
+    small_round(0)
+    for copy in loads:
+        copy.wait()
+
+    def from_peer(k, chunk):
+        where = ring_place(chunk, chips)
+        arrived(peer_in[k].at[where], peer_send.at[k * chips + where], peer_recv.at[k * chips + where])
+        return peer_in[k].at[where]
+
+    awaited = [set() for _ in range(count)]
+    done = 0
+    for step in range(1, half + 1):
+        for slot in (0, 1, 2):
+            for k in range(count):
+                for way in range(2):
+                    if step > hops(k, way, slot) or (step == 1 and slot < 2):
+                        continue
+                    chunk = target(k, way, slot, step)
+                    sources = [held[k].at[slot, chunk]]
+                    if step > 1:
+                        before = ring_at(way, step - 1, slot)
+                        arrived(ring_in[k].at[before], *sems(k, way, step - 1, slot))
+                        sources.append(ring_in[k].at[before])
+                    if slot == 2:
+                        sources.append(from_peer(k, chunk))
+                    at = ring_at(way, step, slot)
+                    add_up(k, sources, ring_out[k].at[at], items[k][1])
+                    send(ring_out[k].at[at], ring_in[k].at[at], *sems(k, way, step, slot), ways[way])
+        for _ in range(-(-rounds // half) if step < half else rounds):
+            if done < rounds - 1:
+                small_finish(done)
+                done += 1
+                small_round(done)
+    for slot in (0, 1, 2):
+        for k in range(count):
+            sources = [held[k].at[slot, chip]]
+            for way in range(2):
+                last = hops(k, way, slot)
+                at = ring_at(way, last, slot)
+                arrived(ring_in[k].at[at], *sems(k, way, last, slot))
+                sources.append(ring_in[k].at[at])
+            if slot == 2:
+                sources.append(from_peer(k, chip))
+            add_up(k, sources, last_out[k].at[slot], items[k][1])
+            send(last_out[k].at[slot], last_in[k].at[slot], last_send.at[k * 3 + slot], last_recv.at[k * 3 + slot], peer)
+    while done < rounds:
+        small_finish(done)
+        done += 1
+        if done < rounds:
+            small_round(done)
+    for slot in (0, 1, 2):
+        for k in range(count):
+            arrived(last_in[k].at[slot], last_send.at[k * 3 + slot], last_recv.at[k * 3 + slot])
+            width = items[k][1]
+            if slot < 2:
+                add_up(k, [last_out[k].at[slot], last_in[k].at[slot]], outs[k].at[slot], width)
+            else:
+                add_up(k, [last_out[k].at[slot]], outs[k].at[2 + plane], width)
+                add_up(k, [last_in[k].at[slot]], outs[k].at[3 - plane], width)
+    for copy in pending:
+        copy.wait_send()
+
+
+def reduce_scatter(arrays, small, devices):
+    count = len(arrays)
+    chips = devices // 2
+    half = chips // 2
+    rounds = devices.bit_length()
+    items = tuple(a.shape[2:] for a in arrays)
+    dma = pltpu.SemaphoreType.DMA
+    vm = lambda lead, dtype=bf16: [pltpu.VMEM(lead + item, dtype) for item in items]
+    return pl.pallas_call(
+        functools.partial(reduce_kernel, chips, items, rounds),
+        in_specs=[pl.BlockSpec(memory_space=pl.ANY)] * count + [pl.BlockSpec(memory_space=pltpu.VMEM)],
+        out_specs=[pl.BlockSpec(memory_space=pltpu.VMEM)] * (count + 1),
+        out_shape=[jax.ShapeDtypeStruct((4,) + item, f32) for item in items] + [jax.ShapeDtypeStruct(small.shape, f32)],
+        scratch_shapes=vm((3, chips)) + vm((6 * half,)) + vm((6 * half,)) + vm((chips,)) + vm((3,)) + vm((3,)) + [
+            pltpu.VMEM((rounds,) + small.shape, f32), pltpu.VMEM((rounds,) + small.shape, f32),
+            dma((3 * count,)),
+            dma((6 * half * count,)), dma((6 * half * count,)),
+            dma((chips * count,)), dma((chips * count,)),
+            dma((3 * count,)), dma((3 * count,)),
+            dma((rounds,)), dma((rounds,)),
+        ],
+        compiler_params=pltpu.CompilerParams(collective_id=1, has_side_effects=True, vmem_limit_bytes=62 << 20),
+        name="reduce_gradients",
+    )(*arrays, small)
+
+
+def parts_kernel(a_ref, a2_ref, b_ref, b2_ref, o_ref):
+    o_ref[...] = (dot(a_ref[...], b_ref[...]) + dot(a2_ref[...], b2_ref[...])).astype(bf16)
+
+
+def grad_parts(left, left2, right, right2, name):
+    rows, tokens = left.shape
+    width = right.shape[1]
+    tile = min(GROUP, width)
+    return pl.pallas_call(
+        parts_kernel,
+        grid=(width // tile,),
+        in_specs=[
+            pl.BlockSpec((rows, tokens), lambda i: (0, 0)),
+            pl.BlockSpec((rows, tokens), lambda i: (0, 0)),
+            pl.BlockSpec((tokens, tile), lambda i: (0, i)),
+            pl.BlockSpec((tokens, tile), lambda i: (0, i)),
+        ],
+        out_specs=pl.BlockSpec((rows, tile), lambda i: (0, i)),
+        out_shape=jax.ShapeDtypeStruct((rows, width), bf16),
+        compiler_params=pltpu.CompilerParams(vmem_limit_bytes=32 << 20),
+        cost_estimate=pl.CostEstimate(flops=4 * rows * tokens * width, bytes_accessed=2 * (2 * rows * tokens + 2 * tokens * width + rows * width), transcendentals=0),
+        name=name,
+    )(left, left2, right, right2)
+
+
+def input_kernel(groups, used, gz_ref, px_ref, pr_ref, w_ref, tok_ref, cot_ref, gain_ref, gt_ref, gn_ref, acc):
+    step = pl.program_id(0)
+
+    @pl.when(step == 0)
+    def _():
+        acc[...] = jnp.zeros_like(acc)
+
+    @pl.when(step < groups)
+    def _():
+        acc[...] += dot(gz_ref[...], w_ref[...], NT)
+
+    @pl.when((step >= groups) & (step < 2 * groups))
+    def _():
+        acc[...] += dot(px_ref[...], w_ref[...], NT)
+
+    @pl.when(step == 2 * groups)
+    def _():
+        size = pr_ref.shape[1]
+        col = lax.broadcasted_iota(jnp.int32, (w_ref.shape[0], size), 1)
+        tail = jnp.where(col < used, w_ref[:, :size].astype(f32), 0.0).astype(bf16)
+        acc[...] += dot(pr_ref[...], tail, NT)
+        rows, width = acc.shape
+        chunk = BLOCK
+        total = jnp.zeros((1, width), f32)
+        for i in range(rows // chunk):
+            sl = slice(i * chunk, (i + 1) * chunk)
+            u = tok_ref[sl].astype(f32)
+            rstd = lax.rsqrt(jnp.mean(u * u, axis=1, keepdims=True) + epsilon)
+            unit = u * rstd
+            gn = acc[sl]
+            total = total + jnp.sum(gn * unit, axis=0, keepdims=True)
+            gu = gn * gain_ref[0:1, :]
+            inward = jnp.mean(gu * unit, axis=1, keepdims=True)
+            gt_ref[sl] = cot_ref[sl].astype(f32) + rstd * (gu - unit * inward)
+        gn_ref[...] = jnp.broadcast_to(total, gn_ref.shape)
+
+
+def grad_input(gz, px, pr, w_in_full, tokens, cot, gain, used):
+    rows, width = tokens.shape
+    groups = gz.shape[1] // GROUP
+    return pl.pallas_call(
+        functools.partial(input_kernel, groups, used),
+        grid=(2 * groups + 1,),
+        in_specs=[
+            pl.BlockSpec((rows, GROUP), lambda i: (0, jnp.minimum(i, groups - 1))),
+            pl.BlockSpec((rows, GROUP), lambda i: (0, jnp.clip(i - groups, 0, groups - 1))),
+            pl.BlockSpec((rows, pr.shape[1]), lambda i: (0, 0)),
+            pl.BlockSpec((width, GROUP), lambda i: (0, i)),
+            pl.BlockSpec((rows, width), lambda i: (0, 0)),
+            pl.BlockSpec((rows, width), lambda i: (0, 0)),
+            pl.BlockSpec((8, width), lambda i: (0, 0)),
+        ],
+        out_specs=[pl.BlockSpec((rows, width), lambda i: (0, 0)), pl.BlockSpec((8, width), lambda i: (0, 0))],
+        out_shape=[jax.ShapeDtypeStruct((rows, width), f32), jax.ShapeDtypeStruct((8, width), f32)],
+        scratch_shapes=[pltpu.VMEM((rows, width), f32)],
+        compiler_params=pltpu.CompilerParams(vmem_limit_bytes=48 << 20),
+        cost_estimate=pl.CostEstimate(flops=2 * rows * width * w_in_full.shape[1], bytes_accessed=32 * 10**6, transcendentals=0),
+        name="grad_input",
+    )(gz, px, pr, w_in_full, tokens, cot, gain)
+
+
 def small_rows(size):
     return 16 * (-(-size // (16 * LANES)))
 
@@ -627,6 +908,11 @@
     share_n, share_c, share_g = norm_gain.shape[0], conv_bias.shape[0], gate_gain.shape[0]
     conv_width = devices * share_c
     state = (conv_width - inner) // 2
+    chips = devices // 2
+    me = lax.axis_index("fsdp")
+    core = me % 2
+    swap = [(i, i + 1 - 2 * (i % 2)) for i in range(devices)]
+    partner = lambda value: lax.ppermute(value, "fsdp", swap)
 
     size = share_n + share_g + (taps + 1) * share_c
     pack = flat_pack([norm_gain, gate_gain, conv_weight, conv_bias], small_rows(size))
@@ -641,57 +927,69 @@
     kernel_full = pack_all[:, cuts[1] : cuts[2]].reshape(devices, taps, share_c).transpose(1, 0, 2).reshape(taps, conv_width)
     shift_full = pack_all[:, cuts[2] : cuts[3]].reshape(conv_width)
 
-    residual = tokens.reshape(rows, width).astype(f32)
+    flat_tokens = tokens.reshape(rows, width)
+    residual = flat_tokens.astype(f32)
     rstd = lax.rsqrt(jnp.mean(residual * residual, axis=-1, keepdims=True) + epsilon)
-    unit = residual * rstd
     gain_f = gain_full.astype(f32)
-    normed = (unit * gain_f).astype(bf16)
+    normed = (residual * rstd * gain_f).astype(bf16)
     grad_rows = cotangent.reshape(rows, width)
+    grad_rows2 = partner(grad_rows)
+
+    def split_rows(value):
+        turned = value.T.reshape(chips, 2, -1, rows)
+        mine = lax.dynamic_index_in_dim(turned, core, 1, keepdims=False)
+        theirs = lax.dynamic_index_in_dim(turned, 1 - core, 1, keepdims=False)
+        return mine.reshape(-1, rows), partner(theirs).reshape(-1, rows)
+
     projected = dot(normed, w_in_full)
     gm = dot(grad_rows, w_out_full, NT)
+    normed_t, normed_t2 = split_rows(normed)
     tables = mixer_tables(segments, kernel_full, shift_full, dt_bias, a_log, d_skip, gate_full)
     mixed, gz, gy, rs, gg = mixer_forward(projected, gm, *tables, heads, state)
+    gz2 = partner(gz)
+    mixed_t, mixed_t2 = split_rows(mixed)
     block_out = (residual + dot(mixed, w_out_full)).astype(bf16)
-    grad_w_out = lax.dot_general(mixed, grad_rows, (((0,), (0,)), ((), ())), preferred_element_type=f32).astype(bf16)
     px, pr, gp, gbc, gh = mixer_backward(projected, gy, rs, *tables, heads, state)
-    proj_back = jnp.concatenate([gz, px, pr[:, : 2 * state + heads]], axis=1)
-    grad_normed = dot(proj_back, w_in_full, NT)
-    grad_w_in = lax.dot_general(normed, proj_back, (((0,), (0,)), ((), ())), preferred_element_type=f32).astype(bf16)
-    grad_norm = jnp.sum(grad_normed * unit, axis=0)
-    grad_unit = grad_normed * gain_f
-    grad_tokens = grad_rows.astype(f32) + rstd * (grad_unit - unit * jnp.mean(grad_unit * unit, axis=-1, keepdims=True))
+    px2, pr2 = partner(px), partner(pr)
+    part_out = grad_parts(mixed_t, mixed_t2, grad_rows, grad_rows2, "grad_out")
+    part_z = grad_parts(normed_t, normed_t2, gz, gz2, "grad_z")
+    gain8 = jnp.broadcast_to(gain_f[None], (8, width))
+    grad_tokens, grad_norm = grad_input(gz, px, pr, w_in_full, flat_tokens, grad_rows, gain8, 2 * state + heads)
+    part_x = grad_parts(normed_t, normed_t2, px, px2, "grad_x")
+    part_r = grad_parts(normed_t, normed_t2, pr, pr2, "grad_r")
 
     gp, gbc, gh = gp.sum(0), gbc.sum(0), gh.sum(0)
     grad_kernel = jnp.concatenate([gp[:taps], gbc[:taps]], axis=1)
     grad_shift = jnp.concatenate([gp[taps], gbc[taps]])
     grad_gate = gg[:, 0].sum(0)
     grad_skip = gp[taps + 1].reshape(heads, inner // heads).sum(1)
-
     small = jnp.concatenate([
-        grad_norm.reshape(devices, share_n), grad_gate.reshape(devices, share_g),
+        grad_norm[0].reshape(devices, share_n), grad_gate.reshape(devices, share_g),
         grad_kernel.reshape(taps, devices, share_c).transpose(1, 0, 2).reshape(devices, taps * share_c),
         grad_shift.reshape(devices, share_c)], axis=1)
-    small = lax.psum_scatter(small, "fsdp", scatter_dimension=0, tiled=True)
-    small = lax.psum(small, "dp")[0]
-    head_grads = lax.psum(jnp.stack([gh[0, :heads], gh[1, :heads], grad_skip]), ("fsdp", "dp"))
-
-    def owned(full):
-        mine = lax.psum_scatter(full, "fsdp", scatter_dimension=0, tiled=True)
-        other = lax.ppermute(mine, "dp", [(0, 1), (1, 0)])
-        return mine.astype(f32) + other.astype(f32)
-
+    each = -(-size // LANES)
+    small = jnp.pad(small, ((0, 0), (0, each * LANES - size))).reshape(devices * each, LANES)
+    head = pad_lanes(jnp.stack([gh[0, :heads], gh[1, :heads], grad_skip]))
+    small = jnp.concatenate([head, small])
+    small = jnp.pad(small, ((0, -small.shape[0] % 8), (0, 0)))
+
+    quarters = lambda part: part.reshape(chips, QUARTERS, -1, part.shape[1])
+    own_out, own_z, own_x, own_r, small = reduce_scatter([quarters(p) for p in (part_out, part_z, part_x, part_r)], small, devices)
+    grad_w_in = jnp.concatenate([o.reshape(-1, o.shape[2]) for o in (own_z, own_x, own_r)], axis=1)[:, :proj_width]
+    head_grads = small[:3, :heads]
+    mine = lax.dynamic_slice(small, (3 + me * each, 0), (each, LANES)).reshape(-1)
     return (
         block_out.reshape(seqs, length, width),
         grad_tokens.reshape(seqs, length, width),
-        small[: cuts[0]],
-        owned(grad_w_in),
-        small[cuts[1] : cuts[2]].reshape(taps, share_c),
-        small[cuts[2] : cuts[3]],
+        mine[: cuts[0]],
+        grad_w_in,
+        mine[cuts[1] : cuts[2]].reshape(taps, share_c),
+        mine[cuts[2] : cuts[3]],
         head_grads[0],
         head_grads[1],
         head_grads[2],
-        small[cuts[0] : cuts[1]],
-        owned(grad_w_out),
+        mine[cuts[0] : cuts[1]],
+        own_out.reshape(-1, width),
     )
 
 

time: 641 us -> 501 us (0.78)
  waiting for transfers between devices: 278 us -> 0.02 us
  Pallas kernels: 193 us -> 380 us
  blocking collectives: 46.7 us -> 0 us
  local copies, waits for them, and re-layouts: 15.4 us -> 57.7 us
  matrix products: 78.6 us -> 38.2 us
  between operations: 14.2 us -> 1.05 us
  other arithmetic: 9.97 us -> 18.3 us
    reduce_scatter x2 -> x0, waiting for transfers between devices: 190 us -> none  [owned(): mine = lax.psum_scatter(full, 'fsdp', scatter_dimension=0, tiled=True)]
    pallas_call x0 -> x6, Pallas kernels: none -> 186 us  [the longest x1 140 us: reduce_scatter(): pl.pallas_call(functools.partial(reduce_kernel, chips, items, rounds), in...]
    unnamed x4 -> x0, waiting for transfers between devices: 88 us -> none
    psum x2 -> x0, blocking collectives: 46.7 us -> none  [the longest x1 41.8 us: local(): lax.psum(jnp.stack([gh[0, :heads], gh[1, :heads], grad_skip]), ('fsdp', '...]
    dot_general x2 -> x0, matrix products: 24.4 us -> none  [the longest x1 17 us: local(): lax.dot_general(normed, proj_back, (((0,), (0,)), ((), ())), preferred_el...]
    dot_general x4 -> x3, matrix products: 54.2 us -> 38.2 us  [dot(): lax.dot_general(a, b, dims, precision=precision, preferred_element_type=f32)]
    unnamed x32 -> x61, local copies, waits for them, and re-layouts: 6.24 us -> 14.3 us
    transpose x0 -> x2, local copies, waits for them, and re-layouts: none -> 7.25 us  [split_rows(): turned = value.T.reshape(chips, 2, -1, rows)]
  transfers between devices with their start and end apart: 5 -> 6, of which waited for: 2 -> 0; matrix products, arithmetic and copies ran while one was open for 9% -> 19% of each run, Pallas kernels for 6% -> 47%
where the time goes in v2:
time: 501 us; the launch traced here: 498 us
  Pallas kernels  380 us (76%)
  local copies, waits for them, and re-layouts  57.7 us (12%)
  matrix products  38.2 us (8%)
  other arithmetic  18.3 us (4%)
    pallas_call x1, Pallas kernels, reduce_scatter(): pl.pallas_call(functools.partial(reduce_kernel, chips, items, rounds), in...  140 us
    pallas_call x1, Pallas kernels, gather(): pl.pallas_call(functools.partial(gather_kernel, chips, count), in_specs=[...  122 us
    dot_general x3, matrix products, dot(): lax.dot_general(a, b, dims, precision=precision, preferred_element_type=f32)  38.2 us
    pallas_call x1, Pallas kernels, mixer_forward(): pl.pallas_call(kernel, grid=(seqs, 2, groups), in_specs=[pl.BlockSpec((le...  36.9 us
    pallas_call x1, Pallas kernels, mixer_backward(): pl.pallas_call(kernel, grid=(seqs, groups), in_specs=[pl.BlockSpec((lengt...  35.5 us
    pallas_call x4, Pallas kernels, grad_parts(): pl.pallas_call(parts_kernel, grid=(width // tile,), in_specs=[pl.BlockSpe...  25 us
    pallas_call x1, Pallas kernels, grad_input(): pl.pallas_call(functools.partial(input_kernel, groups, used), grid=(2 * g...  21.4 us
    unnamed x61, local copies, waits for them, and re-layouts  14.3 us
  transfers between devices with their start and end apart: 6, of which 0 were waited for; matrix products, arithmetic and copies ran while one was open for 19% of the time, Pallas kernels for 47%

profile of v2, /device:TPU:0, one launch (start us, length us, event | category | flops | bytes accessed | tf_op | source)
XLA Modules:
  0.0 497.8 jit_solution(15835509359508445763)
XLA Ops:
  2.1 2.1 concatenate.27
  4.8 121.9 %gather_weights.1 = (bf16[16,3,32,6448]{3,2,1,0:T(8,128)(2,1)}, bf16[16,3,64,1536]{3,2,1,0:T(8,128)(2,1)}, bf16[16,16,128]{2,1,0:T(8,128)(2,1)}) custom-call(bf16[3,32,6448]{2,1,0:T(8,128)(2,1)} %bitcast.91, bf16[3,64,1536]{2,1,0:T(8,128)(2,1)} %bitcast.95, bf16[16,128]{1,0:T(8,128)(2,1)} %pad_bitcast_fusion.refs_2_), custom_call_target="tpu_custom_call" | custom-call | tf_op jit(solution)/shard_map/gather_weights/pallas_call | solution.py:595
  136.0 10.8 %convolution_bitcast_fusion.gm_ref = f32[512,3072]{1,0:T(8,128)} fusion(bf16[3072,1536]{1,0:T(8,128)(2,1)} %bitcast.111, bf16[512,1536]{1,0:T(8,128)(2,1)S(1)} %bitcast.85), kind=kOutput, calls=%fused_computation | convolution fusion | flops 4831838208 | bytes 17301504 | tf_op jit(solution)/shard_map/dot_general | solution.py:22
  147.6 17.7 %fusion.12.z_ref.x_ref.bc_ref.dtr_ref = f32[512,6448]{1,0:T(8,128)} fusion(bf16[512,1536]{1,0:T(8,128)(2,1)S(1)} %bitcast.90, bf16[1536,6448]{1,0:T(8,128)(2,1)} %bitcast.109), kind=kOutput, calls=%fused_computation.61 | convolution fusion | flops 10141827072 | bytes 34586624 | tf_op jit(solution)/shard_map/dot_general | solution.py:22
  165.7 36.9 %mixer_forward.1 = (bf16[512,3072]{1,0:T(8,128)(2,1)S(1)}, bf16[512,3072]{1,0:T(8,128)(2,1)}, f32[512,3072]{1,0:T(8,128)}, f32[2,256,128]{2,1,0:T(8,128)S(1)}, f32[2,8,3072]{2,1,0:T(8,128)S(1)}) custom-call(f32[512,6448]{1,0:T(8,128)} %fusion.12.z_ref.x_ref.bc_ref.dtr_ref, f32[512,6448]{1,0:T(8,128)} %fusion.12.z_ref.x_ref.bc_ref.dtr_ref, ...), custom_call_target="tpu_custom_call" | custom-call | flops 10000000000 | bytes 45000000 | tf_op jit(solution)/shard_map/mixer_forward/pallas_call | solution.py:326
  202.6 1.7 copy-done.4
  205.0 35.5 %mixer_backward.1 = (bf16[512,3072]{1,0:T(8,128)(2,1)}, bf16[512,384]{1,0:T(8,128)(2,1)S(1)}, f32[2,8,3072]{2,1,0:T(8,128)S(1)}, f32[2,8,256]{2,1,0:T(8,128)S(1)}, f32[2,8,128]{2,1,0:T(8,128)S(1)}) custom-call(f32[512,6448]{1,0:T(8,128)} %fusion.12.z_ref.x_ref.bc_ref.dtr_ref, f32[512,6448]{1,0:T(8,128)} %fusion.12.z_ref.x_ref.bc_ref.dtr_ref, ...), custom_call_target="tpu_custom_call" | custom-call | flops 10000000000 | bytes 30000000 | tf_op jit(solution)/shard_map/mixer_backward/pallas_call | solution.py:376
  242.7 4.6 copy.96
  247.4 3.3 dynamic-slice_bitcast_fusion
  250.7 1.6 reduce_sum.56
  252.3 2.2 slice_reduce_fusion.1
  257.9 21.4 %grad_input.1 = (f32[512,1536]{1,0:T(8,128)}, f32[8,1536]{1,0:T(8,128)S(1)}) custom-call(bf16[512,3072]{1,0:T(8,128)(2,1)} %get-tuple-element.35.gz_ref.b_ref, bf16[512,3072]{1,0:T(8,128)(2,1)} %get-tuple-element.38.px_ref.b_ref, bf16[512,384]{1,0:T(8,128)(2,1)S(1)} %get-tuple-element.39.pr_ref.b_ref, bf16[1536,6448]{1,0:T(8,128)(2,1)} %bitcast.110, ...), custom_call_target="tpu_custom_call" | custom-call | flops 10141827072 | bytes 32000000 | tf_op jit(solution)/shard_map/grad_input/pallas_call | solution.py:871
  300.4 2.6 copy.97
  303.1 1.7 select_maximum_fusion.3.refs_4_
  306.9 9.8 %fusion.5 = bf16[512,1536]{1,0:T(8,128)(2,1)} fusion(bf16[512,3072]{1,0:T(8,128)(2,1)S(1)} %copy-done.5, bf16[3072,1536]{1,0:T(8,128)(2,1)} %bitcast.112, bf16[512,1536]{1,0:T(8,128)(2,1)S(1)} %bitcast.71), kind=kOutput, calls=%fused_computation.10 | convolution fusion | flops 4834197504 | bytes 15728640 | tf_op jit(solution)/shard_map/dot_general | solution.py:22
  316.7 2.0 grad_r.1
  319.5 7.4 %grad_out.1 = bf16[1536,1536]{1,0:T(8,128)(2,1)S(1)} custom-call(bf16[1536,512]{1,0:T(8,128)(2,1)S(1)} %bitcast.80, bf16[1536,512]{1,0:T(8,128)(2,1)} %bitcast.21.a2_ref, bf16[512,1536]{1,0:T(8,128)(2,1)S(1)} %bitcast.87, bf16[512,1536]{1,0:T(8,128)(2,1)} %collective-permute-done.1.b2_ref), custom_call_target="tpu_custom_call" | custom-call | flops 4831838208 | bytes 11010048 | tf_op jit(solution)/shard_map/grad_out/pallas_call | solution.py:814
  326.9 2.1 copy-done.1
  329.0 7.8 %grad_x.1 = bf16[768,3072]{1,0:T(8,128)(2,1)S(1)} custom-call(bf16[768,512]{1,0:T(8,128)(2,1)S(1)} %bitcast.77, bf16[768,512]{1,0:T(8,128)(2,1)S(1)} %bitcast.82, bf16[512,3072]{1,0:T(8,128)(2,1)} %get-tuple-element.38.px_ref.b_ref, bf16[512,3072]{1,0:T(8,128)(2,1)} %collective-permute-done.4.b2_ref), custom_call_target="tpu_custom_call" | custom-call | flops 4831838208 | bytes 12582912 | tf_op jit(solution)/shard_map/grad_x/pallas_call | solution.py:814
  336.8 2.2 copy-done.2
  339.0 7.8 %grad_z.1 = bf16[768,3072]{1,0:T(8,128)(2,1)S(1)} custom-call(bf16[768,512]{1,0:T(8,128)(2,1)S(1)} %bitcast.78, bf16[768,512]{1,0:T(8,128)(2,1)S(1)} %bitcast.83, bf16[512,3072]{1,0:T(8,128)(2,1)} %get-tuple-element.35.gz_ref.b_ref, bf16[512,3072]{1,0:T(8,128)(2,1)} %collective-permute-done.3.b2_ref), custom_call_target="tpu_custom_call" | custom-call | flops 4831838208 | bytes 12582912 | tf_op jit(solution)/shard_map/grad_z/pallas_call | solution.py:814
  346.8 2.2 copy-done.3
  349.0 139.8 %reduce_gradients.1 = (f32[4,48,1536]{2,1,0:T(8,128)}, f32[4,24,3072]{2,1,0:T(8,128)}, f32[4,24,3072]{2,1,0:T(8,128)}, f32[4,24,384]{2,1,0:T(8,128)}, f32[184,128]{1,0:T(8,128)}) custom-call(bf16[8,4,48,1536]{3,2,1,0:T(8,128)(2,1)} %bitcast.72, bf16[8,4,24,3072]{3,2,1,0:T(8,128)(2,1)} %bitcast.74, bf16[8,4,24,3072]{3,2,1,0:T(8,128)(2,1)} %bitcast.73, ...), custom_call_target="tpu_custom_call" | custom-call | tf_op jit(solution)/shard_map/reduce_gradients/pallas_call | solution.py:788
  493.5 3.3 pad_maximum_fusion
  (136 shorter events, 48.5 us)
Async XLA Ops:
  0.6 135.4 %copy-start.11 = (bf16[2,256,1536]{2,1,0:T(8,128)(2,1)S(1)}, bf16[2,256,1536]{2,1,0:T(8,128)(2,1)}, u32[]{:S(2)}) copy-start(bf16[2,256,1536]{2,1,0:T(8,128)(2,1)} %param.23) | copy-start | bytes 4718596
  0.7 132.7 %copy-start = (bf16[2,256,1536]{2,1,0:T(8,128)(2,1)S(1)}, bf16[2,256,1536]{2,1,0:T(8,128)(2,1)}, u32[]{:S(2)}) copy-start(bf16[2,256,1536]{2,1,0:T(8,128)(2,1)} %param.12) | copy-start | bytes 4718596
  0.7 318.8 %collective-permute-start.1 = (bf16[512,1536]{1,0:T(8,128)(2,1)}, bf16[512,1536]{1,0:T(8,128)(2,1)}, u32[]{:S(2)}, u32[]{:S(2)}) collective-permute-start(bf16[512,1536]{1,0:T(8,128)(2,1)} %bitcast.84), channel_id=1, source_target_pairs={{0,2},{2,0},{4,6},{6,4},{8,10},{10,8},{12,14},{14,12},{16,18},{18,... | collective-permute-start | bytes 4718600 | tf_op jit(solution)/shard_map/ppermute | solution.py:915
  133.4 13.6 %copy-start.18 = (f32[1536]{0:T(1024)}, f32[1536]{0:T(1024)S(1)}, u32[]{:S(2)}) copy-start(f32[1536]{0:T(1024)S(1)} %reshape.227) | copy-start | bytes 18436
  136.0 10.8 %copy-start.20 = (f32[16,192]{1,0:T(8,128)S(1)}, f32[16,192]{1,0:T(8,128)}, u32[]{:S(2)}) copy-start(f32[16,192]{1,0:T(8,128)} %slice_convert_fusion.1) | copy-start | bytes 36868
  136.0 10.9 %copy-start.26 = (f32[48]{0:T(128)S(1)}, f32[48]{0:T(128)}, u32[]{:S(2)}) copy-start(f32[48]{0:T(128)} %param.20) | copy-start | bytes 580
  147.5 17.7 %copy-start.21 = (f32[3328]{0:T(1024)S(1)}, f32[3328]{0:T(1024)}, u32[]{:S(2)}) copy-start(f32[3328]{0:T(1024)} %reshape.232) | copy-start | bytes 39940
  147.5 17.8 %copy-start.27 = (f32[48]{0:T(128)S(1)}, f32[48]{0:T(128)}, u32[]{:S(2)}) copy-start(f32[48]{0:T(128)} %param.19) | copy-start | bytes 580
  147.5 17.8 %copy-start.28 = (f32[48]{0:T(128)S(1)}, f32[48]{0:T(128)}, u32[]{:S(2)}) copy-start(f32[48]{0:T(128)} %param.18) | copy-start | bytes 580
  147.5 17.8 %copy-start.15 = (f32[2,256,1]{2,1,0:T(8,128)S(1)}, f32[2,256,1]{2,1,0:T(8,128)}, u32[]{:S(2)}) copy-start(f32[2,256,1]{2,1,0:T(8,128)} %copy.86) | copy-start | bytes 6148
  147.5 17.8 %copy-start.16 = (f32[2,256,1]{2,1,0:T(8,128)S(1)}, f32[2,256,1]{2,1,0:T(8,128)}, u32[]{:S(2)}) copy-start(f32[2,256,1]{2,1,0:T(8,128)} %copy.87) | copy-start | bytes 6148
  147.5 17.8 %copy-start.17 = (f32[2,256,1]{2,1,0:T(8,128)S(1)}, f32[2,256,1]{2,1,0:T(8,128)}, u32[]{:S(2)}) copy-start(f32[2,256,1]{2,1,0:T(8,128)} %copy.84) | copy-start | bytes 6148
  241.7 64.6 %collective-permute-start.5 = (bf16[512,384]{1,0:T(8,128)(2,1)S(1)}, bf16[512,384]{1,0:T(8,128)(2,1)}, u32[]{:S(2)}, u32[]{:S(2)}) collective-permute-start(bf16[512,384]{1,0:T(8,128)(2,1)S(1)} %get-tuple-element.39.pr_ref.b_ref), channel_id=1, source_target_pairs={{0,2},{2,0},{4,6},{6,4},{8,10},{10,8},{12,14},{14,12},{16,18},{18,... | collective-permute-start | bytes 1179656 | tf_op jit(solution)/shard_map/ppermute | solution.py:915
  242.2 86.8 %collective-permute-start.4 = (bf16[512,3072]{1,0:T(8,128)(2,1)}, bf16[512,3072]{1,0:T(8,128)(2,1)}, u32[]{:S(2)}, u32[]{:S(2)}) collective-permute-start(bf16[512,3072]{1,0:T(8,128)(2,1)} %get-tuple-element.38.px_ref.b_ref), channel_id=1, source_target_pairs={{0,2},{2,0},{4,6},{6,4},{8,10},{10,8},{12,14},{14,12},{16,18},{18,... | collective-permute-start | bytes 9437192 | tf_op jit(solution)/shard_map/ppermute | solution.py:915
  242.2 96.8 %collective-permute-start.3 = (bf16[512,3072]{1,0:T(8,128)(2,1)}, bf16[512,3072]{1,0:T(8,128)(2,1)}, u32[]{:S(2)}, u32[]{:S(2)}) collective-permute-start(bf16[512,3072]{1,0:T(8,128)(2,1)} %get-tuple-element.35.gz_ref.b_ref), channel_id=1, source_target_pairs={{0,2},{2,0},{4,6},{6,4},{8,10},{10,8},{12,14},{14,12},{16,18},{18,... | collective-permute-start | bytes 9437192 | tf_op jit(solution)/shard_map/ppermute | solution.py:915
  250.7 68.8 %collective-permute-start = (bf16[8,192,512]{2,1,0:T(8,128)(2,1)}, bf16[8,192,512]{2,1,0:T(8,128)(2,1)}, u32[]{:S(2)}, u32[]{:S(2)}) collective-permute-start(bf16[8,192,512]{2,1,0:T(8,128)(2,1)} %get-tuple-element.51), channel_id=1, source_target_pairs={{0,2},{2,0},{4,6},{6,4},{8,10},{10,8},{12,14},{14,12},{16,18},{18,... | collective-permute-start | bytes 4718600 | tf_op jit(solution)/shard_map/ppermute | solution.py:915
  257.9 23.0 %copy-start.23 = (f32[1,2,2,128]{3,2,1,0:T(2,128)S(1)}, f32[1,2,2,128]{3,2,1,0:T(2,128)}, u32[]{:S(2)}) copy-start(f32[1,2,2,128]{3,2,1,0:T(2,128)} %get-tuple-element.60) | copy-start | bytes 6148
  257.9 23.0 %copy-start.19 = (f32[1536]{0:T(1024)S(1)}, f32[1536]{0:T(1024)}, u32[]{:S(2)}) copy-start(f32[1536]{0:T(1024)} %copy-done.18) | copy-start | bytes 18436
  279.3 7.2 %copy-start.9 = (f32[2,8,128]{2,1,0:T(8,128)S(1)}, f32[2,8,128]{2,1,0:T(8,128)}, u32[]{:S(2)}) copy-start(f32[2,8,128]{2,1,0:T(8,128)} %copy-done.8) | copy-start | bytes 24580
  297.3 5.7 %copy-start.24 = (f32[2,48]{1,0:T(2,128)S(1)}, f32[2,48]{1,0:T(2,128)}, u32[]{:S(2)}) copy-start(f32[2,48]{1,0:T(2,128)} %slice.82) | copy-start | bytes 1156
  297.3 5.7 %copy-start.25 = (f32[48]{0:T(128)S(1)}, f32[48]{0:T(128)}, u32[]{:S(2)}) copy-start(f32[48]{0:T(128)} %reduce_sum.57) | copy-start | bytes 580
  306.3 13.2 %copy-start.13 = (bf16[2,256,1536]{2,1,0:T(8,128)(2,1)S(1)}, bf16[2,256,1536]{2,1,0:T(8,128)(2,1)}, u32[]{:S(2)}) copy-start(bf16[2,256,1536]{2,1,0:T(8,128)(2,1)} %param.23) | copy-start | bytes 4718596
  306.3 10.4 %collective-permute-start.2 = (bf16[8,96,512]{2,1,0:T(8,128)(2,1)S(1)}, bf16[8,96,512]{2,1,0:T(8,128)(2,1)S(1)}, u32[]{:S(2)}, u32[]{:S(2)}) collective-permute-start(bf16[8,96,512]{2,1,0:T(8,128)(2,1)S(1)} %get-tuple-element.53), channel_id=1, source_target_pairs={{0,2},{2,0},{4,6},{6,4},{8,10},{10,8},{12,14},{14,12},{16,18},{18,... | collective-permute-start | bytes 2359304 | tf_op jit(solution)/shard_map/ppermute | solution.py:915
  488.8 8.0 %copy-start.14 = (f32[4,48,1536]{2,1,0:T(8,128)S(1)}, f32[4,48,1536]{2,1,0:T(8,128)}, u32[]{:S(2)}) copy-start(f32[4,48,1536]{2,1,0:T(8,128)} %get-tuple-element.50) | copy-start | bytes 3538948
  (13 other events, 26.4 us)

commit v3 on v1

--- a/solution.py
+++ b/solution.py
@@ -53,11 +53,13 @@
     return gx, grads
 
 
-def prologue(heads, bc_ref, dtr_ref, segc_ref, segr_ref, cwbc_ref, hp_ref, mask_s, b_s, c_s, dt_s, cum_s, cumt_s, ef_s, la_s, sp_s):
+def prologue(heads, bc_ref, dtr_ref, segr_ref, cwbc_ref, hp_ref, mask_s, b_s, c_s, dt_s, cum_s, cumt_s, ef_s, la_s, sp_s):
     length = bc_ref.shape[0]
-    segc = segc_ref[0]
-    for j in range(3):
-        mask_s[2 - j] = jnp.broadcast_to(segc[:, j + 1 : j + 2], (length, LANES))
+    segc = segr_ref[0].T
+    here = lax.broadcasted_iota(jnp.int32, segc.shape, 0)
+    for shift in (1, 2, 3):
+        alike = (pltpu.roll(segc, shift, 0) == segc) & (here >= shift)
+        mask_s[3 - shift] = jnp.broadcast_to(jnp.where(alike, 1.0, 0.0)[:, 0:1], (length, LANES))
     masks = [mask_s[k] for k in range(3)]
     for half, ref in ((0, b_s), (1, c_s)):
         sl = slice(half * LANES, (half + 1) * LANES)
@@ -98,8 +100,8 @@
     return dot(jnp.concatenate([hi, lo], axis=1), pick)
 
 
-def fwd_kernel(heads, z_ref, x_ref, bc_ref, dtr_ref, gm_ref, segc_ref, segr_ref, cwx_ref, cwbc_ref, hp_ref, cp_ref,
-               mixed_ref, gz_ref, gy_ref, rs_ref, gg_ref,
+def fwd_kernel(heads, z_ref, x_ref, bc_ref, dtr_ref, gm_ref, segr_ref, cwx_ref, cwbc_ref, hp_ref, cp_ref,
+               mixed_ref, mixt_ref, gz_ref, gy_ref, rs_ref, gg_ref,
                mask_s, b_s, c_s, dt_s, cum_s, cumt_s, ef_s, la_s, sp_s, sm_s, ssm_s, yd_s, u_s, st_s, rs_s):
     phase, group = pl.program_id(1), pl.program_id(2)
     length = z_ref.shape[0]
@@ -109,7 +111,7 @@
 
     @pl.when((phase == 0) & (group == 0))
     def _():
-        row, col, same = prologue(heads, bc_ref, dtr_ref, segc_ref, segr_ref, cwbc_ref, hp_ref, mask_s, b_s, c_s, dt_s, cum_s, cumt_s, ef_s, la_s, sp_s)
+        row, col, same = prologue(heads, bc_ref, dtr_ref, segr_ref, cwbc_ref, hp_ref, mask_s, b_s, c_s, dt_s, cum_s, cumt_s, ef_s, la_s, sp_s)
         scores = dot(c_s[...], b_s[...], NT, precision=highest)
         sm_s[...] = jnp.where(row >= col, scores * same, 0.0)
         st_s[...] = jnp.zeros_like(st_s)
@@ -183,8 +185,12 @@
             unit = gated * scale
             gain = cp_ref[1:2, sl]
             gm = gm_ref[:, sl]
-            mixed_ref[:, sl] = (unit * gain).astype(bf16)
-            gg_ref[0, :, sl] = jnp.broadcast_to(jnp.sum(gm * unit, axis=0, keepdims=True), (8, LANES))
+            mixed = unit * gain
+            mixed_ref[:, sl] = mixed.astype(bf16)
+            mixt_ref[sl, :] = mixed.T.astype(bf16)
+            gain_sum = jnp.sum(gm * unit, axis=0, keepdims=True)
+            old = gg_ref[0:1, place]
+            gg_ref[:, place] = jnp.broadcast_to(jnp.where(pl.program_id(0) == 0, gain_sum, old + gain_sum), (8, LANES))
             ggated = scale * (gm * gain) - gated * lean
             gz_ref[:, sl] = (ggated * ssm * dsilu).astype(bf16)
             gy = ggated * silu
@@ -198,18 +204,26 @@
         rs_ref[0] = total
 
 
-def bwd_kernel(heads, x_ref, bc_ref, dtr_ref, gy_ref, rs_ref, segc_ref, segr_ref, cwx_ref, cwbc_ref, hp_ref, cp_ref,
-               px_ref, pr_ref, gp_ref, gbc_ref, gh_ref,
+def mixer_back(heads, groups, group, opening, x_ref, bc_ref, dtr_ref, gy_ref, rs_ref, segr_ref, cwx_ref, cwbc_ref, hp_ref, cp_ref,
+               px_ref, pr_ref, sg_ref,
                mask_s, b_s, c_s, dt_s, cum_s, cumt_s, ef_s, la_s, sp_s, smt_s, gst_s, gc_s, gd_s):
-    group = pl.program_id(1)
     length = x_ref.shape[0]
+    inner_width = groups * GROUP
+
+    def keep(row, cols, value):
+        sg_ref[row : row + 1, cols] = sg_ref[row : row + 1, cols] + value
+
+    @pl.when(opening)
+    def _():
+        sg_ref[...] = jnp.zeros_like(sg_ref)
+
     lane = lax.broadcasted_iota(jnp.int32, (length, LANES), 1)
     first = lane < 64
     half = lax.broadcasted_iota(jnp.int32, (BLOCK, LANES), 1) < 64
 
     @pl.when(group == 0)
     def _():
-        row, col, same = prologue(heads, bc_ref, dtr_ref, segc_ref, segr_ref, cwbc_ref, hp_ref, mask_s, b_s, c_s, dt_s, cum_s, cumt_s, ef_s, la_s, sp_s)
+        row, col, same = prologue(heads, bc_ref, dtr_ref, segr_ref, cwbc_ref, hp_ref, mask_s, b_s, c_s, dt_s, cum_s, cumt_s, ef_s, la_s, sp_s)
         scores = dot(b_s[...], c_s[...], NT, precision=highest)
         smt_s[...] = jnp.where(row <= col, scores * same, 0.0)
         gst_s[...] = jnp.zeros_like(gst_s)
@@ -267,17 +281,17 @@
         gx, grads = conv_back(gsum, xin, cw, masks, length)
         px_ref[:, sl] = gx.astype(bf16)
         grads.append(jnp.sum(gy * xs, axis=0, keepdims=True))
+        place = pl.ds(pl.multiple_of(group * GROUP + j * LANES, LANES), LANES)
         for k, value in enumerate(grads):
-            gp_ref[0, k : k + 1, sl] = value
-        gp_ref[0, 6:8, sl] = jnp.zeros((2, LANES), f32)
+            keep(k, place, value)
     gc_s[...] = gcum
     gd_s[...] = gdir
 
-    @pl.when(group == pl.num_programs(1) - 1)
+    @pl.when(group == groups - 1)
     def _():
         row = lax.broadcasted_iota(jnp.int32, (length, length), 0)
         col = lax.broadcasted_iota(jnp.int32, (length, length), 1)
-        same = segc_ref[0][:, 0:1] == segr_ref[0, 0:1, :]
+        same = segr_ref[0].T[:, 0:1] == segr_ref[0, 0:1, :]
         gscore = jnp.where((row <= col) & same, gst_s[...], 0.0)
         backs = (dot(gscore, c_s[...], precision=highest), dot(gscore.T, b_s[...], precision=highest))
         for part in range(2):
@@ -290,16 +304,15 @@
             gx, grads = conv_back(gsum, xin, cw, masks, length)
             pr_ref[:, sl] = gx.astype(bf16)
             for k, value in enumerate(grads):
-                gbc_ref[0, k : k + 1, sl] = value
-            gbc_ref[0, 5:8, sl] = jnp.zeros((3, LANES), f32)
+                keep(k, slice(inner_width + part * LANES, inner_width + (part + 1) * LANES), value)
         upper = jnp.where(row <= col, 1.0, 0.0).astype(f32)
         gla = dot(upper, gc_s[...] + rs_ref[0], precision=highest)
         graw = (gd_s[...] - gla * jnp.exp(hp_ref[1:2, :])) * sp_s[...]
         graw = jnp.where(lane < heads, graw, 0.0)
         pr_ref[:, 2 * LANES :] = graw.astype(bf16)
-        gh_ref[0, 0:1] = jnp.sum(graw, axis=0, keepdims=True)
-        gh_ref[0, 1:2] = jnp.sum(jnp.where(lane < heads, gla * la_s[...], 0.0), axis=0, keepdims=True)
-        gh_ref[0, 2:8] = jnp.zeros((6, LANES), f32)
+        tail = slice(inner_width + 2 * LANES, inner_width + 3 * LANES)
+        keep(0, tail, jnp.sum(graw, axis=0, keepdims=True))
+        keep(1, tail, jnp.sum(jnp.where(lane < heads, gla * la_s[...], 0.0), axis=0, keepdims=True))
 
 
 def small_scratch(length):
@@ -316,8 +329,8 @@
     ]
 
 
-def mixer_forward(projected, gm, segc, segr, cw, hp, cp, heads, state):
-    seqs, length = segc.shape[:2]
+def mixer_forward(projected, gm, segr, cw, hp, cp, heads, state):
+    seqs, _, length = segr.shape
     inner = gm.shape[1]
     groups = inner // GROUP
     rows = seqs * length
@@ -332,7 +345,6 @@
             pl.BlockSpec((length, 2 * state), lambda b, p, g: (b, 2 * inner // (2 * state))),
             pl.BlockSpec((length, LANES), lambda b, p, g: (b, (2 * inner + 2 * state) // LANES)),
             pl.BlockSpec((length, GROUP), lambda b, p, g: (b, g)),
-            pl.BlockSpec((1, length, LANES), lambda b, p, g: (b, 0, 0)),
             pl.BlockSpec((1, 8, length), lambda b, p, g: (b, 0, 0)),
             pl.BlockSpec((8, GROUP), lambda b, p, g: (0, g)),
             pl.BlockSpec((8, 2 * state), lambda b, p, g: (0, inner // (2 * state))),
@@ -341,17 +353,19 @@
         ],
         out_specs=[
             pl.BlockSpec((length, GROUP), out_row),
+            pl.BlockSpec((GROUP, length), lambda b, p, g: (g * p, b)),
             pl.BlockSpec((length, GROUP), out_row),
             pl.BlockSpec((length, GROUP), out_row),
             pl.BlockSpec((1, length, LANES), lambda b, p, g: (b, 0, 0)),
-            pl.BlockSpec((1, 8, GROUP), lambda b, p, g: (b, 0, g * p)),
+            pl.BlockSpec((8, inner), lambda b, p, g: (0, 0)),
         ],
         out_shape=[
             jax.ShapeDtypeStruct((rows, inner), bf16),
+            jax.ShapeDtypeStruct((inner, rows), bf16),
             jax.ShapeDtypeStruct((rows, inner), bf16),
             jax.ShapeDtypeStruct((rows, inner), f32),
             jax.ShapeDtypeStruct((seqs, length, LANES), f32),
-            jax.ShapeDtypeStruct((seqs, 8, inner), f32),
+            jax.ShapeDtypeStruct((8, inner), f32),
         ],
         scratch_shapes=small_scratch(length) + [
             pltpu.VMEM((length, length), f32),
@@ -364,55 +378,7 @@
         compiler_params=pltpu.CompilerParams(vmem_limit_bytes=48 << 20),
         cost_estimate=pl.CostEstimate(flops=10**10, bytes_accessed=45 * 10**6, transcendentals=10**7),
         name="mixer_forward",
-    )(projected, projected, projected, projected, gm, segc, segr, cw, cw, hp, cp)
-
-
-def mixer_backward(projected, gy, rs, segc, segr, cw, hp, cp, heads, state):
-    seqs, length = segc.shape[:2]
-    inner = gy.shape[1]
-    groups = inner // GROUP
-    rows = seqs * length
-    kernel = functools.partial(bwd_kernel, heads)
-    return pl.pallas_call(
-        kernel,
-        grid=(seqs, groups),
-        in_specs=[
-            pl.BlockSpec((length, GROUP), lambda b, g: (b, groups + g)),
-            pl.BlockSpec((length, 2 * state), lambda b, g: (b, 2 * inner // (2 * state))),
-            pl.BlockSpec((length, LANES), lambda b, g: (b, (2 * inner + 2 * state) // LANES)),
-            pl.BlockSpec((length, GROUP), lambda b, g: (b, g)),
-            pl.BlockSpec((1, length, LANES), lambda b, g: (b, 0, 0)),
-            pl.BlockSpec((1, length, LANES), lambda b, g: (b, 0, 0)),
-            pl.BlockSpec((1, 8, length), lambda b, g: (b, 0, 0)),
-            pl.BlockSpec((8, GROUP), lambda b, g: (0, g)),
-            pl.BlockSpec((8, 2 * state), lambda b, g: (0, inner // (2 * state))),
-            pl.BlockSpec((8, LANES), lambda b, g: (0, 0)),
-            pl.BlockSpec((8, GROUP), lambda b, g: (0, g)),
-        ],
-        out_specs=[
-            pl.BlockSpec((length, GROUP), lambda b, g: (b, g)),
-            pl.BlockSpec((length, 3 * LANES), lambda b, g: (b, 0)),
-            pl.BlockSpec((1, 8, GROUP), lambda b, g: (b, 0, g)),
-            pl.BlockSpec((1, 8, 2 * state), lambda b, g: (b, 0, 0)),
-            pl.BlockSpec((1, 8, LANES), lambda b, g: (b, 0, 0)),
-        ],
-        out_shape=[
-            jax.ShapeDtypeStruct((rows, inner), bf16),
-            jax.ShapeDtypeStruct((rows, 3 * LANES), bf16),
-            jax.ShapeDtypeStruct((seqs, 8, inner), f32),
-            jax.ShapeDtypeStruct((seqs, 8, 2 * state), f32),
-            jax.ShapeDtypeStruct((seqs, 8, LANES), f32),
-        ],
-        scratch_shapes=small_scratch(length) + [
-            pltpu.VMEM((length, length), f32),
-            pltpu.VMEM((length, length), f32),
-            pltpu.VMEM((length, LANES), f32),
-            pltpu.VMEM((length, LANES), f32),
-        ],
-        compiler_params=pltpu.CompilerParams(vmem_limit_bytes=48 << 20),
-        cost_estimate=pl.CostEstimate(flops=10**10, bytes_accessed=30 * 10**6, transcendentals=10**7),
-        name="mixer_backward",
-    )(projected, projected, projected, gy, rs, segc, segr, cw, cw, hp, cp)
+    )(projected, projected, projected, projected, gm, segr, cw, cw, hp, cp)
 
 
 def pad_lanes(v, width=LANES):
@@ -422,19 +388,13 @@
 def mixer_tables(segments, kernel_full, shift_full, dt_bias, a_log, d_skip, gate_full):
     taps = kernel_full.shape[0]
     seqs, length = segments.shape
-    columns = [segments.astype(f32)]
-    where = jnp.arange(length)[None, :]
-    for j in range(1, taps):
-        before = jnp.pad(segments, ((0, 0), (j, 0)))[:, :length]
-        columns.append(((before == segments) & (where >= j)).astype(f32))
-    segc = jnp.pad(jnp.stack(columns, axis=-1), ((0, 0), (0, 0), (0, LANES - taps)))
     segr = jnp.broadcast_to(segments.astype(f32)[:, None, :], (seqs, 8, length))
     cw = jnp.concatenate([kernel_full.astype(f32), jnp.broadcast_to(shift_full.astype(f32)[None], (8 - taps, shift_full.shape[0]))])
     hp = pad_lanes(jnp.concatenate([dt_bias[None], jnp.broadcast_to(a_log[None], (7, a_log.shape[0]))]))
     heads = dt_bias.shape[0]
     size = gate_full.shape[0] // heads
     cp = jnp.concatenate([jnp.repeat(d_skip, size)[None], jnp.broadcast_to(gate_full.astype(f32)[None], (7, gate_full.shape[0]))])
-    return segc, segr, cw, hp, cp
+    return segr, cw, hp, cp
 
 
 MESH = pl.DeviceIdType.MESH
@@ -608,6 +568,535 @@
     )(*arrays)
 
 
+QUARTERS = 4
+TILE = 512
+FULL = 62 << 20
+
+
+def add_up(sources, store, width):
+    tile = min(TILE, width)
+
+    def total(cols):
+        value = sources[0][:, cols].astype(f32)
+        for source in sources[1:]:
+            value = value + source[:, cols].astype(f32)
+        store[:, cols] = value.astype(store.dtype)
+
+    def one(i, carry):
+        total(pl.ds(pl.multiple_of(i * tile, LANES), tile))
+        return carry
+
+    lax.fori_loop(0, width // tile, one, 0)
+    if width % tile:
+        total(slice(width - width % tile, width))
+
+
+class Links:
+    def __init__(self, chips):
+        self.chips, self.half = chips, chips // 2
+        me = lax.axis_index("fsdp")
+        self.plane = lax.axis_index("dp")
+        self.chip, self.core = me // 2, me % 2
+        self.place = ring_place(self.chip, chips)
+        self.ways = tuple(
+            {"fsdp": 2 * ring_chip(self.place + move, chips) + self.core} for move in (1, chips - 1))
+        self.peer = {"dp": 1 - self.plane}
+        self.pair = {"fsdp": me + 1 - 2 * self.core}
+        self.turns = [{"fsdp": me + bit - 2 * bit * ((me // bit) % 2)} for bit in (1 << k for k in range(chips.bit_length()))] + [self.peer]
+        self.sent = []
+
+    def greet(self, others):
+        barrier = pltpu.get_barrier_semaphore()
+        for other in others:
+            pl.semaphore_signal(barrier, inc=1, device_id=other, device_id_type=MESH)
+        pl.semaphore_wait(barrier, len(others))
+
+    def send(self, source, target, send_sem, recv_sem, device):
+        make = lambda: pltpu.make_async_remote_copy(
+            src_ref=source(), dst_ref=target(), send_sem=send_sem(), recv_sem=recv_sem(), device_id=device, device_id_type=MESH)
+        make().start()
+        self.sent.append(make)
+
+    def arrived(self, target, send_sem, recv_sem):
+        pltpu.make_async_remote_copy(
+            src_ref=target, dst_ref=target, send_sem=send_sem, recv_sem=recv_sem, device_id=self.peer, device_id_type=MESH).wait_recv()
+
+    def finish(self):
+        for make in self.sent:
+            make().wait_send()
+
+
+class Ring:
+    def __init__(self, links, items, shift, parts, held, ring_in, ring_out, peer_in, held_sem, ring_send, ring_recv, peer_send, peer_recv):
+        self.links, self.items, self.shift, self.parts = links, items, shift, parts
+        self.held, self.ring_in, self.ring_out, self.peer_in = held, ring_in, ring_out, peer_in
+        self.held_sem, self.ring_send, self.ring_recv = held_sem, ring_send, ring_recv
+        self.peer_send, self.peer_recv = peer_send, peer_recv
+
+    def hops(self, k, way, slot):
+        return self.links.half - (slot + (k + self.shift if slot == 2 else 0) + way) % 2
+
+    def target(self, k, way, slot, step):
+        chips = self.links.chips
+        ahead = self.hops(k, way, slot) - step + 1
+        return ring_chip(self.links.place + (ahead if way == 0 else chips - ahead), chips)
+
+    def quarter(self, slot):
+        return slot if slot < 2 else 2 + self.links.plane
+
+    def at(self, way, step, slot):
+        return (way * self.links.half + step - 1) * 3 + slot
+
+    def sems(self, k, way, step, slot):
+        at = k * 6 * self.links.half + self.at(way, step, slot)
+        return self.ring_send.at[at], self.ring_recv.at[at]
+
+    def push(self, k, way, step, slot, source):
+        at = self.at(way, step, slot)
+        self.links.send(
+            source, lambda: self.ring_in[k].at[at],
+            lambda: self.sems(k, way, step, slot)[0], lambda: self.sems(k, way, step, slot)[1], self.links.ways[way])
+
+    def start(self):
+        links, count = self.links, len(self.items)
+        for slot in (0, 1):
+            for k in range(count):
+                for way in range(2):
+                    self.push(k, way, 1, slot, lambda k=k, way=way, slot=slot: self.parts[k].at[self.target(k, way, slot, 1), slot])
+        for move in self.order():
+            for k in range(count):
+                def where(move=move):
+                    return (links.place + move) % links.chips
+                links.send(
+                    lambda k=k, where=where: self.parts[k].at[ring_chip(where(), links.chips), 3 - links.plane],
+                    lambda k=k, where=where: self.peer_in[k].at[where()],
+                    lambda k=k, where=where: self.peer_send.at[k * links.chips + where()],
+                    lambda k=k, where=where: self.peer_recv.at[k * links.chips + where()], links.peer)
+        for copy in self.loads():
+            copy.start()
+
+    def order(self):
+        chips, half = self.links.chips, self.links.half
+        moves = []
+        for ahead in range(half, -1, -1):
+            moves.append(ahead)
+            if 0 < ahead < half:
+                moves.append(chips - ahead)
+        return moves
+
+    def loads(self):
+        return [
+            pltpu.make_async_copy(self.parts[k].at[:, self.quarter(slot)], self.held[k].at[slot], self.held_sem.at[k * 3 + slot])
+            for k in range(len(self.items)) for slot in range(3)]
+
+    def from_peer(self, k, chunk):
+        where = ring_place(chunk, self.links.chips)
+        at = k * self.links.chips + where
+        self.links.arrived(self.peer_in[k].at[where], self.peer_send.at[at], self.peer_recv.at[at])
+        return self.peer_in[k].at[where]
+
+    def hop(self, step, slot):
+        for k in range(len(self.items)):
+            for way in range(2):
+                if step > self.hops(k, way, slot) or (step == 1 and slot < 2):
+                    continue
+                chunk = self.target(k, way, slot, step)
+                sources = [self.held[k].at[slot, chunk]]
+                if step > 1:
+                    before = self.at(way, step - 1, slot)
+                    self.links.arrived(self.ring_in[k].at[before], *self.sems(k, way, step - 1, slot))
+                    sources.append(self.ring_in[k].at[before])
+                if slot == 2:
+                    sources.append(self.from_peer(k, chunk))
+                at = self.at(way, step, slot)
+                add_up(sources, self.ring_out[k].at[at], self.items[k][1])
+                self.push(k, way, step, slot, lambda k=k, at=at: self.ring_out[k].at[at])
+
+    def land(self, k, slot, store):
+        links = self.links
+        sources = [self.held[k].at[slot, links.chip]]
+        for way in range(2):
+            last = self.hops(k, way, slot)
+            at = self.at(way, last, slot)
+            links.arrived(self.ring_in[k].at[at], *self.sems(k, way, last, slot))
+            sources.append(self.ring_in[k].at[at])
+        if slot == 2:
+            sources.append(self.from_peer(k, links.chip))
+        add_up(sources, store, self.items[k][1])
+
+
+def ring_scratch(items, chips):
+    dma = pltpu.SemaphoreType.DMA
+    half, count = chips // 2, len(items)
+    vm = lambda *lead: [pltpu.VMEM(lead + item, bf16) for item in items]
+    return vm(3, chips) + vm(6 * half) + vm(6 * half) + vm(chips) + [
+        dma((3 * count,)), dma((6 * half * count,)), dma((6 * half * count,)), dma((chips * count,)), dma((chips * count,))]
+
+
+def split_scratch(refs, count):
+    return [refs[i * count : (i + 1) * count] for i in range(4)], refs[4 * count : 4 * count + 5]
+
+
+def middle_kernel(heads, chips, seqs, groups, items, x_ref, bc_ref, dtr_ref, gy_ref, rs_ref, segr_ref, cwx_ref, cwbc_ref, hp_ref, cp_ref,
+                  gg_ref, mixed_ref, wout_ref, tok_ref, gz_ref, win_ref, *refs):
+    count = len(items)
+    parts, refs = refs[:count], refs[count:]
+    px_ref, pr_ref, px2_ref, pr2_ref, sg_ref, bo_ref, gn_ref = refs[:7]
+    owns, refs = refs[7 : 7 + count], refs[7 + count :]
+    back, (acc, pxs, prs, px_send, px_recv, pr_send, pr_recv), refs = refs[:13], refs[13:20], refs[20:]
+    (held, ring_in, ring_out, peer_in), sems = split_scratch(refs, count)
+    step = pl.program_id(0)
+    turns = seqs * groups
+    last = turns + 2 * groups - 1
+    length = x_ref.shape[0]
+    links = Links(chips)
+    ring = Ring(links, items, 0, parts, held, ring_in, ring_out, peer_in, *sems)
+
+    @pl.when(step == 0)
+    def _():
+        links.greet([links.ways[0], links.ways[1], links.peer, links.pair])
+        ring.start()
+
+    plan = {}
+    for q in range(2, 3 * links.half):
+        plan.setdefault(min(last, max(3, (24 // (links.half * 2)) * (q - 1))), []).append((q // 3 + 1, q % 3))
+
+    def px_copy(turn):
+        rows = pl.ds(pl.multiple_of(turn // groups * length, length), length)
+        cols = pl.ds(pl.multiple_of(turn % groups * GROUP, GROUP), GROUP)
+        return pltpu.make_async_remote_copy(
+            src_ref=pxs.at[turn], dst_ref=px2_ref.at[rows, cols], send_sem=px_send.at[turn], recv_sem=px_recv.at[turn],
+            device_id=links.pair, device_id_type=MESH)
+
+    def pr_copy(seq):
+        rows = pl.ds(pl.multiple_of(seq * length, length), length)
+        return pltpu.make_async_remote_copy(
+            src_ref=prs.at[seq], dst_ref=pr2_ref.at[rows, :], send_sem=pr_send.at[seq], recv_sem=pr_recv.at[seq],
+            device_id=links.pair, device_id_type=MESH)
+
+    @pl.when(step < turns)
+    def _():
+        group = step % groups
+        mixer_back(heads, groups, group, step == 0, x_ref, bc_ref, dtr_ref, gy_ref, rs_ref, segr_ref, cwx_ref, cwbc_ref, hp_ref, cp_ref,
+                   px_ref, pr_ref, sg_ref, *back)
+        pxs[step] = px_ref[...]
+        px_copy(step).start()
+
+        @pl.when(group == groups - 1)
+        def _():
+            seq = step // groups
+            prs[seq] = pr_ref[...]
+            pr_copy(seq).start()
+
+    @pl.when((step >= turns) & (step < turns + groups))
+    def _():
+        part = dot(mixed_ref[...], wout_ref[...])
+
+        @pl.when(step == turns)
+        def _():
+            acc[...] = tok_ref[...].astype(f32) + part
+
+        @pl.when((step > turns) & (step < turns + groups - 1))
+        def _():
+            acc[...] += part
+
+        @pl.when(step == turns + groups - 1)
+        def _():
+            bo_ref[...] = (acc[...] + part).astype(bf16)
+
+    @pl.when(step >= turns + groups)
+    def _():
+        part = dot(gz_ref[...], win_ref[...], NT)
+
+        @pl.when(step == turns + groups)
+        def _():
+            gn_ref[...] = part
+
+        @pl.when(step > turns + groups)
+        def _():
+            gn_ref[...] += part
+
+    for when in sorted(plan):
+        @pl.when(step == when)
+        def _(when=when):
+            if when == min(plan):
+                for copy in ring.loads():
+                    copy.wait()
+            for hop, slot in plan[when]:
+                ring.hop(hop, slot)
+
+    @pl.when(step == last)
+    def _():
+        sg_ref[6:7, : gg_ref.shape[1]] = gg_ref[0:1, :]
+        for slot in range(3):
+            for k in range(count):
+                ring.land(k, slot, owns[k].at[slot])
+        for turn in range(turns):
+            px_copy(turn).wait()
+        for seq in range(seqs):
+            pr_copy(seq).wait()
+        links.finish()
+
+
+def middle(projected, gy, rs, segr, cw, hp, cp, gg, mixed, w_out_full, tokens, gz, w_in_full, arrays, heads, state, devices):
+    seqs, _, length = segr.shape
+    inner = gy.shape[1]
+    width = tokens.shape[1]
+    groups = inner // GROUP
+    rows = seqs * length
+    turns = seqs * groups
+    chips = devices // 2
+    items = tuple(a.shape[2:] for a in arrays)
+    count = len(items)
+    dma = pltpu.SemaphoreType.DMA
+    seq = lambda i: jnp.minimum(i // groups, seqs - 1)
+    grp = lambda i: jnp.where(i < turns, i % groups, groups - 1)
+    out_at = lambda i: jnp.clip(i - turns, 0, groups - 1)
+    in_at = lambda i: jnp.clip(i - turns - groups, 0, groups - 1)
+    const = lambda *shape: pl.BlockSpec(shape, lambda i: (0,) * len(shape), pipeline_mode=pl.Buffered(1))
+    any_spec = pl.BlockSpec(memory_space=pl.ANY)
+    small_width = inner + 3 * LANES
+    return pl.pallas_call(
+        functools.partial(middle_kernel, heads, chips, seqs, groups, items),
+        grid=(turns + 2 * groups,),
+        in_specs=[
+            pl.BlockSpec((length, GROUP), lambda i: (seq(i), groups + grp(i))),
+            pl.BlockSpec((length, 2 * state), lambda i: (seq(i), 2 * inner // (2 * state))),
+            pl.BlockSpec((length, LANES), lambda i: (seq(i), (2 * inner + 2 * state) // LANES)),
+            pl.BlockSpec((length, GROUP), lambda i: (seq(i), grp(i))),
+            pl.BlockSpec((1, length, LANES), lambda i: (seq(i), 0, 0)),
+            pl.BlockSpec((1, 8, length), lambda i: (seq(i), 0, 0)),
+            pl.BlockSpec((8, GROUP), lambda i: (0, grp(i))),
+            pl.BlockSpec((8, 2 * state), lambda i: (0, inner // (2 * state))),
+            pl.BlockSpec((8, LANES), lambda i: (0, 0)),
+            pl.BlockSpec((8, GROUP), lambda i: (0, grp(i))),
+            const(8, inner),
+            pl.BlockSpec((rows, GROUP), lambda i: (0, out_at(i))),
+            pl.BlockSpec((GROUP, width), lambda i: (out_at(i), 0)),
+            const(rows, width),
+            pl.BlockSpec((rows, GROUP), lambda i: (0, in_at(i))),
+            pl.BlockSpec((width, GROUP), lambda i: (0, in_at(i))),
+        ] + [any_spec] * count,
+        out_specs=[
+            pl.BlockSpec((length, GROUP), lambda i: (seq(i), grp(i))),
+            pl.BlockSpec((length, 3 * LANES), lambda i: (seq(i), 0)),
+            any_spec,
+            any_spec,
+            const(8, small_width),
+            const(rows, width),
+            const(rows, width),
+        ] + [const(3, *item) for item in items],
+        out_shape=[
+            jax.ShapeDtypeStruct((rows, inner), bf16),
+            jax.ShapeDtypeStruct((rows, 3 * LANES), bf16),
+            jax.ShapeDtypeStruct((rows, inner), bf16),
+            jax.ShapeDtypeStruct((rows, 3 * LANES), bf16),
+            jax.ShapeDtypeStruct((8, small_width), f32),
+            jax.ShapeDtypeStruct((rows, width), bf16),
+            jax.ShapeDtypeStruct((rows, width), f32),
+        ] + [jax.ShapeDtypeStruct((3,) + item, bf16) for item in items],
+        scratch_shapes=small_scratch(length) + [
+            pltpu.VMEM((length, length), f32),
+            pltpu.VMEM((length, length), f32),
+            pltpu.VMEM((length, LANES), f32),
+            pltpu.VMEM((length, LANES), f32),
+            pltpu.VMEM((rows, width), f32),
+            pltpu.VMEM((turns, length, GROUP), bf16),
+            pltpu.VMEM((seqs, length, 3 * LANES), bf16),
+            dma((turns,)), dma((turns,)), dma((seqs,)), dma((seqs,)),
+        ] + ring_scratch(items, chips),
+        compiler_params=pltpu.CompilerParams(collective_id=1, has_side_effects=True, vmem_limit_bytes=FULL),
+        name="middle",
+    )(projected, projected, projected, gy, rs, segr, cw, cw, hp, cp, gg, mixed, w_out_full, tokens, gz, w_in_full, *arrays)
+
+
+def tail_kernel(chips, groups, used, items, early, px_ref, pr_ref, win_ref, gacc_ref, tok_ref, cot_ref, gain_ref, sg_ref, *refs):
+    count, first = len(items), len(early)
+    parts, halves, refs = refs[:count], refs[count : count + first], refs[count + first :]
+    gt_ref, small_ref, refs = refs[0], refs[1], refs[2:]
+    outs, refs = refs[: first + count], refs[first + count :]
+    last_in, last_out, refs = refs[: first + count], refs[first + count : first + 2 * count], refs[first + 2 * count :]
+    (small_in, small_sent, small_recv, small_send, small_sem, last_send, last_recv, half_sem), refs = refs[:8], refs[8:]
+    early_held, refs = refs[:first], refs[first:]
+    (held, ring_in, ring_out, peer_in), sems = split_scratch(refs, count)
+    step = pl.program_id(0)
+    links = Links(chips)
+    ring = Ring(links, items, 0, parts, held, ring_in, ring_out, peer_in, *sems)
+    rounds = len(links.turns)
+
+    def swap(k, slot, source):
+        at = k * 3 + slot
+        links.send(source, lambda: last_in[k].at[slot], lambda: last_send.at[at], lambda: last_recv.at[at], links.peer)
+
+    def settle(k, slot, mine):
+        at = k * 3 + slot
+        width = outs[k].shape[2]
+        links.arrived(last_in[k].at[slot], last_send.at[at], last_recv.at[at])
+        if slot < 2:
+            add_up([mine, last_in[k].at[slot]], outs[k].at[slot], width)
+        else:
+            add_up([mine], outs[k].at[2 + links.plane], width)
+            add_up([last_in[k].at[slot]], outs[k].at[3 - links.plane], width)
+
+    halves_in = lambda: [pltpu.make_async_copy(halves[k], early_held[k], half_sem.at[k]) for k in range(first)]
+
+    @pl.when(step == 0)
+    def _():
+        links.greet(list(links.ways) + links.turns)
+        ring.start()
+        for slot in range(3):
+            for k in range(first):
+                swap(k, slot, lambda k=k, slot=slot: halves[k].at[slot])
+        for copy in halves_in():
+            copy.start()
+        gt_ref[...] = gacc_ref[...] + dot(px_ref[...], win_ref[...], NT)
+
+    @pl.when((step > 0) & (step < groups))
+    def _():
+        gt_ref[...] += dot(px_ref[...], win_ref[...], NT)
+
+    @pl.when(step == 2)
+    def _():
+        for copy in ring.loads():
+            copy.wait()
+        ring.hop(1, 2)
+
+    @pl.when(step == groups - 1)
+    def _():
+        ring.hop(2, 0)
+
+    def small_round(turn):
+        links.send(
+            lambda: small_in if turn == 0 else small_sent.at[turn - 1], lambda: small_recv.at[turn],
+            lambda: small_send.at[turn], lambda: small_sem.at[turn], links.turns[turn])
+
+    def small_finish(turn):
+        value = small_in if turn == 0 else small_sent.at[turn - 1]
+        links.arrived(small_recv.at[turn], small_send.at[turn], small_sem.at[turn])
+        store = small_ref if turn == rounds - 1 else small_sent.at[turn]
+        store[...] = value[...] + small_recv[turn]
+
+    @pl.when(step == groups)
+    def _():
+        size = pr_ref.shape[1]
+        col = lax.broadcasted_iota(jnp.int32, (win_ref.shape[0], size), 1)
+        rest = jnp.where(col < used, win_ref[:, :size].astype(f32), 0.0).astype(bf16)
+        rows, width = gt_ref.shape
+        total = jnp.zeros((1, width), f32)
+        for i in range(rows // BLOCK):
+            sl = slice(i * BLOCK, (i + 1) * BLOCK)
+            u = tok_ref[sl].astype(f32)
+            rstd = lax.rsqrt(jnp.mean(u * u, axis=1, keepdims=True) + epsilon)
+            unit = u * rstd
+            gn = gt_ref[sl] + dot(pr_ref[sl], rest, NT)
+            total = total + jnp.sum(gn * unit, axis=0, keepdims=True)
+            gu = gn * gain_ref[0:1, :]
+            inward = jnp.mean(gu * unit, axis=1, keepdims=True)
+            gt_ref[sl] = cot_ref[sl].astype(f32) + rstd * (gu - unit * inward)
+        small_in[...] = sg_ref[...]
+        small_in[7:8, :width] = total
+        small_round(0)
+        done = 0
+        hops = [(q // 3 + 1, q % 3) for q in range(4, 3 * links.half)]
+        every = max(1, len(hops) // rounds)
+        for n, (hop, slot) in enumerate(hops):
+            ring.hop(hop, slot)
+            if n % every == every - 1 and done < rounds - 1:
+                small_finish(done)
+                done += 1
+                small_round(done)
+        for slot in range(3):
+            for k in range(count):
+                ring.land(k, slot, last_out[k].at[slot])
+                swap(first + k, slot, lambda k=k, slot=slot: last_out[k].at[slot])
+        while done < rounds:
+            small_finish(done)
+            done += 1
+            if done < rounds:
+                small_round(done)
+        for copy in halves_in():
+            copy.wait()
+        for slot in range(3):
+            for k in range(first):
+                settle(k, slot, early_held[k].at[slot])
+        for slot in range(3):
+            for k in range(count):
+                settle(first + k, slot, last_out[k].at[slot])
+        links.finish()
+
+
+def tail(px, pr, w_in_full, gacc, tokens, cot, gain, sg, arrays, halves, used, devices):
+    rows, width = tokens.shape
+    groups = px.shape[1] // GROUP
+    chips = devices // 2
+    items = tuple(a.shape[2:] for a in arrays)
+    early = tuple(h.shape[1:] for h in halves)
+    count, first = len(items), len(early)
+    rounds = chips.bit_length() + 1
+    dma = pltpu.SemaphoreType.DMA
+    const = lambda *shape: pl.BlockSpec(shape, lambda i: (0,) * len(shape), pipeline_mode=pl.Buffered(1))
+    any_spec = pl.BlockSpec(memory_space=pl.ANY)
+    every = early + items
+    return pl.pallas_call(
+        functools.partial(tail_kernel, chips, groups, used, items, early),
+        grid=(groups + 1,),
+        in_specs=[
+            pl.BlockSpec((rows, GROUP), lambda i: (0, jnp.minimum(i, groups - 1))),
+            const(rows, pr.shape[1]),
+            pl.BlockSpec((width, GROUP), lambda i: (0, groups + i)),
+            const(rows, width),
+            const(rows, width),
+            const(rows, width),
+            const(8, width),
+            const(*sg.shape),
+        ] + [any_spec] * (count + first),
+        out_specs=[const(rows, width), const(*sg.shape)] + [const(4, *item) for item in every],
+        out_shape=[jax.ShapeDtypeStruct((rows, width), f32), jax.ShapeDtypeStruct(sg.shape, f32)]
+        + [jax.ShapeDtypeStruct((4,) + item, f32) for item in every],
+        scratch_shapes=[pltpu.VMEM((3,) + item, bf16) for item in every] + [pltpu.VMEM((3,) + item, bf16) for item in items] + [
+            pltpu.VMEM(sg.shape, f32), pltpu.VMEM((rounds,) + sg.shape, f32), pltpu.VMEM((rounds,) + sg.shape, f32),
+            dma((rounds,)), dma((rounds,)), dma((3 * (first + count),)), dma((3 * (first + count),)), dma((first,)),
+        ] + [pltpu.VMEM((3,) + item, bf16) for item in early] + ring_scratch(items, chips),
+        compiler_params=pltpu.CompilerParams(collective_id=2, has_side_effects=True, vmem_limit_bytes=FULL),
+        name="tail",
+    )(px, pr, w_in_full, gacc, tokens, cot, gain, sg, *arrays, *halves)
+
+
+def parts_kernel(core_ref, a_ref, a2_ref, b_ref, b2_ref, o_ref):
+    rows = o_ref.shape[0]
+    a = a_ref[...].reshape(rows, a_ref.shape[3])
+    a2 = a2_ref[...].reshape(rows, a2_ref.shape[3])
+    o_ref[...] = (dot(a, b_ref[...]) + dot(a2, b2_ref[...])).astype(bf16)
+
+
+def grad_parts(core, left, left2, right, right2, name):
+    chips, _, rows, tokens = left.shape
+    if rows % 16:
+        pick = lambda v: lax.dynamic_index_in_dim(v, core, 1, keepdims=False).reshape(1, 1, chips * rows, tokens)
+        left, left2, core, chips, rows = pick(left), pick(left2), 0, 1, chips * rows
+    width = right.shape[1]
+    tile = min(GROUP, width)
+    left_spec = pl.BlockSpec((chips, 1, rows, tokens), lambda i, c: (0, c[0], 0, 0), pipeline_mode=pl.Buffered(1))
+    total = chips * rows
+    return pl.pallas_call(
+        parts_kernel,
+        grid_spec=pltpu.PrefetchScalarGridSpec(
+            num_scalar_prefetch=1,
+            grid=(width // tile,),
+            in_specs=[
+                left_spec, left_spec,
+                pl.BlockSpec((tokens, tile), lambda i, c: (0, i)),
+                pl.BlockSpec((tokens, tile), lambda i, c: (0, i)),
+            ],
+            out_specs=pl.BlockSpec((total, tile), lambda i, c: (0, i)),
+        ),
+        out_shape=jax.ShapeDtypeStruct((total, width), bf16),
+        compiler_params=pltpu.CompilerParams(vmem_limit_bytes=FULL),
+        cost_estimate=pl.CostEstimate(flops=4 * total * tokens * width, bytes_accessed=2 * (2 * total * tokens + 2 * tokens * width + total * width), transcendentals=0),
+        name=name,
+    )(jnp.full((1,), core, jnp.int32), left, left2, right, right2)
+
+
 def small_rows(size):
     return 16 * (-(-size // (16 * LANES)))
 
@@ -627,6 +1116,11 @@
     share_n, share_c, share_g = norm_gain.shape[0], conv_bias.shape[0], gate_gain.shape[0]
     conv_width = devices * share_c
     state = (conv_width - inner) // 2
+    chips = devices // 2
+    me = lax.axis_index("fsdp")
+    core = me % 2
+    swap = [(i, i + 1 - 2 * (i % 2)) for i in range(devices)]
+    partner = lambda value: lax.ppermute(value, "fsdp", swap)
 
     size = share_n + share_g + (taps + 1) * share_c
     pack = flat_pack([norm_gain, gate_gain, conv_weight, conv_bias], small_rows(size))
@@ -641,57 +1135,49 @@
     kernel_full = pack_all[:, cuts[1] : cuts[2]].reshape(devices, taps, share_c).transpose(1, 0, 2).reshape(taps, conv_width)
     shift_full = pack_all[:, cuts[2] : cuts[3]].reshape(conv_width)
 
-    residual = tokens.reshape(rows, width).astype(f32)
+    flat_tokens = tokens.reshape(rows, width)
+    residual = flat_tokens.astype(f32)
     rstd = lax.rsqrt(jnp.mean(residual * residual, axis=-1, keepdims=True) + epsilon)
-    unit = residual * rstd
     gain_f = gain_full.astype(f32)
-    normed = (unit * gain_f).astype(bf16)
+    normed = (residual * rstd * gain_f).astype(bf16)
     grad_rows = cotangent.reshape(rows, width)
+    grad_rows2 = partner(grad_rows)
+    normed_t = normed.T.reshape(chips, 2, -1, rows)
+    normed_t2 = partner(normed_t)
     projected = dot(normed, w_in_full)
     gm = dot(grad_rows, w_out_full, NT)
     tables = mixer_tables(segments, kernel_full, shift_full, dt_bias, a_log, d_skip, gate_full)
-    mixed, gz, gy, rs, gg = mixer_forward(projected, gm, *tables, heads, state)
-    block_out = (residual + dot(mixed, w_out_full)).astype(bf16)
-    grad_w_out = lax.dot_general(mixed, grad_rows, (((0,), (0,)), ((), ())), preferred_element_type=f32).astype(bf16)
-    px, pr, gp, gbc, gh = mixer_backward(projected, gy, rs, *tables, heads, state)
-    proj_back = jnp.concatenate([gz, px, pr[:, : 2 * state + heads]], axis=1)
-    grad_normed = dot(proj_back, w_in_full, NT)
-    grad_w_in = lax.dot_general(normed, proj_back, (((0,), (0,)), ((), ())), preferred_element_type=f32).astype(bf16)
-    grad_norm = jnp.sum(grad_normed * unit, axis=0)
-    grad_unit = grad_normed * gain_f
-    grad_tokens = grad_rows.astype(f32) + rstd * (grad_unit - unit * jnp.mean(grad_unit * unit, axis=-1, keepdims=True))
-
-    gp, gbc, gh = gp.sum(0), gbc.sum(0), gh.sum(0)
-    grad_kernel = jnp.concatenate([gp[:taps], gbc[:taps]], axis=1)
-    grad_shift = jnp.concatenate([gp[taps], gbc[taps]])
-    grad_gate = gg[:, 0].sum(0)
-    grad_skip = gp[taps + 1].reshape(heads, inner // heads).sum(1)
-
-    small = jnp.concatenate([
-        grad_norm.reshape(devices, share_n), grad_gate.reshape(devices, share_g),
-        grad_kernel.reshape(taps, devices, share_c).transpose(1, 0, 2).reshape(devices, taps * share_c),
-        grad_shift.reshape(devices, share_c)], axis=1)
-    small = lax.psum_scatter(small, "fsdp", scatter_dimension=0, tiled=True)
-    small = lax.psum(small, "dp")[0]
-    head_grads = lax.psum(jnp.stack([gh[0, :heads], gh[1, :heads], grad_skip]), ("fsdp", "dp"))
-
-    def owned(full):
-        mine = lax.psum_scatter(full, "fsdp", scatter_dimension=0, tiled=True)
-        other = lax.ppermute(mine, "dp", [(0, 1), (1, 0)])
-        return mine.astype(f32) + other.astype(f32)
-
+    mixed, mixed_t, gz, gy, rs, gg = mixer_forward(projected, gm, *tables, heads, state)
+    mixed_t = mixed_t.reshape(chips, 2, -1, rows)
+    gz2, mixed_t2 = partner(gz), partner(mixed_t)
+    quarters = lambda part: part.reshape(chips, QUARTERS, -1, part.shape[1])
+    part_out = quarters(grad_parts(core, mixed_t, mixed_t2, grad_rows, grad_rows2, "grad_out"))
+    part_z = quarters(grad_parts(core, normed_t, normed_t2, gz, gz2, "grad_z"))
+    px, pr, px2, pr2, sg, block_out, gacc, half_out, half_z = middle(
+        projected, gy, rs, *tables, gg, mixed, w_out_full, flat_tokens, gz, w_in_full, [part_out, part_z], heads, state, devices)
+    part_x = quarters(grad_parts(core, normed_t, normed_t2, px, px2, "grad_x"))
+    part_r = quarters(grad_parts(core, normed_t, normed_t2, pr, pr2, "grad_r"))
+    gain8 = jnp.broadcast_to(gain_f[None], (8, width))
+    grad_tokens, small, own_out, own_z, own_x, own_r = tail(
+        px, pr, w_in_full, gacc, flat_tokens, grad_rows, gain8, sg, [part_x, part_r], [half_out, half_z], 2 * state + heads, devices)
+
+    grad_w_in = jnp.concatenate([o.reshape(-1, o.shape[2]) for o in (own_z, own_x, own_r)], axis=1)[:, :proj_width]
+    conv = lax.dynamic_slice(small, (0, me * share_c), (taps + 1, share_c))
+    gate = lax.dynamic_slice(small, (6, me * share_g), (1, share_g))
+    norm = lax.dynamic_slice(small, (7, me * share_n), (1, share_n))
+    skip = small[taps + 1, :inner].reshape(heads, inner // heads).sum(1)
     return (
         block_out.reshape(seqs, length, width),
         grad_tokens.reshape(seqs, length, width),
-        small[: cuts[0]],
-        owned(grad_w_in),
-        small[cuts[1] : cuts[2]].reshape(taps, share_c),
-        small[cuts[2] : cuts[3]],
-        head_grads[0],
-        head_grads[1],
-        head_grads[2],
-        small[cuts[0] : cuts[1]],
-        owned(grad_w_out),
+        norm[0],
+        grad_w_in,
+        conv[:taps],
+        conv[taps],
+        small[0, conv_width : conv_width + heads],
+        small[1, conv_width : conv_width + heads],
+        skip,
+        gate[0],
+        own_out.reshape(-1, width),
     )
 
 

time: 641 us -> 421 us (0.66)
  waiting for transfers between devices: 278 us -> 8.42 us
  Pallas kernels: 193 us -> 355 us
  matrix products: 78.6 us -> 25 us
  blocking collectives: 46.7 us -> 0 us
  between operations: 14.2 us -> 1.02 us
  local copies, waits for them, and re-layouts: 15.4 us -> 22.5 us
    reduce_scatter x2 -> x0, waiting for transfers between devices: 190 us -> none  [owned(): mine = lax.psum_scatter(full, 'fsdp', scatter_dimension=0, tiled=True)]
    pallas_call x1 -> x6, Pallas kernels: 35.2 us -> 195 us  [the longest x1 91.8 us: middle(): pl.pallas_call(functools.partial(middle_kernel, heads, chips, seqs, group...]
    unnamed x4 -> x0, waiting for transfers between devices: 88 us -> none
    psum x2 -> x0, blocking collectives: 46.7 us -> none  [the longest x1 41.8 us: local(): lax.psum(jnp.stack([gh[0, :heads], gh[1, :heads], grad_skip]), ('fsdp', '...]
    dot_general x4 -> x2, matrix products: 54.2 us -> 25 us  [dot(): lax.dot_general(a, b, dims, precision=precision, preferred_element_type=f32)]
    dot_general x2 -> x0, matrix products: 24.4 us -> none  [the longest x1 17 us: local(): lax.dot_general(normed, proj_back, (((0,), (0,)), ((), ())), preferred_el...]
    ppermute x2 -> x4, waiting for transfers between devices: 0.01 us -> 8.42 us  [local(): partner = lambda value: lax.ppermute(value, 'fsdp', swap)]
    add x3 -> x0, other arithmetic: 6.77 us -> none  [the longest x2 3.96 us: owned(): return mine.astype(f32) + other.astype(f32)]
  transfers between devices with their start and end apart: 5 -> 4, of which waited for: 2 -> 1; matrix products, arithmetic and copies ran while one was open for 9% -> 1% of each run, Pallas kernels for 6% -> 2%
where the time goes in v3:
time: 421 us; the launch traced here: 419 us
  Pallas kernels  355 us (84%)
  matrix products  25 us (6%)
  local copies, waits for them, and re-layouts  22.5 us (5%)
  waiting for transfers between devices  8.42 us (2%)
  other arithmetic  6.77 us (2%)
    pallas_call x1, Pallas kernels, gather(): pl.pallas_call(functools.partial(gather_kernel, chips, count), in_specs=[...  121 us
    pallas_call x1, Pallas kernels, middle(): pl.pallas_call(functools.partial(middle_kernel, heads, chips, seqs, group...  91.8 us
    pallas_call x1, Pallas kernels, tail(): pl.pallas_call(functools.partial(tail_kernel, chips, groups, used, items,...  71.7 us
    pallas_call x1, Pallas kernels, mixer_forward(): pl.pallas_call(kernel, grid=(seqs, 2, groups), in_specs=[pl.BlockSpec((le...  37.8 us
    pallas_call x4, Pallas kernels, grad_parts(): pl.pallas_call(parts_kernel, grid_spec=pltpu.PrefetchScalarGridSpec(num_s...  31.9 us
    dot_general x2, matrix products, dot(): lax.dot_general(a, b, dims, precision=precision, preferred_element_type=f32)  25 us
    ppermute x4, waiting for transfers between devices, local(): partner = lambda value: lax.ppermute(value, 'fsdp', swap)  8.42 us
  transfers between devices with their start and end apart: 4, of which 1 were waited for; matrix products, arithmetic and copies ran while one was open for 1% of the time, Pallas kernels for 2%

profile of v3, /device:TPU:0, one launch (start us, length us, event | category | flops | bytes accessed | tf_op | source)
XLA Modules:
  0.0 419.5 jit_solution(14361445569869915707)
XLA Ops:
  1.6 2.1 concatenate.15
  4.2 121.3 %gather_weights.1 = (bf16[16,3,32,6448]{3,2,1,0:T(8,128)(2,1)}, bf16[16,3,64,1536]{3,2,1,0:T(8,128)(2,1)}, bf16[16,16,128]{2,1,0:T(8,128)(2,1)}) custom-call(bf16[3,32,6448]{2,1,0:T(8,128)(2,1)} %bitcast.72, bf16[3,64,1536]{2,1,0:T(8,128)(2,1)} %bitcast.76, bf16[16,128]{1,0:T(8,128)(2,1)} %pad_bitcast_fusion.refs_2_), custom_call_target="tpu_custom_call" | custom-call | tf_op jit(solution)/shard_map/gather_weights/pallas_call | solution.py:555
  128.3 18.0 %fusion.5.z_ref.x_ref.bc_ref.dtr_ref = f32[512,6448]{1,0:T(8,128)} fusion(bf16[512,1536]{1,0:T(8,128)(2,1)S(1)} %bitcast.71, bf16[1536,6448]{1,0:T(8,128)(2,1)} %bitcast.48), kind=kOutput, calls=%fused_computation.28 | convolution fusion | flops 10141827072 | bytes 34586624 | tf_op jit(solution)/shard_map/dot_general | solution.py:22
  146.4 7.0 %convolution_bitcast_fusion.gm_ref = f32[512,3072]{1,0:T(8,128)} fusion(bf16[3072,1536]{1,0:T(8,128)(2,1)S(1)} %bitcast.56, bf16[512,1536]{1,0:T(8,128)(2,1)S(1)} %bitcast.69), kind=kOutput, calls=%fused_computation | convolution fusion | flops 4831838208 | bytes 17301504 | tf_op jit(solution)/shard_map/dot_general | solution.py:22
  153.6 37.8 %mixer_forward.1 = (bf16[512,3072]{1,0:T(8,128)(2,1)S(1)}, bf16[3072,512]{1,0:T(8,128)(2,1)}, bf16[512,3072]{1,0:T(8,128)(2,1)}, f32[512,3072]{1,0:T(8,128)}, f3...) custom-call(f32[512,6448]{1,0:T(8,128)} %fusion.5.z_ref.x_ref.bc_ref.dtr_ref, ...), custom_call_target="tpu_custom_call" | custom-call | flops 10000000000 | bytes 45000000 | tf_op jit(solution)/shard_map/mixer_forward/pallas_call | solution.py:339
  191.4 1.7 copy-done
  194.9 1.6 fusion.3
  196.5 1.7 copy.41
  198.9 8.4 %collective-permute-done.2.a2_ref = bf16[8,2,96,512]{3,2,1,0:T(8,128)(2,1)} collective-permute-done((bf16[8,2,96,512]{3,2,1,0:T(8,128)(2,1)S(1)}, bf16[8,2,96,512]{3,2,1,0:T(8,128)(2,1)}, u32[]{:S(2)}, u32[]{:S(2)}) %collective-permute-start.2) | collective-permute-done | bytes 1572896 | tf_op jit(solution)/shard_map/ppermute | solution.py:1123
  207.3 9.8 %grad_z.1 = bf16[768,3072]{1,0:T(8,128)(2,1)} custom-call(s32[1]{0:T(128)} %bitcast.11.core_ref, bf16[8,2,96,512]{3,2,1,0:T(8,128)(2,1)} %bitcast.58, bf16[8,2,96,512]{3,2,1,0:T(8,128)(2,1)} %collective-permute-done.2.a2_ref, bf16[512,3072]{1,0:T(8,128)(2,1)} %get-tuple-element.42.b_ref.gz_ref, bf16[512,3072]{1,0:T(8,128)(2,1)} %collective-permute-done.3.b2_ref), custom_call_target="tpu_custom_call" | custom-call | flops 4831838208 | bytes 12582912 | tf_op jit(solution)/shard_map/grad_z/pallas_call | solution.py:1081
  217.1 9.0 %grad_out.1 = bf16[1536,1536]{1,0:T(8,128)(2,1)} custom-call(s32[1]{0:T(128)} %bitcast.11.core_ref, bf16[8,2,192,512]{3,2,1,0:T(8,128)(2,1)} %bitcast.89, bf16[8,2,192,512]{3,2,1,0:T(8,128)(2,1)} %collective-permute-done.a2_ref, bf16[512,1536]{1,0:T(8,128)(2,1)} %bitcast.67, bf16[512,1536]{1,0:T(8,128)(2,1)} %collective-permute-done.1.b2_ref), custom_call_target="tpu_custom_call" | custom-call | flops 4831838208 | bytes 11010048 | tf_op jit(solution)/shard_map/grad_out/pallas_call | solution.py:1081
  226.1 91.8 %middle.1 = (bf16[512,3072]{1,0:T(8,128)(2,1)}, bf16[512,384]{1,0:T(8,128)(2,1)}, bf16[512,3072]{1,0:T(8,128)(2,1)}, bf16[512,384]{1,0:T(8,128)(2,1)}, f32[8,345...) custom-call(f32[512,6448]{1,0:T(8,128)} %fusion.5.z_ref.x_ref.bc_ref, ...), custom_call_target="tpu_custom_call" | custom-call | tf_op jit(solution)/shard_map/middle/pallas_call | solution.py:859
  317.8 3.4 grad_r.1
  321.2 9.8 %grad_x.1 = bf16[768,3072]{1,0:T(8,128)(2,1)} custom-call(s32[1]{0:T(128)} %bitcast.11.core_ref, bf16[8,2,96,512]{3,2,1,0:T(8,128)(2,1)} %bitcast.60, bf16[8,2,96,512]{3,2,1,0:T(8,128)(2,1)} %collective-permute-done.2.a2_ref, bf16[512,3072]{1,0:T(8,128)(2,1)} %get-tuple-element.45.b_ref.px_ref, bf16[512,3072]{1,0:T(8,128)(2,1)} %get-tuple-element.49.b2_ref), custom_call_target="tpu_custom_call" | custom-call | flops 4831838208 | bytes 12582912 | tf_op jit(solution)/shard_map/grad_x/pallas_call | solution.py:1081
  331.6 71.7 %tail.1 = (f32[512,1536]{1,0:T(8,128)}, f32[8,3456]{1,0:T(8,128)}, f32[4,48,1536]{2,1,0:T(8,128)}, f32[4,24,3072]{2,1,0:T(8,128)}, f32[4,24,3072]{2,1,0:T(8,128)}, /*index=5*/f32[4,24,384]{2,1,0:T(8,128)}) custom-call(bf16[512,3072]{1,0:T(8,128)(2,1)} %get-tuple-element.45.b_ref.px_ref, bf16[512,384]{1,0:T(8,128)(2,1)} %get-tuple-element.46.b_ref.pr_ref, ...), custom_call_target="tpu_custom_call" | custom-call | tf_op jit(solution)/shard_map/tail/pallas_call | solution.py:1040
  403.4 1.0 slice_reduce_fusion
  404.4 1.3 slice_bitcast_fusion
  405.8 1.4 constant_dynamic-slice_fusion.1
  407.2 1.3 dynamic-slice.1
  408.5 1.3 constant_dynamic-slice_fusion
  409.8 1.3 dynamic-slice_bitcast_fusion
  411.7 3.5 pad_maximum_fusion
  415.2 1.1 copy.54
  416.4 1.7 copy.55
  (78 shorter events, 9.5 us)
Async XLA Ops:
  0.6 126.1 %copy-start.7 = (bf16[2,256,1536]{2,1,0:T(8,128)(2,1)S(1)}, bf16[2,256,1536]{2,1,0:T(8,128)(2,1)}, u32[]{:S(2)}) copy-start(bf16[2,256,1536]{2,1,0:T(8,128)(2,1)} %param.12) | copy-start | bytes 4718596
  0.7 126.9 %copy-start.14 = (f32[48]{0:T(128)S(1)}, f32[48]{0:T(128)}, u32[]{:S(2)}) copy-start(f32[48]{0:T(128)} %param.20) | copy-start | bytes 580
  0.7 127.1 %copy-start.13 = (s32[2,256]{1,0:T(2,128)S(1)}, s32[2,256]{1,0:T(2,128)}, u32[]{:S(2)}) copy-start(s32[2,256]{1,0:T(2,128)} %param.13) | copy-start | bytes 6148
  127.8 18.6 %slice-start = ((s8[9437184]{0:T(1024)(128)(4,1)}), s8[4194304]{0:T(1024)(128)(4,1)S(1)}, s32[]{:S(2)}) async-start(s8[9437184]{0:T(1024)(128)(4,1)} %bitcast.54), calls=%async_computation | async-start | bytes 8388608
  128.2 18.1 %slice-start.1 = ((s8[9437184]{0:T(1024)(128)(4,1)}), s8[4194304]{0:T(1024)(128)(4,1)S(1)}, s32[]{:S(2)}) async-start(s8[9437184]{0:T(1024)(128)(4,1)} %bitcast.54), calls=%async_computation.1 | async-start | bytes 8388608
  128.2 18.1 %slice-start.2 = ((s8[9437184]{0:T(1024)(128)(4,1)}), s8[1048576]{0:T(1024)(128)(4,1)S(1)}, s32[]{:S(2)}) async-start(s8[9437184]{0:T(1024)(128)(4,1)} %bitcast.54), calls=%async_computation.2 | async-start | bytes 2097152
  128.2 18.1 %copy-start.10 = (bf16[2,256,1536]{2,1,0:T(8,128)(2,1)S(1)}, bf16[2,256,1536]{2,1,0:T(8,128)(2,1)}, u32[]{:S(2)}) copy-start(bf16[2,256,1536]{2,1,0:T(8,128)(2,1)} %param.23) | copy-start | bytes 4718596
  146.3 7.2 %copy-start.1 = (f32[8,3328]{1,0:T(8,128)}, f32[8,3328]{1,0:T(8,128)S(1)}, u32[]{:S(2)}) copy-start(f32[8,3328]{1,0:T(8,128)S(1)} %pad_maximum_fusion.2.cwx_ref.cwbc_ref) | copy-start | bytes 319492
  146.4 7.1 %copy-start.15 = (f32[48]{0:T(128)S(1)}, f32[48]{0:T(128)}, u32[]{:S(2)}) copy-start(f32[48]{0:T(128)} %param.19) | copy-start | bytes 580
  146.4 7.1 %copy-start.16 = (f32[48]{0:T(128)S(1)}, f32[48]{0:T(128)}, u32[]{:S(2)}) copy-start(f32[48]{0:T(128)} %param.18) | copy-start | bytes 580
  153.5 37.9 %copy-start.2 = (f32[8,3072]{1,0:T(8,128)}, f32[8,3072]{1,0:T(8,128)S(1)}, u32[]{:S(2)}) copy-start(f32[8,3072]{1,0:T(8,128)S(1)} %pad_maximum_fusion.3.cp_ref) | copy-start | bytes 294916
  153.5 37.8 %copy-start.6 = (f32[8,128]{1,0:T(8,128)}, f32[8,128]{1,0:T(8,128)S(1)}, u32[]{:S(2)}) copy-start(f32[8,128]{1,0:T(8,128)S(1)} %select_maximum_fusion.hp_ref) | copy-start | bytes 12292
  153.5 37.8 %copy-start.4 = (f32[2,8,256]{2,1,0:T(8,128)}, f32[2,8,256]{2,1,0:T(8,128)S(1)}, u32[]{:S(2)}) copy-start(f32[2,8,256]{2,1,0:T(8,128)S(1)} %broadcast_in_dim.16.segr_ref) | copy-start | bytes 49156
  191.3 1.7 copy-start
  193.0 0.7 copy-start.3
  193.7 0.6 copy-start.5
  194.4 12.9 %collective-permute-start.3 = (bf16[512,3072]{1,0:T(8,128)(2,1)}, bf16[512,3072]{1,0:T(8,128)(2,1)}, u32[]{:S(2)}, u32[]{:S(2)}) collective-permute-start(bf16[512,3072]{1,0:T(8,128)(2,1)} %get-tuple-element.42.b_ref.gz_ref), channel_id=1, source_target_pairs={{0,2},{2,0},{4,6},{6,4},{8,10},{10,8},{12,14},{14,12},{16,18},{18,... | collective-permute-start | bytes 9437192 | tf_op jit(solution)/shard_map/ppermute | solution.py:1123
  194.9 22.2 %collective-permute-start = (bf16[8,2,192,512]{3,2,1,0:T(8,128)(2,1)}, bf16[8,2,192,512]{3,2,1,0:T(8,128)(2,1)}, u32[]{:S(2)}, u32[]{:S(2)}) collective-permute-start(bf16[8,2,192,512]{3,2,1,0:T(8,128)(2,1)} %bitcast.88), channel_id=1, source_target_pairs={{0,2},{2,0},{4,6},{6,4},{8,10},{10,8},{12,14},{14,12},{16,18},{18,... | collective-permute-start | bytes 9437192 | tf_op jit(solution)/shard_map/ppermute | solution.py:1123
  198.2 9.1 %copy-start.8 = (bf16[1536,512]{1,0:T(8,128)(2,1)}, bf16[1536,512]{1,0:T(8,128)(2,1)S(1)}, u32[]{:S(2)}) copy-start(bf16[1536,512]{1,0:T(8,128)(2,1)S(1)} %copy.41) | copy-start | bytes 4718596
  198.2 9.1 %collective-permute-start.2 = (bf16[8,2,96,512]{3,2,1,0:T(8,128)(2,1)S(1)}, bf16[8,2,96,512]{3,2,1,0:T(8,128)(2,1)}, u32[]{:S(2)}, u32[]{:S(2)}) collective-permute-start(bf16[8,2,96,512]{3,2,1,0:T(8,128)(2,1)S(1)} %bitcast.57), channel_id=1, source_target_pairs={{0,2},{2,0},{4,6},{6,4},{8,10},{10,8},{12,14},{14,12},{16,18},{18,... | collective-permute-start | bytes 4718600 | tf_op jit(solution)/shard_map/ppermute | solution.py:1123
  198.8 18.3 %collective-permute-start.1 = (bf16[512,1536]{1,0:T(8,128)(2,1)}, bf16[512,1536]{1,0:T(8,128)(2,1)}, u32[]{:S(2)}, u32[]{:S(2)}) collective-permute-start(bf16[512,1536]{1,0:T(8,128)(2,1)} %bitcast.66), channel_id=1, source_target_pairs={{0,2},{2,0},{4,6},{6,4},{8,10},{10,8},{12,14},{14,12},{16,18},{18,... | collective-permute-start | bytes 4718600 | tf_op jit(solution)/shard_map/ppermute | solution.py:1123
  403.4 11.8 %copy-start.11 = (bf16[512,1536]{1,0:T(8,128)(2,1)S(1)}, bf16[512,1536]{1,0:T(8,128)(2,1)}, u32[]{:S(2)}) copy-start(bf16[512,1536]{1,0:T(8,128)(2,1)} %get-tuple-element.44) | copy-start | bytes 4718596
  411.7 4.6 %copy-start.9 = (f32[512,1536]{1,0:T(8,128)S(1)}, f32[512,1536]{1,0:T(8,128)}, u32[]{:S(2)}) copy-start(f32[512,1536]{1,0:T(8,128)} %get-tuple-element.53) | copy-start | bytes 9437188
  416.4 2.1 copy-start.12

commit v4 on v3

--- a/solution.py
+++ b/solution.py
@@ -627,9 +627,9 @@
 
 
 class Ring:
-    def __init__(self, links, items, shift, parts, held, ring_in, ring_out, peer_in, held_sem, ring_send, ring_recv, peer_send, peer_recv):
+    def __init__(self, links, items, shift, parts, held, ring_in, peer_in, held_sem, ring_send, ring_recv, peer_send, peer_recv):
         self.links, self.items, self.shift, self.parts = links, items, shift, parts
-        self.held, self.ring_in, self.ring_out, self.peer_in = held, ring_in, ring_out, peer_in
+        self.held, self.ring_in, self.peer_in = held, ring_in, peer_in
         self.held_sem, self.ring_send, self.ring_recv = held_sem, ring_send, ring_recv
         self.peer_send, self.peer_recv = peer_send, peer_recv
 
@@ -675,6 +675,17 @@
         for copy in self.loads():
             copy.start()
 
+    def sequence(self):
+        half = self.links.half
+        main = [("hop", step, slot) for step in range(2, half + 1) for slot in (0, 1)]
+        other = [("hop", step, 2) for step in range(1, half + 1)]
+        out = []
+        for n, entry in enumerate(main):
+            out.append(entry)
+            if n >= 3 and n % 2 and len(other) > 2:
+                out.append(other.pop(0))
+        return out + [("land", 0, 0), ("land", 0, 1)] + other + [("land", 0, 2)]
+
     def order(self):
         chips, half = self.links.chips, self.links.half
         moves = []
@@ -702,15 +713,18 @@
                     continue
                 chunk = self.target(k, way, slot, step)
                 sources = [self.held[k].at[slot, chunk]]
+                if slot == 2:
+                    sources.append(self.from_peer(k, chunk))
                 if step > 1:
                     before = self.at(way, step - 1, slot)
                     self.links.arrived(self.ring_in[k].at[before], *self.sems(k, way, step - 1, slot))
                     sources.append(self.ring_in[k].at[before])
-                if slot == 2:
-                    sources.append(self.from_peer(k, chunk))
-                at = self.at(way, step, slot)
-                add_up(sources, self.ring_out[k].at[at], self.items[k][1])
-                self.push(k, way, step, slot, lambda k=k, at=at: self.ring_out[k].at[at])
+                    store = lambda k=k, before=before: self.ring_in[k].at[before]
+                else:
+                    store = lambda k=k, way=way, slot=slot, step=step: self.peer_in[k].at[
+                        ring_place(self.target(k, way, slot, step), self.links.chips)]
+                add_up(sources, store(), self.items[k][1])
+                self.push(k, way, step, slot, store)
 
     def land(self, k, slot, store):
         links = self.links
@@ -729,49 +743,52 @@
     dma = pltpu.SemaphoreType.DMA
     half, count = chips // 2, len(items)
     vm = lambda *lead: [pltpu.VMEM(lead + item, bf16) for item in items]
-    return vm(3, chips) + vm(6 * half) + vm(6 * half) + vm(chips) + [
+    return vm(3, chips) + vm(6 * half) + vm(chips) + [
         dma((3 * count,)), dma((6 * half * count,)), dma((6 * half * count,)), dma((chips * count,)), dma((chips * count,))]
 
 
 def split_scratch(refs, count):
-    return [refs[i * count : (i + 1) * count] for i in range(4)], refs[4 * count : 4 * count + 5]
+    return [refs[i * count : (i + 1) * count] for i in range(3)], refs[3 * count : 3 * count + 5]
 
 
 def middle_kernel(heads, chips, seqs, groups, items, x_ref, bc_ref, dtr_ref, gy_ref, rs_ref, segr_ref, cwx_ref, cwbc_ref, hp_ref, cp_ref,
-                  gg_ref, mixed_ref, wout_ref, tok_ref, gz_ref, win_ref, *refs):
+                  gg_ref, mixed_ref, wout_ref, tok_ref, gz_ref, win_ref, nt_ref, nt2_ref, *refs):
     count = len(items)
     parts, refs = refs[:count], refs[count:]
-    px_ref, pr_ref, px2_ref, pr2_ref, sg_ref, bo_ref, gn_ref = refs[:7]
-    owns, refs = refs[7 : 7 + count], refs[7 + count :]
-    back, (acc, pxs, prs, px_send, px_recv, pr_send, pr_recv), refs = refs[:13], refs[13:20], refs[20:]
-    (held, ring_in, ring_out, peer_in), sems = split_scratch(refs, count)
+    px_ref, pr_ref, partx_ref, partr_ref, sg_ref, bo_ref, gn_ref = refs[:7]
+    owns, nears, refs = refs[7 : 7 + count], refs[7 + count : 7 + 2 * count], refs[7 + 2 * count :]
+    back, (nts, nts2, pxs, prs, px2s, pr2s, nt_sem, px_send, px_recv, pr_send, pr_recv, near_send, near_recv), refs = refs[:13], refs[13:26], refs[26:]
+    (held, ring_in, peer_in), sems = split_scratch(refs, count)
     step = pl.program_id(0)
     turns = seqs * groups
-    last = turns + 2 * groups - 1
+    last = turns + 3 * groups
     length = x_ref.shape[0]
     links = Links(chips)
-    ring = Ring(links, items, 0, parts, held, ring_in, ring_out, peer_in, *sems)
+    ring = Ring(links, items, 0, parts, held, ring_in, peer_in, *sems)
+    turned = lambda: [
+        pltpu.make_async_copy(source.at[:, links.core], target, nt_sem.at[n])
+        for n, (source, target) in enumerate(((nt_ref, nts), (nt2_ref, nts2)))]
 
     @pl.when(step == 0)
     def _():
         links.greet([links.ways[0], links.ways[1], links.peer, links.pair])
         ring.start()
+        for copy in turned():
+            copy.start()
 
     plan = {}
-    for q in range(2, 3 * links.half):
-        plan.setdefault(min(last, max(3, (24 // (links.half * 2)) * (q - 1))), []).append((q // 3 + 1, q % 3))
+    sequence = ring.sequence()
+    for n, entry in enumerate(sequence):
+        plan.setdefault(max(2, (n + 1) * last // len(sequence)), []).append(entry)
 
     def px_copy(turn):
-        rows = pl.ds(pl.multiple_of(turn // groups * length, length), length)
-        cols = pl.ds(pl.multiple_of(turn % groups * GROUP, GROUP), GROUP)
         return pltpu.make_async_remote_copy(
-            src_ref=pxs.at[turn], dst_ref=px2_ref.at[rows, cols], send_sem=px_send.at[turn], recv_sem=px_recv.at[turn],
+            src_ref=pxs.at[turn], dst_ref=px2s.at[turn], send_sem=px_send.at[turn], recv_sem=px_recv.at[turn],
             device_id=links.pair, device_id_type=MESH)
 
     def pr_copy(seq):
-        rows = pl.ds(pl.multiple_of(seq * length, length), length)
         return pltpu.make_async_remote_copy(
-            src_ref=prs.at[seq], dst_ref=pr2_ref.at[rows, :], send_sem=pr_send.at[seq], recv_sem=pr_recv.at[seq],
+            src_ref=prs.at[seq], dst_ref=pr2s.at[seq], send_sem=pr_send.at[seq], recv_sem=pr_recv.at[seq],
             device_id=links.pair, device_id_type=MESH)
 
     @pl.when(step < turns)
@@ -794,17 +811,17 @@
 
         @pl.when(step == turns)
         def _():
-            acc[...] = tok_ref[...].astype(f32) + part
+            gn_ref[...] = tok_ref[...].astype(f32) + part
 
         @pl.when((step > turns) & (step < turns + groups - 1))
         def _():
-            acc[...] += part
+            gn_ref[...] += part
 
         @pl.when(step == turns + groups - 1)
         def _():
-            bo_ref[...] = (acc[...] + part).astype(bf16)
-
-    @pl.when(step >= turns + groups)
+            bo_ref[...] = (gn_ref[...] + part).astype(bf16)
+
+    @pl.when((step >= turns + groups) & (step < turns + 2 * groups))
     def _():
         part = dot(gz_ref[...], win_ref[...], NT)
 
@@ -815,6 +832,39 @@
         @pl.when(step > turns + groups)
         def _():
             gn_ref[...] += part
+
+    def own_rows(mine, theirs, store):
+        many, each, tokens = nts.shape
+        pieces = [(n * length, left, right) for left, rights in ((nts, mine), (nts2, theirs)) for n, right in enumerate(rights)]
+        if each % 16 == 0:
+            total = None
+            for at, left, right in pieces:
+                part = dot(left[:, :, at : at + length].reshape(many * each, length), right)
+                total = part if total is None else total + part
+            store[...] = total.astype(bf16)
+        else:
+            for n in range(many):
+                total = sum(dot(left[n, :, at : at + length], right) for at, left, right in pieces)
+                store[n * each : (n + 1) * each, :] = total.astype(bf16)
+
+    @pl.when(step == turns + 2 * groups)
+    def _():
+        for copy in turned():
+            copy.wait()
+        for turn in range(turns):
+            px_copy(turn).wait()
+        for seq in range(seqs):
+            pr_copy(seq).wait()
+
+    @pl.when((step >= turns + 2 * groups) & (step < turns + 3 * groups))
+    def _():
+        group = step - turns - 2 * groups
+        at = [group + seq * groups for seq in range(seqs)]
+        own_rows([pxs[n] for n in at], [px2s[n] for n in at], partx_ref)
+
+    @pl.when(step == last)
+    def _():
+        own_rows([prs[n] for n in range(seqs)], [pr2s[n] for n in range(seqs)], partr_ref)
 
     for when in sorted(plan):
         @pl.when(step == when)
@@ -822,23 +872,27 @@
             if when == min(plan):
                 for copy in ring.loads():
                     copy.wait()
-            for hop, slot in plan[when]:
-                ring.hop(hop, slot)
+            for kind, hop, slot in plan[when]:
+                if kind == "hop":
+                    ring.hop(hop, slot)
+                    continue
+                for k in range(count):
+                    ring.land(k, slot, owns[k].at[slot])
+                    if slot < 2:
+                        links.send(
+                            lambda k=k, slot=slot: owns[k].at[slot], lambda k=k, slot=slot: nears[k].at[slot],
+                            lambda k=k, slot=slot: near_send.at[2 * k + slot], lambda k=k, slot=slot: near_recv.at[2 * k + slot], links.peer)
 
     @pl.when(step == last)
     def _():
         sg_ref[6:7, : gg_ref.shape[1]] = gg_ref[0:1, :]
-        for slot in range(3):
+        for slot in range(2):
             for k in range(count):
-                ring.land(k, slot, owns[k].at[slot])
-        for turn in range(turns):
-            px_copy(turn).wait()
-        for seq in range(seqs):
-            pr_copy(seq).wait()
+                links.arrived(nears[k].at[slot], near_send.at[2 * k + slot], near_recv.at[2 * k + slot])
         links.finish()
 
 
-def middle(projected, gy, rs, segr, cw, hp, cp, gg, mixed, w_out_full, tokens, gz, w_in_full, arrays, heads, state, devices):
+def middle(projected, gy, rs, segr, cw, hp, cp, gg, mixed, w_out_full, tokens, gz, w_in_full, left, left2, arrays, heads, state, devices):
     seqs, _, length = segr.shape
     inner = gy.shape[1]
     width = tokens.shape[1]
@@ -853,12 +907,14 @@
     grp = lambda i: jnp.where(i < turns, i % groups, groups - 1)
     out_at = lambda i: jnp.clip(i - turns, 0, groups - 1)
     in_at = lambda i: jnp.clip(i - turns - groups, 0, groups - 1)
+    x_at = lambda i: jnp.clip(i - turns - 2 * groups, 0, groups - 1)
+    total = chips * left.shape[2]
     const = lambda *shape: pl.BlockSpec(shape, lambda i: (0,) * len(shape), pipeline_mode=pl.Buffered(1))
     any_spec = pl.BlockSpec(memory_space=pl.ANY)
     small_width = inner + 3 * LANES
     return pl.pallas_call(
         functools.partial(middle_kernel, heads, chips, seqs, groups, items),
-        grid=(turns + 2 * groups,),
+        grid=(turns + 3 * groups + 1,),
         in_specs=[
             pl.BlockSpec((length, GROUP), lambda i: (seq(i), groups + grp(i))),
             pl.BlockSpec((length, 2 * state), lambda i: (seq(i), 2 * inner // (2 * state))),
@@ -876,94 +932,89 @@
             const(rows, width),
             pl.BlockSpec((rows, GROUP), lambda i: (0, in_at(i))),
             pl.BlockSpec((width, GROUP), lambda i: (0, in_at(i))),
-        ] + [any_spec] * count,
+        ] + [any_spec] * (2 + count),
         out_specs=[
             pl.BlockSpec((length, GROUP), lambda i: (seq(i), grp(i))),
             pl.BlockSpec((length, 3 * LANES), lambda i: (seq(i), 0)),
-            any_spec,
-            any_spec,
+            pl.BlockSpec((total, GROUP), lambda i: (0, x_at(i))),
+            const(total, 3 * LANES),
             const(8, small_width),
             const(rows, width),
             const(rows, width),
-        ] + [const(3, *item) for item in items],
+        ] + [const(3, *item) for item in items] + [any_spec] * count,
         out_shape=[
             jax.ShapeDtypeStruct((rows, inner), bf16),
             jax.ShapeDtypeStruct((rows, 3 * LANES), bf16),
-            jax.ShapeDtypeStruct((rows, inner), bf16),
-            jax.ShapeDtypeStruct((rows, 3 * LANES), bf16),
+            jax.ShapeDtypeStruct((total, inner), bf16),
+            jax.ShapeDtypeStruct((total, 3 * LANES), bf16),
             jax.ShapeDtypeStruct((8, small_width), f32),
             jax.ShapeDtypeStruct((rows, width), bf16),
             jax.ShapeDtypeStruct((rows, width), f32),
-        ] + [jax.ShapeDtypeStruct((3,) + item, bf16) for item in items],
+        ] + [jax.ShapeDtypeStruct((3,) + item, bf16) for item in items] + [jax.ShapeDtypeStruct((2,) + item, bf16) for item in items],
         scratch_shapes=small_scratch(length) + [
             pltpu.VMEM((length, length), f32),
             pltpu.VMEM((length, length), f32),
             pltpu.VMEM((length, LANES), f32),
             pltpu.VMEM((length, LANES), f32),
-            pltpu.VMEM((rows, width), f32),
+            pltpu.VMEM((chips,) + left.shape[2:], bf16),
+            pltpu.VMEM((chips,) + left.shape[2:], bf16),
             pltpu.VMEM((turns, length, GROUP), bf16),
             pltpu.VMEM((seqs, length, 3 * LANES), bf16),
-            dma((turns,)), dma((turns,)), dma((seqs,)), dma((seqs,)),
+            pltpu.VMEM((turns, length, GROUP), bf16),
+            pltpu.VMEM((seqs, length, 3 * LANES), bf16),
+            dma((2,)), dma((turns,)), dma((turns,)), dma((seqs,)), dma((seqs,)), dma((2 * count,)), dma((2 * count,)),
         ] + ring_scratch(items, chips),
         compiler_params=pltpu.CompilerParams(collective_id=1, has_side_effects=True, vmem_limit_bytes=FULL),
         name="middle",
-    )(projected, projected, projected, gy, rs, segr, cw, cw, hp, cp, gg, mixed, w_out_full, tokens, gz, w_in_full, *arrays)
+    )(projected, projected, projected, gy, rs, segr, cw, cw, hp, cp, gg, mixed, w_out_full, tokens, gz, w_in_full, left, left2, *arrays)
 
 
 def tail_kernel(chips, groups, used, items, early, px_ref, pr_ref, win_ref, gacc_ref, tok_ref, cot_ref, gain_ref, sg_ref, *refs):
     count, first = len(items), len(early)
     parts, halves, refs = refs[:count], refs[count : count + first], refs[count + first :]
     gt_ref, small_ref, refs = refs[0], refs[1], refs[2:]
-    outs, refs = refs[: first + count], refs[first + count :]
     last_in, last_out, refs = refs[: first + count], refs[first + count : first + 2 * count], refs[first + 2 * count :]
-    (small_in, small_sent, small_recv, small_send, small_sem, last_send, last_recv, half_sem), refs = refs[:8], refs[8:]
-    early_held, refs = refs[:first], refs[first:]
-    (held, ring_in, ring_out, peer_in), sems = split_scratch(refs, count)
+    (small_in, small_sent, small_recv, small_send, small_sem, last_send, last_recv), refs = refs[:7], refs[7:]
+    (held, ring_in, peer_in), sems = split_scratch(refs, count)
     step = pl.program_id(0)
     links = Links(chips)
-    ring = Ring(links, items, 0, parts, held, ring_in, ring_out, peer_in, *sems)
+    ring = Ring(links, items, 0, parts, held, ring_in, peer_in, *sems)
     rounds = len(links.turns)
 
     def swap(k, slot, source):
         at = k * 3 + slot
         links.send(source, lambda: last_in[k].at[slot], lambda: last_send.at[at], lambda: last_recv.at[at], links.peer)
 
-    def settle(k, slot, mine):
-        at = k * 3 + slot
-        width = outs[k].shape[2]
-        links.arrived(last_in[k].at[slot], last_send.at[at], last_recv.at[at])
-        if slot < 2:
-            add_up([mine, last_in[k].at[slot]], outs[k].at[slot], width)
-        else:
-            add_up([mine], outs[k].at[2 + links.plane], width)
-            add_up([last_in[k].at[slot]], outs[k].at[3 - links.plane], width)
-
-    halves_in = lambda: [pltpu.make_async_copy(halves[k], early_held[k], half_sem.at[k]) for k in range(first)]
-
     @pl.when(step == 0)
     def _():
         links.greet(list(links.ways) + links.turns)
         ring.start()
-        for slot in range(3):
-            for k in range(first):
-                swap(k, slot, lambda k=k, slot=slot: halves[k].at[slot])
-        for copy in halves_in():
-            copy.start()
+        for k in range(first):
+            links.send(lambda k=k: halves[k].at[2], lambda k=k: last_in[k].at[0], lambda k=k: last_send.at[3 * k], lambda k=k: last_recv.at[3 * k], links.peer)
         gt_ref[...] = gacc_ref[...] + dot(px_ref[...], win_ref[...], NT)
 
     @pl.when((step > 0) & (step < groups))
     def _():
         gt_ref[...] += dot(px_ref[...], win_ref[...], NT)
 
-    @pl.when(step == 2)
-    def _():
-        for copy in ring.loads():
-            copy.wait()
-        ring.hop(1, 2)
-
-    @pl.when(step == groups - 1)
-    def _():
-        ring.hop(2, 0)
+    every = ring.sequence()
+    inside, later = every[:2], every[2:]
+
+    def run(kind, hop, slot):
+        if kind == "hop":
+            ring.hop(hop, slot)
+            return
+        for k in range(count):
+            ring.land(k, slot, last_out[k].at[slot])
+            swap(first + k, slot, lambda k=k, slot=slot: last_out[k].at[slot])
+
+    for n, entry in enumerate(inside):
+        @pl.when(step == min(groups - 1, 2 + 2 * n))
+        def _(n=n, entry=entry):
+            if n == 0:
+                for copy in ring.loads():
+                    copy.wait()
+            run(*entry)
 
     def small_round(turn):
         links.send(
@@ -982,46 +1033,43 @@
         col = lax.broadcasted_iota(jnp.int32, (win_ref.shape[0], size), 1)
         rest = jnp.where(col < used, win_ref[:, :size].astype(f32), 0.0).astype(bf16)
         rows, width = gt_ref.shape
-        total = jnp.zeros((1, width), f32)
-        for i in range(rows // BLOCK):
+
+        def close(i):
             sl = slice(i * BLOCK, (i + 1) * BLOCK)
             u = tok_ref[sl].astype(f32)
             rstd = lax.rsqrt(jnp.mean(u * u, axis=1, keepdims=True) + epsilon)
             unit = u * rstd
             gn = gt_ref[sl] + dot(pr_ref[sl], rest, NT)
-            total = total + jnp.sum(gn * unit, axis=0, keepdims=True)
+            small_in[7:8, :width] = small_in[7:8, :width] + jnp.sum(gn * unit, axis=0, keepdims=True)
             gu = gn * gain_ref[0:1, :]
             inward = jnp.mean(gu * unit, axis=1, keepdims=True)
             gt_ref[sl] = cot_ref[sl].astype(f32) + rstd * (gu - unit * inward)
+
         small_in[...] = sg_ref[...]
-        small_in[7:8, :width] = total
-        small_round(0)
-        done = 0
-        hops = [(q // 3 + 1, q % 3) for q in range(4, 3 * links.half)]
-        every = max(1, len(hops) // rounds)
-        for n, (hop, slot) in enumerate(hops):
-            ring.hop(hop, slot)
-            if n % every == every - 1 and done < rounds - 1:
-                small_finish(done)
-                done += 1
-                small_round(done)
-        for slot in range(3):
-            for k in range(count):
-                ring.land(k, slot, last_out[k].at[slot])
-                swap(first + k, slot, lambda k=k, slot=slot: last_out[k].at[slot])
+        chunks, done = 0, -1
+        for entry in later:
+            if chunks < rows // BLOCK:
+                close(chunks)
+                chunks += 1
+            run(*entry)
+            if chunks == rows // BLOCK:
+                if done < 0:
+                    small_round(0)
+                    done = 0
+                elif done < rounds - 1:
+                    small_finish(done)
+                    done += 1
+                    small_round(done)
         while done < rounds:
             small_finish(done)
             done += 1
             if done < rounds:
                 small_round(done)
-        for copy in halves_in():
-            copy.wait()
         for slot in range(3):
-            for k in range(first):
-                settle(k, slot, early_held[k].at[slot])
-        for slot in range(3):
-            for k in range(count):
-                settle(first + k, slot, last_out[k].at[slot])
+            for k in range(first + count):
+                at = k * 3 + slot
+                if k >= first or slot == 0:
+                    links.arrived(last_in[k].at[slot], last_send.at[at], last_recv.at[at])
         links.finish()
 
 
@@ -1050,16 +1098,68 @@
             const(8, width),
             const(*sg.shape),
         ] + [any_spec] * (count + first),
-        out_specs=[const(rows, width), const(*sg.shape)] + [const(4, *item) for item in every],
+        out_specs=[const(rows, width), const(*sg.shape)] + [any_spec] * len(every) + [const(3, *item) for item in items],
         out_shape=[jax.ShapeDtypeStruct((rows, width), f32), jax.ShapeDtypeStruct(sg.shape, f32)]
-        + [jax.ShapeDtypeStruct((4,) + item, f32) for item in every],
-        scratch_shapes=[pltpu.VMEM((3,) + item, bf16) for item in every] + [pltpu.VMEM((3,) + item, bf16) for item in items] + [
+        + [jax.ShapeDtypeStruct(((1 if k < first else 3),) + item, bf16) for k, item in enumerate(every + items)],
+        scratch_shapes=[
             pltpu.VMEM(sg.shape, f32), pltpu.VMEM((rounds,) + sg.shape, f32), pltpu.VMEM((rounds,) + sg.shape, f32),
-            dma((rounds,)), dma((rounds,)), dma((3 * (first + count),)), dma((3 * (first + count),)), dma((first,)),
-        ] + [pltpu.VMEM((3,) + item, bf16) for item in early] + ring_scratch(items, chips),
+            dma((rounds,)), dma((rounds,)), dma((3 * (first + count),)), dma((3 * (first + count),)),
+        ] + ring_scratch(items, chips),
         compiler_params=pltpu.CompilerParams(collective_id=2, has_side_effects=True, vmem_limit_bytes=FULL),
         name="tail",
     )(px, pr, w_in_full, gacc, tokens, cot, gain, sg, *arrays, *halves)
+
+
+def finish_kernel(sizes, count, first, where_ref, *refs):
+    taps, share_c, share_g, share_n, heads, columns = sizes
+    mine, theirs, nears, refs = refs[:count], refs[count : 2 * count], refs[2 * count : 2 * count + first], refs[2 * count + first :]
+    small_ref, w_out_ref, w_in_ref, norm_ref, kernel_ref, shift_ref, dt_ref, rate_ref, skip_ref, gate_ref = refs
+    me, plane = where_ref[0], where_ref[1]
+    span = small_ref.shape[1]
+    begin = 0
+    for k in range(count):
+        rows, width = mine[k].shape[1:]
+        store = w_out_ref if k == 0 else w_in_ref
+        left = 0 if k == 0 else begin
+        used = min(width, store.shape[1] - left)
+        for slot in range(2):
+            total = mine[k][slot].astype(f32) + (nears if k < first else theirs)[k][slot].astype(f32)
+            store[slot * rows : (slot + 1) * rows, left : left + used] = total[:, :used]
+        own, other = mine[k][2].astype(f32), theirs[k][0 if k < first else 2].astype(f32)
+        low = jnp.where(plane == 0, own, other)
+        high = jnp.where(plane == 0, other, own)
+        store[2 * rows : 3 * rows, left : left + used] = low[:, :used]
+        store[3 * rows : 4 * rows, left : left + used] = high[:, :used]
+        if k:
+            begin += width
+    small = small_ref[...]
+    conv = pltpu.roll(small, lax.rem(span - me * share_c, span), 1)
+    kernel_ref[...] = conv[:taps, :share_c]
+    shift_ref[...] = conv[taps : taps + 1, :share_c]
+    gate_ref[...] = pltpu.roll(small, lax.rem(span - me * share_g, span), 1)[6:7, :share_g]
+    norm_ref[...] = pltpu.roll(small, lax.rem(span - me * share_n, span), 1)[7:8, :share_n]
+    inner = span - 3 * LANES
+    dt_ref[...] = small[0:1, inner + 2 * LANES : inner + 2 * LANES + heads]
+    rate_ref[...] = small[1:2, inner + 2 * LANES : inner + 2 * LANES + heads]
+    size = inner // heads
+    source = lax.broadcasted_iota(jnp.int32, (inner, LANES), 0) // size
+    pick = (source == lax.broadcasted_iota(jnp.int32, (inner, LANES), 1)).astype(f32)
+    skip_ref[...] = dot(small[:, :inner], pick, precision=highest)[taps + 1 : taps + 2, :heads]
+
+
+def finish(me, plane, mine, theirs, nears, small, taps, share_c, share_g, share_n, heads, columns):
+    count = len(mine)
+    out = lambda *shape: jax.ShapeDtypeStruct(shape, f32)
+    spec = pl.BlockSpec(memory_space=pltpu.VMEM)
+    shapes = [out(4 * mine[0].shape[1], mine[0].shape[2]), out(4 * mine[1].shape[1], columns), out(1, share_n), out(taps, share_c),
+              out(1, share_c), out(1, heads), out(1, heads), out(1, heads), out(1, share_g)]
+    return pl.pallas_call(
+        functools.partial(finish_kernel, (taps, share_c, share_g, share_n, heads, columns), count, len(nears)),
+        in_specs=[pl.BlockSpec(memory_space=pltpu.SMEM)] + [spec] * (2 * count + len(nears) + 1),
+        out_specs=[spec] * len(shapes),
+        out_shape=shapes,
+        name="finish",
+    )(jnp.stack([me, plane]).astype(jnp.int32), *mine, *theirs, *nears, small)
 
 
 def parts_kernel(core_ref, a_ref, a2_ref, b_ref, b2_ref, o_ref):
@@ -1142,42 +1242,39 @@
     normed = (residual * rstd * gain_f).astype(bf16)
     grad_rows = cotangent.reshape(rows, width)
     grad_rows2 = partner(grad_rows)
-    normed_t = normed.T.reshape(chips, 2, -1, rows)
+    normed, normed_t = lax.optimization_barrier((normed, normed.T.reshape(chips, 2, -1, rows)))
     normed_t2 = partner(normed_t)
     projected = dot(normed, w_in_full)
     gm = dot(grad_rows, w_out_full, NT)
     tables = mixer_tables(segments, kernel_full, shift_full, dt_bias, a_log, d_skip, gate_full)
+    segr, cw, hp, cp = tables
+    hp, normed_t2, grad_rows2 = lax.optimization_barrier((hp, normed_t2, grad_rows2))
+    tables = segr, cw, hp, cp
     mixed, mixed_t, gz, gy, rs, gg = mixer_forward(projected, gm, *tables, heads, state)
     mixed_t = mixed_t.reshape(chips, 2, -1, rows)
     gz2, mixed_t2 = partner(gz), partner(mixed_t)
     quarters = lambda part: part.reshape(chips, QUARTERS, -1, part.shape[1])
     part_out = quarters(grad_parts(core, mixed_t, mixed_t2, grad_rows, grad_rows2, "grad_out"))
     part_z = quarters(grad_parts(core, normed_t, normed_t2, gz, gz2, "grad_z"))
-    px, pr, px2, pr2, sg, block_out, gacc, half_out, half_z = middle(
-        projected, gy, rs, *tables, gg, mixed, w_out_full, flat_tokens, gz, w_in_full, [part_out, part_z], heads, state, devices)
-    part_x = quarters(grad_parts(core, normed_t, normed_t2, px, px2, "grad_x"))
-    part_r = quarters(grad_parts(core, normed_t, normed_t2, pr, pr2, "grad_r"))
+    px, pr, part_x, part_r, sg, block_out, gacc, half_out, half_z, *nears = middle(
+        projected, gy, rs, *tables, gg, mixed, w_out_full, flat_tokens, gz, w_in_full, normed_t, normed_t2, [part_out, part_z], heads, state, devices)
     gain8 = jnp.broadcast_to(gain_f[None], (8, width))
-    grad_tokens, small, own_out, own_z, own_x, own_r = tail(
-        px, pr, w_in_full, gacc, flat_tokens, grad_rows, gain8, sg, [part_x, part_r], [half_out, half_z], 2 * state + heads, devices)
-
-    grad_w_in = jnp.concatenate([o.reshape(-1, o.shape[2]) for o in (own_z, own_x, own_r)], axis=1)[:, :proj_width]
-    conv = lax.dynamic_slice(small, (0, me * share_c), (taps + 1, share_c))
-    gate = lax.dynamic_slice(small, (6, me * share_g), (1, share_g))
-    norm = lax.dynamic_slice(small, (7, me * share_n), (1, share_n))
-    skip = small[taps + 1, :inner].reshape(heads, inner // heads).sum(1)
+    grad_tokens, small, *theirs, half_x, half_r = tail(
+        px, pr, w_in_full, gacc, flat_tokens, grad_rows, gain8, sg, [quarters(part_x), quarters(part_r)], [half_out, half_z], 2 * state + heads, devices)
+    grad_w_out, grad_w_in, norm, kernel, shift, offset, rate, skip, gate = finish(
+        me, lax.axis_index("dp"), [half_out, half_z, half_x, half_r], theirs, nears, small, taps, share_c, share_g, share_n, heads, proj_width)
     return (
         block_out.reshape(seqs, length, width),
         grad_tokens.reshape(seqs, length, width),
         norm[0],
         grad_w_in,
-        conv[:taps],
-        conv[taps],
-        small[0, conv_width : conv_width + heads],
-        small[1, conv_width : conv_width + heads],
-        skip,
+        kernel,
+        shift[0],
+        offset[0],
+        rate[0],
+        skip[0],
         gate[0],
-        own_out.reshape(-1, width),
+        grad_w_out,
     )
 
 

time: 421 us -> 388 us (0.922)
  Pallas kernels: 355 us -> 335 us
  local copies, waits for them, and re-layouts: 22.5 us -> 14.8 us
    pallas_call x4 -> x2, Pallas kernels: 31.9 us -> 18.7 us  [grad_parts(): pl.pallas_call(parts_kernel, grid_spec=pltpu.PrefetchScalarGridSpec(num_s...]
    pallas_call x1, Pallas kernels: 71.7 us -> 65.1 us  [tail(): pl.pallas_call(functools.partial(tail_kernel, chips, groups, used, items,...]
    pallas_call x0 -> x1, Pallas kernels: none -> 4.81 us  [finish(): pl.pallas_call(functools.partial(finish_kernel, (taps, share_c, share_g,...]
  transfers between devices with their start and end apart: 4 -> 4, of which waited for: 1 -> 1; matrix products, arithmetic and copies ran while one was open for 1% -> 7% of each run, Pallas kernels for 2% -> 3%
where the time goes in v4:
time: 388 us; the launch traced here: 386 us
  Pallas kernels  335 us (86%)
  matrix products  26.1 us (7%)
  local copies, waits for them, and re-layouts  14.8 us (4%)
  waiting for transfers between devices  5 us (1%)
    pallas_call x1, Pallas kernels, gather(): pl.pallas_call(functools.partial(gather_kernel, chips, count), in_specs=[...  121 us
    pallas_call x1, Pallas kernels, middle(): pl.pallas_call(functools.partial(middle_kernel, heads, chips, seqs, group...  87.7 us
    pallas_call x1, Pallas kernels, tail(): pl.pallas_call(functools.partial(tail_kernel, chips, groups, used, items,...  65.1 us
    pallas_call x1, Pallas kernels, mixer_forward(): pl.pallas_call(kernel, grid=(seqs, 2, groups), in_specs=[pl.BlockSpec((le...  37.8 us
    dot_general x2, matrix products, dot(): lax.dot_general(a, b, dims, precision=precision, preferred_element_type=f32)  26.1 us
    pallas_call x2, Pallas kernels, grad_parts(): pl.pallas_call(parts_kernel, grid_spec=pltpu.PrefetchScalarGridSpec(num_s...  18.7 us
    unnamed x36, local copies, waits for them, and re-layouts  8.24 us
  transfers between devices with their start and end apart: 4, of which 1 were waited for; matrix products, arithmetic and copies ran while one was open for 7% of the time, Pallas kernels for 3%

profile of v4, /device:TPU:0, one launch (start us, length us, event | category | flops | bytes accessed | tf_op | source)
XLA Modules:
  0.0 386.5 jit_solution(6560351381810971655)
XLA Ops:
  0.7 0.9 reshape.125
  1.5 2.1 concatenate.12
  3.6 0.6 pad_bitcast_fusion.refs_2_
  4.2 121.3 %gather_weights.1 = (bf16[16,3,32,6448]{3,2,1,0:T(8,128)(2,1)}, bf16[16,3,64,1536]{3,2,1,0:T(8,128)(2,1)}, bf16[16,16,128]{2,1,0:T(8,128)(2,1)}) custom-call(bf16[3,32,6448]{2,1,0:T(8,128)(2,1)} %bitcast.57, bf16[3,64,1536]{2,1,0:T(8,128)(2,1)} %bitcast.58, bf16[16,128]{1,0:T(8,128)(2,1)} %pad_bitcast_fusion.refs_2_), custom_call_target="tpu_custom_call" | custom-call | tf_op jit(solution)/shard_map/gather_weights/pallas_call | solution.py:555
  125.6 0.9 copy.49
  126.5 1.8 multiply_reduce_fusion
  128.8 1.8 copy.34
  130.6 0.5 collective-permute-start
  132.0 17.7 %fusion.z_ref.x_ref.bc_ref.dtr_ref = f32[512,6448]{1,0:T(8,128)} fusion(bf16[512,1536]{1,0:T(8,128)(2,1)S(1)} %multiply_convert_fusion, bf16[1536,6448]{1,0:T(8,128)(2,1)} %bitcast.42), kind=kOutput, calls=%fused_computation.15 | convolution fusion | flops 10141827072 | bytes 34586624 | tf_op jit(solution)/shard_map/dot_general | solution.py:22
  149.9 8.4 %convolution_bitcast_fusion.gm_ref = f32[512,3072]{1,0:T(8,128)} fusion(bf16[3072,1536]{1,0:T(8,128)(2,1)S(1)} %bitcast.50, bf16[512,1536]{1,0:T(8,128)(2,1)} %bitcast.8.b_ref.cot_ref), kind=kOutput, calls=%fused_computation | convolution fusion | flops 4831838208 | bytes 17301504 | tf_op jit(solution)/shard_map/dot_general | solution.py:22
  158.3 37.8 %mixer_forward.1 = (bf16[512,3072]{1,0:T(8,128)(2,1)S(1)}, bf16[3072,512]{1,0:T(8,128)(2,1)}, bf16[512,3072]{1,0:T(8,128)(2,1)}, f32[512,3072]{1,0:T(8,128)}, f3...) custom-call(f32[512,6448]{1,0:T(8,128)} %fusion.z_ref.x_ref.bc_ref.dtr_ref, f32[512,6448]{1,0:T(8,128)} %fusion.z_ref.x_ref.bc_ref.dtr_ref, ...), custom_call_target="tpu_custom_call" | custom-call | flops 10000000000 | bytes 45000000 | tf_op jit(solution)/shard_map/mixer_forward/pallas_call | solution.py:339
  196.1 1.7 copy-done
  197.8 0.7 copy-done.3
  198.5 0.6 copy-done.5
  199.6 0.6 pad_add_fusion.where_ref
  200.3 5.0 %collective-permute-done.3.b2_ref = bf16[512,3072]{1,0:T(8,128)(2,1)} collective-permute-done((bf16[512,3072]{1,0:T(8,128)(2,1)}, bf16[512,3072]{1,0:T(8,128)(2,1)}, u32[]{:S(2)}, u32[]{:S(2)}) %collective-permute-start.3) | collective-permute-done | bytes 3145760 | tf_op jit(solution)/shard_map/ppermute | solution.py:1223
  205.3 9.8 %grad_z.1 = bf16[768,3072]{1,0:T(8,128)(2,1)} custom-call(s32[1]{0:T(128)} %bitcast.12.core_ref, bf16[8,2,96,512]{3,2,1,0:T(8,128)(2,1)} %bitcast.5.a_ref.nt_ref, bf16[8,2,96,512]{3,2,1,0:T(8,128)(2,1)} %collective-permute-done.a2_ref.nt2_ref, bf16[512,3072]{1,0:T(8,128)(2,1)} %get-tuple-element.63.b_ref.gz_ref, bf16[512,3072]{1,0:T(8,128)(2,1)} %collective-permute-done.3.b2_ref), custom_call_target="tpu_custom_call" | custom-call | flops 4831838208 | bytes 12582912 | tf_op jit(solution)/shard_map/grad_z/pallas_call | solution.py:1181
  215.0 8.9 %grad_out.1 = bf16[1536,1536]{1,0:T(8,128)(2,1)} custom-call(s32[1]{0:T(128)} %bitcast.12.core_ref, bf16[8,2,192,512]{3,2,1,0:T(8,128)(2,1)} %bitcast.69, bf16[8,2,192,512]{3,2,1,0:T(8,128)(2,1)} %collective-permute-done.2.a2_ref, bf16[512,1536]{1,0:T(8,128)(2,1)} %bitcast.8.b_ref.cot_ref, bf16[512,1536]{1,0:T(8,128)(2,1)} %collective-permute-done.1.b2_ref), custom_call_target="tpu_custom_call" | custom-call | flops 4831838208 | bytes 11010048 | tf_op jit(solution)/shard_map/grad_out/pallas_call | solution.py:1181
  223.9 87.7 %middle.1 = (bf16[512,3072]{1,0:T(8,128)(2,1)}, bf16[512,384]{1,0:T(8,128)(2,1)}, bf16[768,3072]{1,0:T(8,128)(2,1)}, bf16[768,384]{1,0:T(8,128)(2,1)}, f32[8,345...) custom-call(f32[512,6448]{1,0:T(8,128)} %fusion.z_ref.x_ref.bc_ref.d, ...), custom_call_target="tpu_custom_call" | custom-call | tf_op jit(solution)/shard_map/middle/pallas_call | solution.py:915
  311.7 0.6 broadcast_in_dim.23.gain_ref
  312.3 65.1 %tail.1 = (f32[512,1536]{1,0:T(8,128)}, f32[8,3456]{1,0:T(8,128)}, bf16[1,48,1536]{2,1,0:T(8,128)(2,1)}, bf16[1,24,3072]{2,1,0:T(8,128)(2,1)}, bf16[3,24,3072]{2...) custom-call(bf16[512,3072]{1,0:T(8,128)(2,1)} %get-tuple-element.68.px_re, ...), custom_call_target="tpu_custom_call" | custom-call | tf_op jit(solution)/shard_map/tail/pallas_call | solution.py:1088
  377.4 4.8 %finish.1 = (f32[192,1536]{1,0:T(8,128)}, f32[96,6448]{1,0:T(8,128)}, f32[1,96]{1,0:T(1,128)}, f32[4,208]{1,0:T(4,128)}, f32[1,208]{1,0:T(1,128)}, /*index=5*/f3...) custom-call(s32[2]{0:T(128)} %pad_add_fusion.where_ref, ...), custom_call_target="tpu_custom_call" | custom-call | tf_op jit(solution)/shard_map/finish/pallas_call | solution.py:1156
  382.2 2.7 copy.52
  384.8 1.7 copy.53
  (59 shorter events, 2.0 us)
Async XLA Ops:
  0.6 127.7 %copy-start.7 = (bf16[2,256,1536]{2,1,0:T(8,128)(2,1)S(1)}, bf16[2,256,1536]{2,1,0:T(8,128)(2,1)}, u32[]{:S(2)}) copy-start(bf16[2,256,1536]{2,1,0:T(8,128)(2,1)} %param.12) | copy-start | bytes 4718596
  128.4 3.4 copy-start.10
  128.4 3.6 copy-start.9
  128.4 3.6 copy-start.11
  128.4 3.6 copy-start.12
  130.6 27.7 %collective-permute-start = (bf16[8,2,96,512]{3,2,1,0:T(8,128)(2,1)}, bf16[8,2,96,512]{3,2,1,0:T(8,128)(2,1)}, u32[]{:S(2)}, u32[]{:S(2)}) collective-permute-start(bf16[8,2,96,512]{3,2,1,0:T(8,128)(2,1)} %bitcast.5.a_ref.nt_ref), channel_id=1, source_target_pairs={{0,2},{2,0},{4,6},{6,4},{8,10},{10,8},{12,14},{14,12},{16,18},{18,... | collective-permute-start | bytes 4718600 | tf_op jit(solution)/shard_map/ppermute | solution.py:1223
  131.1 27.1 %collective-permute-start.1 = (bf16[512,1536]{1,0:T(8,128)(2,1)}, bf16[512,1536]{1,0:T(8,128)(2,1)}, u32[]{:S(2)}, u32[]{:S(2)}) collective-permute-start(bf16[512,1536]{1,0:T(8,128)(2,1)} %bitcast.8.b_ref.cot_ref), channel_id=1, source_target_pairs={{0,2},{2,0},{4,6},{6,4},{8,10},{10,8},{12,14},{14,12},{16,18},{18,... | collective-permute-start | bytes 4718600 | tf_op jit(solution)/shard_map/ppermute | solution.py:1223
  131.1 18.7 %slice-start = ((s8[9437184]{0:T(1024)(128)(4,1)}), s8[1048576]{0:T(1024)(128)(4,1)S(1)}, s32[]{:S(2)}) async-start(s8[9437184]{0:T(1024)(128)(4,1)} %bitcast.48), calls=%async_computation | async-start | bytes 2097152
  132.0 26.3 %copy-start.6 = (f32[8,128]{1,0:T(8,128)}, f32[8,128]{1,0:T(8,128)S(1)}, u32[]{:S(2)}) copy-start(f32[8,128]{1,0:T(8,128)S(1)} %select_maximum_fusion.hp_ref) | copy-start | bytes 12292
  132.0 17.8 %slice-start.1 = ((s8[9437184]{0:T(1024)(128)(4,1)}), s8[4194304]{0:T(1024)(128)(4,1)S(1)}, s32[]{:S(2)}) async-start(s8[9437184]{0:T(1024)(128)(4,1)} %bitcast.48), calls=%async_computation.1 | async-start | bytes 8388608
  132.0 17.8 %slice-start.2 = ((s8[9437184]{0:T(1024)(128)(4,1)}), s8[4194304]{0:T(1024)(128)(4,1)S(1)}, s32[]{:S(2)}) async-start(s8[9437184]{0:T(1024)(128)(4,1)} %bitcast.48), calls=%async_computation.2 | async-start | bytes 8388608
  149.8 8.5 %copy-start.1 = (f32[8,3328]{1,0:T(8,128)}, f32[8,3328]{1,0:T(8,128)S(1)}, u32[]{:S(2)}) copy-start(f32[8,3328]{1,0:T(8,128)S(1)} %pad_maximum_fusion.cwx_ref.cwbc_ref) | copy-start | bytes 319492
  149.8 8.5 %copy-start.2 = (f32[8,3072]{1,0:T(8,128)}, f32[8,3072]{1,0:T(8,128)S(1)}, u32[]{:S(2)}) copy-start(f32[8,3072]{1,0:T(8,128)S(1)} %pad_maximum_fusion.1.cp_ref) | copy-start | bytes 294916
  158.3 37.8 %copy-start.4 = (f32[2,8,256]{2,1,0:T(8,128)}, f32[2,8,256]{2,1,0:T(8,128)S(1)}, u32[]{:S(2)}) copy-start(f32[2,8,256]{2,1,0:T(8,128)S(1)} %broadcast_in_dim.16.segr_ref) | copy-start | bytes 49156
  196.1 1.7 copy-start
  197.8 0.7 copy-start.3
  198.5 0.6 copy-start.5
  199.1 6.1 %collective-permute-start.3 = (bf16[512,3072]{1,0:T(8,128)(2,1)}, bf16[512,3072]{1,0:T(8,128)(2,1)}, u32[]{:S(2)}, u32[]{:S(2)}) collective-permute-start(bf16[512,3072]{1,0:T(8,128)(2,1)} %get-tuple-element.63.b_ref.gz_ref), channel_id=1, source_target_pairs={{0,2},{2,0},{4,6},{6,4},{8,10},{10,8},{12,14},{14,12},{16,18},{18,... | collective-permute-start | bytes 9437192 | tf_op jit(solution)/shard_map/ppermute | solution.py:1223
  199.6 15.4 %collective-permute-start.2 = (bf16[8,2,192,512]{3,2,1,0:T(8,128)(2,1)}, bf16[8,2,192,512]{3,2,1,0:T(8,128)(2,1)}, u32[]{:S(2)}, u32[]{:S(2)}) collective-permute-start(bf16[8,2,192,512]{3,2,1,0:T(8,128)(2,1)} %bitcast.68), channel_id=1, source_target_pairs={{0,2},{2,0},{4,6},{6,4},{8,10},{10,8},{12,14},{14,12},{16,18},{18,... | collective-permute-start | bytes 9437192 | tf_op jit(solution)/shard_map/ppermute | solution.py:1223
  377.4 7.5 %copy-start.8 = (f32[512,1536]{1,0:T(8,128)S(1)}, f32[512,1536]{1,0:T(8,128)}, u32[]{:S(2)}) copy-start(f32[512,1536]{1,0:T(8,128)} %get-tuple-element.76) | copy-start | bytes 9437188

commit v5 on v4

--- a/solution.py
+++ b/solution.py
@@ -375,7 +375,7 @@
             pltpu.VMEM((2, length, LANES), f32),
             pltpu.VMEM((length, LANES), f32),
         ],
-        compiler_params=pltpu.CompilerParams(vmem_limit_bytes=48 << 20),
+        compiler_params=pltpu.CompilerParams(vmem_limit_bytes=62 << 20),
         cost_estimate=pl.CostEstimate(flops=10**10, bytes_accessed=45 * 10**6, transcendentals=10**7),
         name="mixer_forward",
     )(projected, projected, projected, projected, gm, segr, cw, cw, hp, cp)
@@ -461,7 +461,7 @@
         return ins[k].at[piece]
 
     def slots(k):
-        return (0,) if whole[k] else (0, 1)
+        return (0,) if whole[k] else (1, 0)
 
     pending = []
 
@@ -998,7 +998,7 @@
         gt_ref[...] += dot(px_ref[...], win_ref[...], NT)
 
     every = ring.sequence()
-    inside, later = every[:2], every[2:]
+    inside, later = every[:3], every[3:]
 
     def run(kind, hop, slot):
         if kind == "hop":
@@ -1009,7 +1009,7 @@
             swap(first + k, slot, lambda k=k, slot=slot: last_out[k].at[slot])
 
     for n, entry in enumerate(inside):
-        @pl.when(step == min(groups - 1, 2 + 2 * n))
+        @pl.when(step == min(groups - 1, 1 + 2 * n))
         def _(n=n, entry=entry):
             if n == 0:
                 for copy in ring.loads():
@@ -1047,7 +1047,9 @@
 
         small_in[...] = sg_ref[...]
         chunks, done = 0, -1
+        sent = []
         for entry in later:
+            sent.append(entry)
             if chunks < rows // BLOCK:
                 close(chunks)
                 chunks += 1
@@ -1056,7 +1058,7 @@
                 if done < 0:
                     small_round(0)
                     done = 0
-                elif done < rounds - 1:
+                elif done < rounds - 1 and len(sent) % 2:
                     small_finish(done)
                     done += 1
                     small_round(done)
@@ -1197,15 +1199,6 @@
     )(jnp.full((1,), core, jnp.int32), left, left2, right, right2)
 
 
-def small_rows(size):
-    return 16 * (-(-size // (16 * LANES)))
-
-
-def flat_pack(parts, rows):
-    flat = jnp.concatenate([p.reshape(-1) for p in parts])
-    return jnp.pad(flat, (0, rows * LANES - flat.shape[0])).reshape(rows, LANES)
-
-
 def local(devices, tokens, segments, norm_gain, w_in, conv_weight, conv_bias, dt_bias, a_log, d_skip, gate_gain, w_out, cotangent):
     seqs, length, width = tokens.shape
     rows = seqs * length
@@ -1222,18 +1215,18 @@
     swap = [(i, i + 1 - 2 * (i % 2)) for i in range(devices)]
     partner = lambda value: lax.ppermute(value, "fsdp", swap)
 
-    size = share_n + share_g + (taps + 1) * share_c
-    pack = flat_pack([norm_gain, gate_gain, conv_weight, conv_bias], small_rows(size))
+    span = LANES * (-(-max(share_n, share_g, share_c) // LANES))
+    line = lambda value: pad_lanes(value.reshape(-1, value.shape[-1]), span)
+    pack = jnp.concatenate([line(conv_weight), line(conv_bias), line(gate_gain), line(norm_gain)])
+    pack = jnp.pad(pack, ((0, -pack.shape[0] % 8), (0, 0)))
     win_all, wout_all, pack_all = gather(
         [w_in.reshape(PIECES, -1, proj_width), w_out.reshape(PIECES, -1, width), pack], devices)
     w_in_full = win_all.reshape(width, proj_width)
     w_out_full = wout_all.reshape(inner, width)
-    pack_all = pack_all.reshape(devices, -1)
-    cuts = [share_n, share_n + share_g, share_n + share_g + taps * share_c, size]
-    gain_full = pack_all[:, : cuts[0]].reshape(width)
-    gate_full = pack_all[:, cuts[0] : cuts[1]].reshape(inner)
-    kernel_full = pack_all[:, cuts[1] : cuts[2]].reshape(devices, taps, share_c).transpose(1, 0, 2).reshape(taps, conv_width)
-    shift_full = pack_all[:, cuts[2] : cuts[3]].reshape(conv_width)
+    kernel_full = pack_all[:, :taps, :share_c].transpose(1, 0, 2).reshape(taps, conv_width)
+    shift_full = pack_all[:, taps, :share_c].reshape(conv_width)
+    gate_full = pack_all[:, taps + 1, :share_g].reshape(inner)
+    gain_full = pack_all[:, taps + 2, :share_n].reshape(width)
 
     flat_tokens = tokens.reshape(rows, width)
     residual = flat_tokens.astype(f32)

time: 388 us -> 378 us (0.974)
  Pallas kernels: 335 us -> 329 us
  local copies, waits for them, and re-layouts: 14.8 us -> 9.93 us
    pallas_call x1, Pallas kernels: 121 us -> 117 us  [gather(): pl.pallas_call(functools.partial(gather_kernel, chips, count), in_specs=[...]
    unnamed x36 -> x25, local copies, waits for them, and re-layouts: 8.24 us -> 4.38 us
where the time goes in v5:
time: 378 us; the launch traced here: 377 us
  Pallas kernels  329 us (87%)
  matrix products  24.7 us (7%)
  local copies, waits for them, and re-layouts  9.93 us (3%)
  other arithmetic  6.44 us (2%)
  waiting for transfers between devices  4.89 us (1%)
    pallas_call x1, Pallas kernels, gather(): pl.pallas_call(functools.partial(gather_kernel, chips, count), in_specs=[...  117 us
    pallas_call x1, Pallas kernels, middle(): pl.pallas_call(functools.partial(middle_kernel, heads, chips, seqs, group...  87.7 us
    pallas_call x1, Pallas kernels, tail(): pl.pallas_call(functools.partial(tail_kernel, chips, groups, used, items,...  61.2 us
    pallas_call x1, Pallas kernels, mixer_forward(): pl.pallas_call(kernel, grid=(seqs, 2, groups), in_specs=[pl.BlockSpec((le...  38.9 us
    dot_general x2, matrix products, dot(): lax.dot_general(a, b, dims, precision=precision, preferred_element_type=f32)  24.7 us
    pallas_call x2, Pallas kernels, grad_parts(): pl.pallas_call(parts_kernel, grid_spec=pltpu.PrefetchScalarGridSpec(num_s...  18.7 us
  transfers between devices with their start and end apart: 4, of which 1 were waited for; matrix products, arithmetic and copies ran while one was open for 7% of the time, Pallas kernels for 3%

profile of v5, /device:TPU:0, one launch (start us, length us, event | category | flops | bytes accessed | tf_op | source)
XLA Modules:
  0.0 376.7 jit_solution(3190261559864932852)
XLA Ops:
  0.7 0.8 reshape.119
  1.4 0.7 reshape.120
  2.1 0.7 fusion.7
  3.4 117.3 %gather_weights.1 = (bf16[16,3,32,6448]{3,2,1,0:T(8,128)(2,1)}, bf16[16,3,64,1536]{3,2,1,0:T(8,128)(2,1)}, bf16[16,8,256]{2,1,0:T(8,128)(2,1)}) custom-call(bf16[3,32,6448]{2,1,0:T(8,128)(2,1)} %bitcast.60, bf16[3,64,1536]{2,1,0:T(8,128)(2,1)} %bitcast.61, bf16[8,256]{1,0:T(8,128)(2,1)} %pad.28.refs_2_), custom_call_target="tpu_custom_call" | custom-call | tf_op jit(solution)/shard_map/gather_weights/pallas_call | solution.py:555
  120.8 0.8 convert_reduce_fusion.2
  121.6 1.8 multiply_reduce_fusion
  123.9 1.8 copy.35
  126.9 0.6 select_maximum_fusion.hp_ref
  127.5 17.6 %fusion.9.z_ref.x_ref.bc_ref.dtr_ref = f32[512,6448]{1,0:T(8,128)} fusion(bf16[512,1536]{1,0:T(8,128)(2,1)S(1)} %multiply_convert_fusion, bf16[1536,6448]{1,0:T(8,128)(2,1)} %bitcast.38), kind=kOutput, calls=%fused_computation.28 | convolution fusion | flops 10141827072 | bytes 34586624 | tf_op jit(solution)/shard_map/dot_general | solution.py:22
  145.1 0.7 pad_maximum_fusion.cwx_ref.cwbc_ref
  145.8 0.7 pad_maximum_fusion.1.cp_ref
  146.5 7.1 %convolution_bitcast_fusion.gm_ref = f32[512,3072]{1,0:T(8,128)} fusion(bf16[3072,1536]{1,0:T(8,128)(2,1)S(1)} %bitcast.46, bf16[512,1536]{1,0:T(8,128)(2,1)S(1)} %bitcast.58), kind=kOutput, calls=%fused_computation | convolution fusion | flops 4831838208 | bytes 17301504 | tf_op jit(solution)/shard_map/dot_general | solution.py:22
  153.6 0.6 broadcast_in_dim.16.segr_ref
  154.2 38.9 %mixer_forward.1 = (bf16[512,3072]{1,0:T(8,128)(2,1)}, bf16[3072,512]{1,0:T(8,128)(2,1)}, bf16[512,3072]{1,0:T(8,128)(2,1)}, f32[512,3072]{1,0:T(8,128)}, f32[2,256,128]{2,1,0:T(8,128)}, /*index=5*/f32[8,3072]{1,0:T(8,128)}) custom-call(f32[512,6448]{1,0:T(8,128)} %fusion.9.z_ref.x_ref.bc_ref.dtr_ref, f32[512,6448]{1,0:T(8,128)} %fusion.9.z_ref.x_ref.bc_ref.dtr_ref, ...), custom_call_target="tpu_custom_call" | custom-call | flops 10000000000 | bytes 45000000 | tf_op jit(solution)/shard_map/mixer_forward/pallas_call | solution.py:339
  193.7 0.7 pad_add_fusion.where_ref
  194.4 4.9 %collective-permute-done.3.b2_ref = bf16[512,3072]{1,0:T(8,128)(2,1)} collective-permute-done((bf16[512,3072]{1,0:T(8,128)(2,1)}, bf16[512,3072]{1,0:T(8,128)(2,1)}, u32[]{:S(2)}, u32[]{:S(2)}) %collective-permute-start.3) | collective-permute-done | bytes 3145760 | tf_op jit(solution)/shard_map/ppermute | solution.py:1216
  199.3 9.8 %grad_z.1 = bf16[768,3072]{1,0:T(8,128)(2,1)} custom-call(s32[1]{0:T(128)} %bitcast.12.core_ref, bf16[8,2,96,512]{3,2,1,0:T(8,128)(2,1)} %bitcast.49, bf16[8,2,96,512]{3,2,1,0:T(8,128)(2,1)} %collective-permute-done.a2_ref.nt2_ref, bf16[512,3072]{1,0:T(8,128)(2,1)} %get-tuple-element.63.b_ref.gz_ref, bf16[512,3072]{1,0:T(8,128)(2,1)} %collective-permute-done.3.b2_ref), custom_call_target="tpu_custom_call" | custom-call | flops 4831838208 | bytes 12582912 | tf_op jit(solution)/shard_map/grad_z/pallas_call | solution.py:1183
  209.1 8.9 %grad_out.1 = bf16[1536,1536]{1,0:T(8,128)(2,1)} custom-call(s32[1]{0:T(128)} %bitcast.12.core_ref, bf16[8,2,192,512]{3,2,1,0:T(8,128)(2,1)} %bitcast.67, bf16[8,2,192,512]{3,2,1,0:T(8,128)(2,1)} %collective-permute-done.2.a2_ref, bf16[512,1536]{1,0:T(8,128)(2,1)} %bitcast.56, bf16[512,1536]{1,0:T(8,128)(2,1)} %collective-permute-done.1.b2_ref), custom_call_target="tpu_custom_call" | custom-call | flops 4831838208 | bytes 11010048 | tf_op jit(solution)/shard_map/grad_out/pallas_call | solution.py:1183
  218.0 87.7 %middle.1 = (bf16[512,3072]{1,0:T(8,128)(2,1)}, bf16[512,384]{1,0:T(8,128)(2,1)}, bf16[768,3072]{1,0:T(8,128)(2,1)}, bf16[768,384]{1,0:T(8,128)(2,1)}, f32[8,345...) custom-call(f32[512,6448]{1,0:T(8,128)} %fusion.9.z_ref.x_ref.bc_ref, ...), custom_call_target="tpu_custom_call" | custom-call | tf_op jit(solution)/shard_map/middle/pallas_call | solution.py:915
  305.7 0.6 broadcast_in_dim.23.gain_ref
  306.3 61.2 %tail.1 = (f32[512,1536]{1,0:T(8,128)}, f32[8,3456]{1,0:T(8,128)}, bf16[1,48,1536]{2,1,0:T(8,128)(2,1)}, bf16[1,24,3072]{2,1,0:T(8,128)(2,1)}, bf16[3,24,3072]{2...) custom-call(bf16[512,3072]{1,0:T(8,128)(2,1)} %get-tuple-element.68.px_re, ...), custom_call_target="tpu_custom_call" | custom-call | tf_op jit(solution)/shard_map/tail/pallas_call | solution.py:1090
  367.6 4.8 %finish.1 = (f32[192,1536]{1,0:T(8,128)}, f32[96,6448]{1,0:T(8,128)}, f32[1,96]{1,0:T(1,128)}, f32[4,208]{1,0:T(4,128)}, f32[1,208]{1,0:T(1,128)}, /*index=5*/f3...) custom-call(s32[2]{0:T(128)} %pad_add_fusion.where_ref, ...), custom_call_target="tpu_custom_call" | custom-call | tf_op jit(solution)/shard_map/finish/pallas_call | solution.py:1158
  372.4 2.7 copy.50
  375.1 1.7 copy.51
  (48 shorter events, 2.9 us)
Async XLA Ops:
  0.6 122.8 %copy-start = (bf16[2,256,1536]{2,1,0:T(8,128)(2,1)S(1)}, bf16[2,256,1536]{2,1,0:T(8,128)(2,1)}, u32[]{:S(2)}) copy-start(bf16[2,256,1536]{2,1,0:T(8,128)(2,1)} %param.12) | copy-start | bytes 4718596
  123.4 2.8 copy-start.3
  123.4 3.2 copy-start.5
  123.5 3.4 copy-start.4
  123.5 3.4 copy-start.6
  123.5 3.4 copy-start.7
  123.9 22.5 %slice-start = ((s8[9437184]{0:T(1024)(128)(4,1)}), s8[1048576]{0:T(1024)(128)(4,1)S(1)}, s32[]{:S(2)}) async-start(s8[9437184]{0:T(1024)(128)(4,1)} %bitcast.44), calls=%async_computation | async-start | bytes 2097152
  125.7 27.9 %collective-permute-start = (bf16[8,2,96,512]{3,2,1,0:T(8,128)(2,1)}, bf16[8,2,96,512]{3,2,1,0:T(8,128)(2,1)}, u32[]{:S(2)}, u32[]{:S(2)}) collective-permute-start(bf16[8,2,96,512]{3,2,1,0:T(8,128)(2,1)} %bitcast.48), channel_id=1, source_target_pairs={{0,2},{2,0},{4,6},{6,4},{8,10},{10,8},{12,14},{14,12},{16,18},{18,... | collective-permute-start | bytes 4718600 | tf_op jit(solution)/shard_map/ppermute | solution.py:1216
  126.2 27.3 %collective-permute-start.1 = (bf16[512,1536]{1,0:T(8,128)(2,1)}, bf16[512,1536]{1,0:T(8,128)(2,1)}, u32[]{:S(2)}, u32[]{:S(2)}) collective-permute-start(bf16[512,1536]{1,0:T(8,128)(2,1)} %bitcast.55), channel_id=1, source_target_pairs={{0,2},{2,0},{4,6},{6,4},{8,10},{10,8},{12,14},{14,12},{16,18},{18,... | collective-permute-start | bytes 4718600 | tf_op jit(solution)/shard_map/ppermute | solution.py:1216
  127.5 19.0 %slice-start.1 = ((s8[9437184]{0:T(1024)(128)(4,1)}), s8[4194304]{0:T(1024)(128)(4,1)S(1)}, s32[]{:S(2)}) async-start(s8[9437184]{0:T(1024)(128)(4,1)} %bitcast.44), calls=%async_computation.1 | async-start | bytes 8388608
  127.5 19.0 %slice-start.2 = ((s8[9437184]{0:T(1024)(128)(4,1)}), s8[4194304]{0:T(1024)(128)(4,1)S(1)}, s32[]{:S(2)}) async-start(s8[9437184]{0:T(1024)(128)(4,1)} %bitcast.44), calls=%async_computation.2 | async-start | bytes 8388608
  127.5 19.0 %copy-start.2 = (bf16[2,256,1536]{2,1,0:T(8,128)(2,1)S(1)}, bf16[2,256,1536]{2,1,0:T(8,128)(2,1)}, u32[]{:S(2)}) copy-start(bf16[2,256,1536]{2,1,0:T(8,128)(2,1)} %param.23) | copy-start | bytes 4718596
  193.1 6.2 %collective-permute-start.3 = (bf16[512,3072]{1,0:T(8,128)(2,1)}, bf16[512,3072]{1,0:T(8,128)(2,1)}, u32[]{:S(2)}, u32[]{:S(2)}) collective-permute-start(bf16[512,3072]{1,0:T(8,128)(2,1)} %get-tuple-element.63.b_ref.gz_ref), channel_id=1, source_target_pairs={{0,2},{2,0},{4,6},{6,4},{8,10},{10,8},{12,14},{14,12},{16,18},{18,... | collective-permute-start | bytes 9437192 | tf_op jit(solution)/shard_map/ppermute | solution.py:1216
  193.6 15.4 %collective-permute-start.2 = (bf16[8,2,192,512]{3,2,1,0:T(8,128)(2,1)}, bf16[8,2,192,512]{3,2,1,0:T(8,128)(2,1)}, u32[]{:S(2)}, u32[]{:S(2)}) collective-permute-start(bf16[8,2,192,512]{3,2,1,0:T(8,128)(2,1)} %bitcast.66), channel_id=1, source_target_pairs={{0,2},{2,0},{4,6},{6,4},{8,10},{10,8},{12,14},{14,12},{16,18},{18,... | collective-permute-start | bytes 9437192 | tf_op jit(solution)/shard_map/ppermute | solution.py:1216
  367.6 7.5 %copy-start.1 = (f32[512,1536]{1,0:T(8,128)S(1)}, f32[512,1536]{1,0:T(8,128)}, u32[]{:S(2)}) copy-start(f32[512,1536]{1,0:T(8,128)} %get-tuple-element.76) | copy-start | bytes 9437188
